TPU v7x, 8 devices: a whole 2x2x1 slice. The times are simulated.
8 devices in a mesh: rep: 1 (over z), row: 2 (over y), col: 2 (over x), core: 2 (over core).
Axes of the slice: x: 2, y: 2, z: 1, core: 2. Of those that a mesh axis runs over, the one named last changes fastest.
Arguments:
- x: bfloat16 [2, 768, 384], P(None, ('rep', 'row', 'col', 'core'))
- route_idx: int32 [2, 768, 4], P(None, ('rep', 'row', 'col', 'core'))
- gates: float32 [2, 768, 4], P(None, ('rep', 'row', 'col', 'core'))
- w_gate: bfloat16 [32, 384, 384], P(('rep', 'row', 'col', 'core'))
- w_up: bfloat16 [32, 384, 384], P(('rep', 'row', 'col', 'core'))
- w_down: bfloat16 [32, 384, 384], P(('rep', 'row', 'col', 'core'))
- grad_y: bfloat16 [2, 768, 384], P(None, ('rep', 'row', 'col', 'core'))
Outputs:
- output 1: bfloat16 [2, 768, 384], P(None, ('rep', 'row', 'col', 'core'))
- output 2: bfloat16 [2, 768, 384], P(None, ('rep', 'row', 'col', 'core'))
- output 3: float32 [2, 768, 4], P(None, ('rep', 'row', 'col', 'core'))
- output 4: float32 [32, 384, 384], P(('rep', 'row', 'col', 'core'))
- output 5: float32 [32, 384, 384], P(('rep', 'row', 'col', 'core'))
- output 6: float32 [32, 384, 384], P(('rep', 'row', 'col', 'core'))
All inputs are finite; a program needn't handle non-finite values.
Results may differ from a plain program's by a relative error of at most 0.00857745.
Values are sent between devices in bfloat16 or wider.
A program may use at most 1 GiB of HBM per device.

v0:
```python
import jax
import jax.numpy as jnp
from jax import lax
from jax.sharding import PartitionSpec as P

GROUP_AXES = ("row", "col", "core")
ALL_AXES = ("rep", "row", "col", "core")


def route_tables(route_ids, gates, group_size, capacity, local_experts):
    expert_ids = jnp.arange(group_size)[None, :] * local_experts + jnp.arange(local_experts)[:, None]
    expert_hits = route_ids[None, None, :, :] == expert_ids[:, :, None, None]
    member = jnp.sum(expert_hits.astype(jnp.int32), axis=3)
    slot_rank = jnp.cumsum(member, axis=2) - member
    disp_mask = (member[:, :, None, :] > 0) & (slot_rank[:, :, None, :] == jnp.arange(capacity)[None, None, :, None])
    slot_pos = jnp.sum(jnp.where(expert_hits, slot_rank[:, :, :, None], 0), axis=(0, 1))
    slot_addr = (route_ids % local_experts) * (group_size * capacity) + (route_ids // local_experts) * capacity + slot_pos
    row_gate = jnp.zeros((local_experts * group_size * capacity,), jnp.float32).at[slot_addr.reshape(-1)].set(gates.reshape(-1))
    return disp_mask.astype(jnp.bfloat16), slot_addr, row_gate


def expert_forward(x_rows, w_gate, w_up, w_down):
    gate_pre = jnp.einsum("lnd,ldf->lnf", x_rows, w_gate, preferred_element_type=jnp.float32).astype(jnp.bfloat16)
    up_pre = jnp.einsum("lnd,ldf->lnf", x_rows, w_up, preferred_element_type=jnp.float32).astype(jnp.bfloat16)
    gate_f = gate_pre.astype(jnp.float32)
    hidden = (gate_f * jax.nn.sigmoid(gate_f) * up_pre.astype(jnp.float32)).astype(jnp.bfloat16)
    exp_out = jnp.einsum("lnf,lfd->lnd", hidden, w_down, preferred_element_type=jnp.float32).astype(jnp.bfloat16)
    return exp_out, gate_pre, up_pre, hidden


def expert_backward(x_rows, d_out, gate_pre, up_pre, hidden, w_gate, w_up, w_down):
    gate_f = gate_pre.astype(jnp.float32)
    up_f = up_pre.astype(jnp.float32)
    sigmoid_g = jax.nn.sigmoid(gate_f)
    d_act = jnp.einsum("lnd,lfd->lnf", d_out, w_down, preferred_element_type=jnp.float32)
    d_up = (d_act * gate_f * sigmoid_g).astype(jnp.bfloat16)
    d_gate = (d_act * up_f * sigmoid_g * (1.0 + gate_f * (1.0 - sigmoid_g))).astype(jnp.bfloat16)
    g_down = jnp.einsum("lnf,lnd->lfd", hidden, d_out, preferred_element_type=jnp.float32)
    g_gate = jnp.einsum("lnd,lnf->ldf", x_rows, d_gate, preferred_element_type=jnp.float32)
    g_up = jnp.einsum("lnd,lnf->ldf", x_rows, d_up, preferred_element_type=jnp.float32)
    d_in = (jnp.einsum("lnf,ldf->lnd", d_gate, w_gate, preferred_element_type=jnp.float32) + jnp.einsum("lnf,ldf->lnd", d_up, w_up, preferred_element_type=jnp.float32)).astype(jnp.bfloat16)
    return d_in, g_gate, g_up, g_down


def solution(mesh):
    group_size = mesh.shape["row"] * mesh.shape["col"] * mesh.shape["core"]
    tok_spec = P(None, ALL_AXES, None)
    w_spec = P(ALL_AXES, None, None)

    def exchange(send_buf):
        return lax.all_to_all(send_buf, GROUP_AXES, 1, 1, tiled=True)

    def moe_layer(x, route_idx, gates, w_gate, w_up, w_down, grad_y):
        local_experts = w_gate.shape[0]
        tok_dev = x.shape[1]
        model_dim = x.shape[2]
        capacity = tok_dev // 2
        buf_rows = group_size * capacity
        buf_shape = (local_experts, group_size, capacity, model_dim)
        flat_shape = (local_experts * buf_rows, model_dim)
        outs_y, outs_dx, outs_dg = [], [], []
        sum_gate = jnp.zeros(w_gate.shape, jnp.float32)
        sum_up = jnp.zeros(w_up.shape, jnp.float32)
        sum_down = jnp.zeros(w_down.shape, jnp.float32)
        for micro_idx in range(2):
            x_mb = x[micro_idx]
            dy_mb = grad_y[micro_idx]
            gate_mb = gates[micro_idx]
            disp_mask, slot_addr, row_gate = route_tables(route_idx[micro_idx], gate_mb, group_size, capacity, local_experts)
            send_x = jnp.einsum("lgct,td->lgcd", disp_mask, x_mb, preferred_element_type=jnp.float32).astype(jnp.bfloat16)
            x_rows = exchange(send_x).reshape(local_experts, buf_rows, model_dim)
            exp_out, gate_pre, up_pre, hidden = expert_forward(x_rows, w_gate, w_up, w_down)
            out_back = exchange(exp_out.reshape(buf_shape)).reshape(flat_shape)
            out_slots = jnp.take(out_back, slot_addr, axis=0)
            outs_y.append(jnp.sum(gate_mb[:, :, None] * out_slots.astype(jnp.float32), axis=1).astype(jnp.bfloat16))
            outs_dg.append(jnp.einsum("td,tkd->tk", dy_mb, out_slots, preferred_element_type=jnp.float32))
            dy_rows = jnp.einsum("lgct,td->lgcd", disp_mask, dy_mb, preferred_element_type=jnp.float32)
            send_dout = (row_gate.reshape(local_experts, group_size, capacity)[..., None] * dy_rows).astype(jnp.bfloat16)
            d_out = exchange(send_dout).reshape(local_experts, buf_rows, model_dim)
            d_in, g_gate, g_up, g_down = expert_backward(x_rows, d_out, gate_pre, up_pre, hidden, w_gate, w_up, w_down)
            dx_back = exchange(d_in.reshape(buf_shape)).reshape(flat_shape)
            outs_dx.append(jnp.sum(jnp.take(dx_back, slot_addr, axis=0).astype(jnp.float32), axis=1).astype(jnp.bfloat16))
            sum_gate = sum_gate + g_gate
            sum_up = sum_up + g_up
            sum_down = sum_down + g_down
        return (jnp.stack(outs_y), jnp.stack(outs_dx), jnp.stack(outs_dg), sum_gate, sum_up, sum_down)

    return jax.shard_map(moe_layer, mesh=mesh, in_specs=(tok_spec, tok_spec, tok_spec, w_spec, w_spec, w_spec, tok_spec), out_specs=(tok_spec, tok_spec, tok_spec, w_spec, w_spec, w_spec), check_vma=False)
```

profile of v0, /device:TPU:0, one launch (start us, length us, event | category | flops | bytes accessed | tf_op | source)
XLA Modules:
  0.0 174.2 jit_solution(10954878525609194246)
XLA Ops:
  6.2 4.3 %all-to-all-start.2 = ((bf16[4,8,48,384]{3,2,0,1:T(8,128)(2,1)}), bf16[4,8,48,384]{3,2,0,1:T(8,128)(2,1)S(1)}, u32[]{:S(2)}, u32[]{:S(2)}) async-start(bf16[4,8,48,384]{3,2,0,1:T(8,128)(2,1)} %copy.100), calls=%async_computation.2 | async-start | bytes 2359296 | tf_op jit(solution)/shard_map/all_to_all | solution.py:51
  13.5 2.9 %scatter_custom_fusion.1 = f32[1536]{0:T(1024)S(1)} fusion(s32[384]{0:T(512)S(1)} %fusion.69, f32[384]{0:T(512)S(1)} %reshape.435, f32[]{:T(128)} %constant.73.clone.1), kind=kCustom, calls=%fused_computation.112 | custom fusion | bytes 6148 | tf_op jit(solution)/shard_map/scatter | solution.py:18
  19.9 7.4 %all-to-all-done.2 = bf16[4,8,48,384]{3,2,0,1:T(8,128)(2,1)S(1)} async-done(((bf16[4,8,48,384]{3,2,0,1:T(8,128)(2,1)}), bf16[4,8,48,384]{3,2,0,1:T(8,128)(2,1)S(1)}, u32[]{:S(2)}, u32[]{:S(2)}) %all-to-all-start.2) | async-done | bytes 1179680 | tf_op jit(solution)/shard_map/all_to_all | solution.py:51
  27.3 3.0 %all-to-all-start = ((bf16[4,8,48,384]{3,2,0,1:T(8,128)(2,1)}), bf16[4,8,48,384]{3,2,0,1:T(8,128)(2,1)}, u32[]{:S(2)}, u32[]{:S(2)}) async-start(bf16[4,8,48,384]{3,2,0,1:T(8,128)(2,1)} %copy.93), calls=%async_computation | async-start | bytes 2359296 | tf_op jit(solution)/shard_map/all_to_all | solution.py:51
  35.1 3.1 %scatter_custom_fusion = f32[1536]{0:T(1024)S(1)} fusion(s32[384]{0:T(512)} %fusion.68, f32[384]{0:T(512)S(1)} %reshape.427, f32[]{:T(128)} %constant.73.clone.1), kind=kCustom, calls=%fused_computation.114 | custom fusion | bytes 6656 | tf_op jit(solution)/shard_map/scatter | solution.py:18
  49.3 3.0 %all-to-all-start.6 = ((bf16[4,8,48,384]{3,2,0,1:T(8,128)(2,1)}), bf16[4,8,48,384]{3,2,0,1:T(8,128)(2,1)}, u32[]{:S(2)}, u32[]{:S(2)}) async-start(bf16[4,8,48,384]{3,2,0,1:T(8,128)(2,1)} %copy.118), calls=%async_computation.6 | async-start | bytes 2359296 | tf_op jit(solution)/shard_map/all_to_all | solution.py:51
  53.9 2.0 %convolution_convert_fusion.6 = bf16[4,384,384]{2,1,0:T(8,128)(2,1)} fusion(bf16[4,384,384]{2,1,0:T(8,128)(2,1)S(1)} %bitcast.100, bf16[4,384,384]{2,1,0:T(8,128)(2,1)S(1)} %copy-done.3), kind=kOutput, calls=%fused_computation.51 | convolution fusion | flops 453574656 | bytes 3538944 | tf_op jit(solution)/shard_map/lnd,ldf->lnf/dot_general | solution.py:23
  55.9 1.9 %convolution_convert_fusion.5 = bf16[4,384,384]{2,1,0:T(8,128)(2,1)} fusion(bf16[4,384,384]{2,1,0:T(8,128)(2,1)S(1)} %bitcast.101, bf16[4,384,384]{2,1,0:T(8,128)(2,1)S(1)} %copy-done.6), kind=kOutput, calls=%fused_computation.50 | convolution fusion | flops 453574656 | bytes 3538944 | tf_op jit(solution)/shard_map/lnd,ldf->lnf/dot_general | solution.py:24
  59.8 2.0 %convolution_convert_fusion = bf16[4,384,384]{2,1,0:T(8,128)(2,1)} fusion(bf16[4,384,384]{2,1,0:T(8,128)(2,1)S(1)} %copy-done, bf16[4,384,384]{2,1,0:T(8,128)(2,1)S(1)} %convolution_convert_fusion.1, bf16[4,384,384]{2,1,0:T(8,128)(2,1)S(1)} %copy-done.15), kind=kOutput, calls=%fused_computation.45 | convolution fusion | flops 458293248 | bytes 4718592 | tf_op jit(solution)/shard_map/lnf,lfd->lnd/dot_general | solution.py:27
  61.8 7.2 %all-to-all-done.6 = bf16[4,8,48,384]{3,2,0,1:T(8,128)(2,1)} async-done(((bf16[4,8,48,384]{3,2,0,1:T(8,128)(2,1)}), bf16[4,8,48,384]{3,2,0,1:T(8,128)(2,1)}, u32[]{:S(2)}, u32[]{:S(2)}) %all-to-all-start.6) | async-done | bytes 1179680 | tf_op jit(solution)/shard_map/all_to_all | solution.py:51
  69.0 3.2 %all-to-all-start.4 = ((bf16[4,8,48,384]{3,2,0,1:T(8,128)(2,1)}), bf16[4,8,48,384]{3,2,0,1:T(8,128)(2,1)}, u32[]{:S(2)}, u32[]{:S(2)}) async-start(bf16[4,8,48,384]{3,2,0,1:T(8,128)(2,1)} %copy.109), calls=%async_computation.4 | async-start | bytes 2359296 | tf_op jit(solution)/shard_map/all_to_all | solution.py:51
  82.0 2.0 %add_convert_fusion = bf16[4,384,384]{2,1,0:T(8,128)(2,1)} fusion(f32[4,384,384]{2,1,0:T(8,128)S(1)} %fusion.88, bf16[4,384,384]{2,1,0:T(8,128)(2,1)S(1)} %copy-done.7, f32[4,384,384]{2,1,0:T(8,128)S(1)} %get-tuple-element.28, bf16[4,384,384]{2,1,0:T(8,128)(2,1)S(1)} %copy-done.16), kind=kOutput, calls=%fused_computation.38 | convolution fusion | flops 458293248 | bytes 8257536 | tf_op jit(solution)/shard_map/lnf,ldf->lnd/dot_general | solution.py:41
  84.0 4.6 %all-to-all-done.4 = bf16[4,8,48,384]{3,2,0,1:T(8,128)(2,1)} async-done(((bf16[4,8,48,384]{3,2,0,1:T(8,128)(2,1)}), bf16[4,8,48,384]{3,2,0,1:T(8,128)(2,1)}, u32[]{:S(2)}, u32[]{:S(2)}) %all-to-all-start.4) | async-done | bytes 1179680 | tf_op jit(solution)/shard_map/all_to_all | solution.py:51
  88.6 3.0 %all-to-all-start.3 = ((bf16[4,8,48,384]{3,2,0,1:T(8,128)(2,1)}), bf16[4,8,48,384]{3,2,0,1:T(8,128)(2,1)}, u32[]{:S(2)}, u32[]{:S(2)}) async-start(bf16[4,8,48,384]{3,2,0,1:T(8,128)(2,1)} %copy.102), calls=%async_computation.3 | async-start | bytes 2359296 | tf_op jit(solution)/shard_map/all_to_all | solution.py:51
  93.6 2.5 %fusion.80 = f32[4,384,384]{2,1,0:T(8,128)} fusion(bf16[4,384,384]{2,1,0:T(8,128)(2,1)S(1)} %bitcast.117, bf16[4,384,384]{2,1,0:T(8,128)(2,1)S(1)} %copy-done.25, bf16[4,384,384]{2,1,0:T(8,128)(2,1)S(1)} %copy-done.23), kind=kOutput, calls=%fused_computation.164 | convolution fusion | flops 457703424 | bytes 5898240 | tf_op jit(solution)/shard_map/lnf,lnd->lfd/dot_general | solution.py:38
  96.1 3.0 %fusion.13 = (bf16[4,384,384]{2,1,0:T(8,128)(2,1)}, bf16[4,384,384]{2,1,0:T(8,128)(2,1)}) fusion(bf16[4,384,384]{2,1,0:T(8,128)(2,1)S(1)} %copy-done.23, bf16[4,384,384]{2,1,0:T(8,128)(2,1)S(1)} %copy-done.25, bf16[4,384,384]{2,1,0:T(8,128)(2,1)S(1)} %bitcast.118, bf16[4,384,384]{2,1,0:T(8,128)(2,1)S(1)} %copy-done), kind=kOutput, calls=%fused_computation.31 | convolution fusion | flops 461832192 | bytes 7077888 | tf_op jit(solution)/shard_map/lnd,lfd->lnf/dot_general | solution.py:35
  99.0 9.3 %all-to-all-done.3 = bf16[4,8,48,384]{3,2,0,1:T(8,128)(2,1)} async-done(((bf16[4,8,48,384]{3,2,0,1:T(8,128)(2,1)}), bf16[4,8,48,384]{3,2,0,1:T(8,128)(2,1)}, u32[]{:S(2)}, u32[]{:S(2)}) %all-to-all-start.3) | async-done | bytes 1179680 | tf_op jit(solution)/shard_map/all_to_all | solution.py:51
  108.3 3.0 %all-to-all-start.1 = ((bf16[4,8,48,384]{3,2,0,1:T(8,128)(2,1)}), bf16[4,8,48,384]{3,2,0,1:T(8,128)(2,1)}, u32[]{:S(2)}, u32[]{:S(2)}) async-start(bf16[4,8,48,384]{3,2,0,1:T(8,128)(2,1)} %copy.95), calls=%async_computation.1 | async-start | bytes 2359296 | tf_op jit(solution)/shard_map/all_to_all | solution.py:51
  111.3 2.3 %fusion.87 = f32[4,384,384]{2,1,0:T(8,128)S(1)} fusion(bf16[4,384,384]{2,1,0:T(8,128)(2,1)} %get-tuple-element.14, bf16[4,384,384]{2,1,0:T(8,128)(2,1)S(1)} %copy-done.5), kind=kOutput, calls=%fused_computation.167 | convolution fusion | flops 452984832 | bytes 4718592 | tf_op jit(solution)/shard_map/lnf,ldf->lnd/dot_general | solution.py:41
  118.4 2.5 %convolution_add_fusion = f32[4,384,384]{2,1,0:T(8,128)} fusion(f32[4,384,384]{2,1,0:T(8,128)S(1)} %copy-done.50, bf16[4,384,384]{2,1,0:T(8,128)(2,1)S(1)} %bitcast.114, bf16[4,384,384]{2,1,0:T(8,128)(2,1)S(1)} %copy-done.21, bf16[4,384,384]{2,1,0:T(8,128)(2,1)S(1)} %copy-done.17), kind=kOutput, calls=%fused_computation.42 | convolution fusion | flops 458293248 | bytes 8257536 | tf_op jit(solution)/shard_map/lnf,lnd->lfd/dot_general | solution.py:38
  120.9 7.0 %all-to-all-done.1 = bf16[4,8,48,384]{3,2,0,1:T(8,128)(2,1)} async-done(((bf16[4,8,48,384]{3,2,0,1:T(8,128)(2,1)}), bf16[4,8,48,384]{3,2,0,1:T(8,128)(2,1)}, u32[]{:S(2)}, u32[]{:S(2)}) %all-to-all-start.1) | async-done | bytes 1179680 | tf_op jit(solution)/shard_map/all_to_all | solution.py:51
  128.0 3.2 %all-to-all-start.7 = ((bf16[4,8,48,384]{3,2,0,1:T(8,128)(2,1)}), bf16[4,8,48,384]{3,2,0,1:T(8,128)(2,1)}, u32[]{:S(2)}, u32[]{:S(2)}) async-start(bf16[4,8,48,384]{3,2,0,1:T(8,128)(2,1)} %copy.120), calls=%async_computation.7 | async-start | bytes 2359296 | tf_op jit(solution)/shard_map/all_to_all | solution.py:51
  131.2 2.2 %fusion.90 = f32[4,384,384]{2,1,0:T(8,128)S(1)} fusion(bf16[4,384,384]{2,1,0:T(8,128)(2,1)S(1)} %bitcast.102, bf16[4,384,384]{2,1,0:T(8,128)(2,1)} %get-tuple-element.13), kind=kOutput, calls=%fused_computation.170 | convolution fusion | flops 452984832 | bytes 4718592 | tf_op jit(solution)/shard_map/lnd,lnf->ldf/dot_general | solution.py:40
  135.1 2.3 %fusion.89 = f32[4,384,384]{2,1,0:T(8,128)} fusion(bf16[4,384,384]{2,1,0:T(8,128)(2,1)S(1)} %bitcast.103, bf16[4,384,384]{2,1,0:T(8,128)(2,1)S(1)} %copy-done.13), kind=kOutput, calls=%fused_computation.169 | convolution fusion | flops 452984832 | bytes 4718592 | tf_op jit(solution)/shard_map/lnd,lnf->ldf/dot_general | solution.py:39
  137.4 2.6 %convolution_add_fusion.1 = f32[4,384,384]{2,1,0:T(8,128)} fusion(f32[4,384,384]{2,1,0:T(8,128)S(1)} %fusion.90, bf16[4,384,384]{2,1,0:T(8,128)(2,1)S(1)} %bitcast.106, f32[4,384,384]{2,1,0:T(8,128)S(1)} %copy-done.49, bf16[4,384,384]{2,1,0:T(8,128)(2,1)S(1)} %copy-done.18), kind=kOutput, calls=%fused_computation.43 | convolution fusion | flops 457703424 | bytes 9437184 | tf_op jit(solution)/shard_map/lnd,lnf->ldf/dot_general | solution.py:40
  140.1 7.5 %all-to-all-done.7 = bf16[4,8,48,384]{3,2,0,1:T(8,128)(2,1)} async-done(((bf16[4,8,48,384]{3,2,0,1:T(8,128)(2,1)}), bf16[4,8,48,384]{3,2,0,1:T(8,128)(2,1)}, u32[]{:S(2)}, u32[]{:S(2)}) %all-to-all-start.7) | async-done | bytes 1179680 | tf_op jit(solution)/shard_map/all_to_all | solution.py:51
  147.6 3.0 %all-to-all-start.5 = ((bf16[4,8,48,384]{3,2,0,1:T(8,128)(2,1)}), bf16[4,8,48,384]{3,2,0,1:T(8,128)(2,1)}, u32[]{:S(2)}, u32[]{:S(2)}) async-start(bf16[4,8,48,384]{3,2,0,1:T(8,128)(2,1)} %copy.111), calls=%async_computation.5 | async-start | bytes 2359296 | tf_op jit(solution)/shard_map/all_to_all | solution.py:51
  150.6 3.6 %convolution_add_fusion.2 = f32[4,384,384]{2,1,0:T(8,128)} fusion(f32[4,384,384]{2,1,0:T(8,128)S(1)} %copy-done.9, bf16[4,384,384]{2,1,0:T(8,128)(2,1)S(1)} %bitcast.107, bf16[4,384,384]{2,1,0:T(8,128)(2,1)} %copy-done.12), kind=kOutput, calls=%fused_computation.44 | convolution fusion | flops 453574656 | bytes 7077888 | tf_op jit(solution)/shard_map/lnd,lnf->ldf/dot_general | solution.py:39
  155.6 2.1 %gather_fusion.1 = bf16[384,384]{1,0:T(8,128)(2,1)S(1)} fusion(bf16[1536,384]{1,0:T(8,128)(2,1)S(1)} %bitcast.110, s32[1024]{0:T(1024)S(1)} %pad_clamp_fusion), kind=kCustom, calls=%fused_computation.1.clone | custom fusion | bytes 591360 | tf_op jit(solution)/shard_map/jit(_take)/gather | solution.py:74
  160.0 2.1 %gather_fusion = bf16[384,384]{1,0:T(8,128)(2,1)S(1)} fusion(bf16[1536,384]{1,0:T(8,128)(2,1)S(1)} %bitcast.111, s32[1024]{0:T(1024)S(1)} %pad_clamp_fusion.1), kind=kCustom, calls=%fused_computation.clone | custom fusion | bytes 591360 | tf_op jit(solution)/shard_map/jit(_take)/gather | solution.py:74
  164.3 2.1 %gather_fusion.3 = bf16[384,384]{1,0:T(8,128)(2,1)S(1)} fusion(bf16[1536,384]{1,0:T(8,128)(2,1)S(1)} %bitcast.108, s32[1024]{0:T(1024)S(1)} %pad_clamp_fusion), kind=kCustom, calls=%fused_computation.3.clone | custom fusion | bytes 591360 | tf_op jit(solution)/shard_map/jit(_take)/gather | solution.py:82
  169.5 2.1 %gather_fusion.2 = bf16[384,384]{1,0:T(8,128)(2,1)S(1)} fusion(bf16[1536,384]{1,0:T(8,128)(2,1)S(1)} %bitcast.109, s32[1024]{0:T(1024)S(1)} %pad_clamp_fusion.1), kind=kCustom, calls=%fused_computation.2.clone | custom fusion | bytes 591360 | tf_op jit(solution)/shard_map/jit(_take)/gather | solution.py:82
  (186 shorter events, 60.7 us)
Async XLA Ops:
  0.6 59.2 %copy-start = (bf16[4,384,384]{2,1,0:T(8,128)(2,1)S(1)}, bf16[4,384,384]{2,1,0:T(8,128)(2,1)}, u32[]{:S(2)}) copy-start(bf16[4,384,384]{2,1,0:T(8,128)(2,1)} %param.14) | copy-start | bytes 3538948
  2.7 3.5 %copy-start.41 = (pred[4,8,96]{2,1,0:T(8,128)(4,1)}, pred[4,8,96]{2,1,0:T(8,128)(4,1)S(1)}, u32[]{:S(2)}) copy-start(pred[4,8,96]{2,1,0:T(8,128)(4,1)S(1)} %broadcast_compare_fusion) | copy-start | bytes 9220
  3.7 6.8 %copy-start.32 = (s32[4,8,96]{2,1,0:T(8,128)}, s32[4,8,96]{2,1,0:T(8,128)S(1)}, u32[]{:S(2)}) copy-start(s32[4,8,96]{2,1,0:T(8,128)S(1)} %sub.44) | copy-start | bytes 36868
  6.2 4.4 %copy-start.47 = (f32[2,96,4]{1,2,0:T(4,128)S(1)}, f32[2,96,4]{1,2,0:T(4,128)}, u32[]{:S(2)}) copy-start(f32[2,96,4]{1,2,0:T(4,128)} %param.11) | copy-start | bytes 9220
  6.2 10.9 %copy-start.34 = (bf16[2,96,384]{2,1,0:T(8,128)(2,1)S(1)}, bf16[2,96,384]{2,1,0:T(8,128)(2,1)}, u32[]{:S(2)}) copy-start(bf16[2,96,384]{2,1,0:T(8,128)(2,1)} %param.9) | copy-start | bytes 442372
  6.2 21.1 %all-to-all-start.2 = ((bf16[4,8,48,384]{3,2,0,1:T(8,128)(2,1)}), bf16[4,8,48,384]{3,2,0,1:T(8,128)(2,1)S(1)}, u32[]{:S(2)}, u32[]{:S(2)}) async-start(bf16[4,8,48,384]{3,2,0,1:T(8,128)(2,1)} %copy.100), calls=%async_computation.2 | async-start | bytes 2359296 | tf_op jit(solution)/shard_map/all_to_all | solution.py:51
  27.3 4.3 %copy-start.10 = (bf16[4,8,48,384]{3,2,0,1:T(8,128)(2,1)}, bf16[4,8,48,384]{3,2,0,1:T(8,128)(2,1)S(1)}, u32[]{:S(2)}) copy-start(bf16[4,8,48,384]{3,2,0,1:T(8,128)(2,1)S(1)} %all-to-all-done.2) | copy-start | bytes 3538948
  27.3 22.0 %all-to-all-start = ((bf16[4,8,48,384]{3,2,0,1:T(8,128)(2,1)}), bf16[4,8,48,384]{3,2,0,1:T(8,128)(2,1)}, u32[]{:S(2)}, u32[]{:S(2)}) async-start(bf16[4,8,48,384]{3,2,0,1:T(8,128)(2,1)} %copy.93), calls=%async_computation | async-start | bytes 2359296 | tf_op jit(solution)/shard_map/all_to_all | solution.py:51
  49.3 19.7 %all-to-all-start.6 = ((bf16[4,8,48,384]{3,2,0,1:T(8,128)(2,1)}), bf16[4,8,48,384]{3,2,0,1:T(8,128)(2,1)}, u32[]{:S(2)}, u32[]{:S(2)}) async-start(bf16[4,8,48,384]{3,2,0,1:T(8,128)(2,1)} %copy.118), calls=%async_computation.6 | async-start | bytes 2359296 | tf_op jit(solution)/shard_map/all_to_all | solution.py:51
  53.9 2.0 %copy-start.6 = (bf16[4,384,384]{2,1,0:T(8,128)(2,1)S(1)}, bf16[4,384,384]{2,1,0:T(8,128)(2,1)}, u32[]{:S(2)}) copy-start(bf16[4,384,384]{2,1,0:T(8,128)(2,1)} %param.13) | copy-start | bytes 3538948
  69.0 19.7 %all-to-all-start.4 = ((bf16[4,8,48,384]{3,2,0,1:T(8,128)(2,1)}), bf16[4,8,48,384]{3,2,0,1:T(8,128)(2,1)}, u32[]{:S(2)}, u32[]{:S(2)}) async-start(bf16[4,8,48,384]{3,2,0,1:T(8,128)(2,1)} %copy.109), calls=%async_computation.4 | async-start | bytes 2359296 | tf_op jit(solution)/shard_map/all_to_all | solution.py:51
  75.8 4.5 %copy-start.12 = (bf16[4,384,384]{2,1,0:T(8,128)(2,1)}, bf16[4,384,384]{2,1,0:T(8,128)(2,1)S(1)}, u32[]{:S(2)}) copy-start(bf16[4,384,384]{2,1,0:T(8,128)(2,1)S(1)} %get-tuple-element.27) | copy-start | bytes 3538948
  75.8 5.9 %copy-start.48 = (f32[4,384,384]{2,1,0:T(8,128)}, f32[4,384,384]{2,1,0:T(8,128)S(1)}, u32[]{:S(2)}) copy-start(f32[4,384,384]{2,1,0:T(8,128)S(1)} %get-tuple-element.28) | copy-start | bytes 7077892
  75.8 2.1 %copy-start.29 = (bf16[4,384,384]{2,1,0:T(8,128)(2,1)S(1)}, bf16[4,384,384]{2,1,0:T(8,128)(2,1)}, u32[]{:S(2)}) copy-start(bf16[4,384,384]{2,1,0:T(8,128)(2,1)} %convolution_convert_fusion) | copy-start | bytes 3538948
  88.6 19.7 %all-to-all-start.3 = ((bf16[4,8,48,384]{3,2,0,1:T(8,128)(2,1)}), bf16[4,8,48,384]{3,2,0,1:T(8,128)(2,1)}, u32[]{:S(2)}, u32[]{:S(2)}) async-start(bf16[4,8,48,384]{3,2,0,1:T(8,128)(2,1)} %copy.102), calls=%async_computation.3 | async-start | bytes 2359296 | tf_op jit(solution)/shard_map/all_to_all | solution.py:51
  99.0 12.2 %copy-start.5 = (bf16[4,384,384]{2,1,0:T(8,128)(2,1)S(1)}, bf16[4,384,384]{2,1,0:T(8,128)(2,1)}, u32[]{:S(2)}) copy-start(bf16[4,384,384]{2,1,0:T(8,128)(2,1)} %param.12) | copy-start | bytes 3538948
  108.3 19.7 %all-to-all-start.1 = ((bf16[4,8,48,384]{3,2,0,1:T(8,128)(2,1)}), bf16[4,8,48,384]{3,2,0,1:T(8,128)(2,1)}, u32[]{:S(2)}, u32[]{:S(2)}) async-start(bf16[4,8,48,384]{3,2,0,1:T(8,128)(2,1)} %copy.95), calls=%async_computation.1 | async-start | bytes 2359296 | tf_op jit(solution)/shard_map/all_to_all | solution.py:51
  111.3 2.3 %copy-start.28 = (bf16[4,384,384]{2,1,0:T(8,128)(2,1)S(1)}, bf16[4,384,384]{2,1,0:T(8,128)(2,1)}, u32[]{:S(2)}) copy-start(bf16[4,384,384]{2,1,0:T(8,128)(2,1)} %add_convert_fusion) | copy-start | bytes 3538948
  113.6 2.0 %copy-start.14 = (bf16[4,384,384]{2,1,0:T(8,128)(2,1)S(1)}, bf16[4,384,384]{2,1,0:T(8,128)(2,1)}, u32[]{:S(2)}) copy-start(bf16[4,384,384]{2,1,0:T(8,128)(2,1)} %get-tuple-element.13) | copy-start | bytes 3538948
  115.7 2.0 %copy-start.27 = (bf16[4,8,48,384]{3,2,1,0:T(8,128)(2,1)S(1)}, bf16[4,8,48,384]{3,2,1,0:T(8,128)(2,1)}, u32[]{:S(2)}) copy-start(bf16[4,8,48,384]{3,2,1,0:T(8,128)(2,1)} %copy-done.26) | copy-start | bytes 3538948
  115.7 2.7 %copy-start.50 = (f32[4,384,384]{2,1,0:T(8,128)S(1)}, f32[4,384,384]{2,1,0:T(8,128)}, u32[]{:S(2)}) copy-start(f32[4,384,384]{2,1,0:T(8,128)} %fusion.80) | copy-start | bytes 7077892
  128.0 19.7 %all-to-all-start.7 = ((bf16[4,8,48,384]{3,2,0,1:T(8,128)(2,1)}), bf16[4,8,48,384]{3,2,0,1:T(8,128)(2,1)}, u32[]{:S(2)}, u32[]{:S(2)}) async-start(bf16[4,8,48,384]{3,2,0,1:T(8,128)(2,1)} %copy.120), calls=%async_computation.7 | async-start | bytes 2359296 | tf_op jit(solution)/shard_map/all_to_all | solution.py:51
  135.1 2.4 %copy-start.18 = (bf16[4,384,384]{2,1,0:T(8,128)(2,1)S(1)}, bf16[4,384,384]{2,1,0:T(8,128)(2,1)}, u32[]{:S(2)}) copy-start(bf16[4,384,384]{2,1,0:T(8,128)(2,1)} %convolution_convert_fusion.2) | copy-start | bytes 3538948
  135.1 2.4 %copy-start.49 = (f32[4,384,384]{2,1,0:T(8,128)S(1)}, f32[4,384,384]{2,1,0:T(8,128)}, u32[]{:S(2)}) copy-start(f32[4,384,384]{2,1,0:T(8,128)} %copy-done.48) | copy-start | bytes 7077892
  140.1 10.5 %copy-start.9 = (f32[4,384,384]{2,1,0:T(8,128)S(1)}, f32[4,384,384]{2,1,0:T(8,128)}, u32[]{:S(2)}) copy-start(f32[4,384,384]{2,1,0:T(8,128)} %fusion.89) | copy-start | bytes 7077892
  147.6 20.5 %all-to-all-start.5 = ((bf16[4,8,48,384]{3,2,0,1:T(8,128)(2,1)}), bf16[4,8,48,384]{3,2,0,1:T(8,128)(2,1)}, u32[]{:S(2)}, u32[]{:S(2)}) async-start(bf16[4,8,48,384]{3,2,0,1:T(8,128)(2,1)} %copy.111), calls=%async_computation.5 | async-start | bytes 2359296 | tf_op jit(solution)/shard_map/all_to_all | solution.py:51
  155.6 2.2 %copy-start.38 = (pred[96,4]{1,0:T(8,128)(4,1)S(1)}, pred[96,4]{1,0:T(8,128)(4,1)}, u32[]{:S(2)}) copy-start(pred[96,4]{1,0:T(8,128)(4,1)} %copy.99) | copy-start | bytes 1156
  155.6 2.2 %copy-start.40 = (bf16[96,384,1]{1,0,2:T(8,128)(2,1)S(1)}, bf16[96,384,1]{1,0,2:T(8,128)(2,1)}, u32[]{:S(2)}) copy-start(bf16[96,384,1]{1,0,2:T(8,128)(2,1)} %get-tuple-element.16) | copy-start | bytes 221188
  160.0 2.2 %copy-start.37 = (pred[96,4]{1,0:T(8,128)(4,1)S(1)}, pred[96,4]{1,0:T(8,128)(4,1)}, u32[]{:S(2)}) copy-start(pred[96,4]{1,0:T(8,128)(4,1)} %copy.92) | copy-start | bytes 1156
  160.0 2.2 %copy-start.39 = (bf16[96,384,1]{1,0,2:T(8,128)(2,1)S(1)}, bf16[96,384,1]{1,0,2:T(8,128)(2,1)}, u32[]{:S(2)}) copy-start(bf16[96,384,1]{1,0,2:T(8,128)(2,1)} %get-tuple-element.15) | copy-start | bytes 221188
  164.3 2.7 %copy-start.31 = (f32[96,4]{1,0:T(8,128)S(1)}, f32[96,4]{1,0:T(8,128)}, u32[]{:S(2)}) copy-start(f32[96,4]{1,0:T(8,128)} %copy.98) | copy-start | bytes 4612
  169.5 4.7 %copy-start.1 = (bf16[4,384,384]{2,1,0:T(8,128)(2,1)S(1)}, bf16[4,384,384]{2,1,0:T(8,128)(2,1)}, u32[]{:S(2)}) copy-start(bf16[4,384,384]{2,1,0:T(8,128)(2,1)} %param.14) | copy-start | bytes 3538948
  (27 other events, 42.1 us)
where the time goes:
time: 175 us; the launch traced here: 174 us
  local copies, waits for them, and re-layouts  56.1 us (32%)
  waiting for transfers between devices  43 us (25%)
  matrix products  39.9 us (23%)
  starting transfers between devices  25.6 us (15%)
  other arithmetic  8.13 us (5%)
    all_to_all x8, waiting for transfers between devices, exchange(): return lax.all_to_all(send_buf, GROUP_AXES, 1, 1, tiled=True)  43 us
    all_to_all x8, starting transfers between devices, exchange(): return lax.all_to_all(send_buf, GROUP_AXES, 1, 1, tiled=True)  25.6 us
    all_to_all x8, local copies, waits for them, and re-layouts, exchange(): return lax.all_to_all(send_buf, GROUP_AXES, 1, 1, tiled=True)  10.3 us
    unnamed x102, local copies, waits for them, and re-layouts  8.66 us
    scatter x2, local copies, waits for them, and re-layouts, route_tables(): jnp.zeros((local_experts * group_size * capacity,), jnp.float32)  5.99 us
    dot_general x2, matrix products, expert_backward(): jnp.einsum('lnd,lnf->ldf', x_rows, d_gate, preferred_element_type=jnp.flo...  5.96 us
    dot_general x2, matrix products, expert_backward(): jnp.einsum('lnf,lnd->lfd', hidden, d_out, preferred_element_type=jnp.floa...  5.01 us
    dot_general x2, matrix products, expert_backward(): jnp.einsum('lnd,lnf->ldf', x_rows, d_up, preferred_element_type=jnp.float32)  4.84 us
  transfers between devices with their start and end apart: 8, of which 6 were waited for; matrix products, arithmetic and copies ran while one was open for 48% of the time, Pallas kernels for 0%

commit v1 on v0

v1 whole, which is shorter than its diff:
```python
import functools

import jax
import jax.numpy as jnp
from jax import lax
from jax.experimental import pallas as pl
from jax.experimental.pallas import tpu as pltpu
from jax.sharding import PartitionSpec as P

ALL_AXES = ("rep", "row", "col", "core")
MESH = pl.DeviceIdType.MESH
BF = jnp.bfloat16
F32 = jnp.float32
SLAB = 16
NBLK = 8
NEXP = 4
TOPK = 4


def coords():
    return (lax.axis_index("rep"), lax.axis_index("row"), lax.axis_index("col"), lax.axis_index("core"))


def peer(mask):
    rep, row, col, core = coords()
    flip = lambda pos, bit: 1 - pos if mask & bit else pos
    return (rep, flip(row, 4), flip(col, 2), flip(core, 1))


def number(mask=0):
    _, row, col, core = peer(mask)
    return row * 4 + col * 2 + core


def enter():
    barrier = pltpu.get_barrier_semaphore()
    for mask in range(1, NBLK):
        pl.semaphore_signal(barrier, inc=1, device_id=peer(mask), device_id_type=MESH)
    pl.semaphore_wait(barrier, NBLK - 1)


def remote(src, dst, send_sem, recv_sem, mask):
    return pltpu.make_async_remote_copy(src_ref=src, dst_ref=dst, send_sem=send_sem, recv_sem=recv_sem, device_id=peer(mask), device_id_type=MESH)


def gather_kernel(x_ref, dy_ref, route_ref, gate_ref, xg_ref, dyg_ref, rt_ref, mine, send_sem, recv_sem, rt_send, rt_recv):
    enter()
    me, at_x, at_y, at_d = number(0), number(2), number(4), number(6)
    outs = (xg_ref, dyg_ref)
    ins = (x_ref, dy_ref)
    PART = 6

    def copy(mb, kind):
        ss, rs = send_sem.at[mb, kind], recv_sem.at[mb, kind]
        if kind in (0, 1):
            return remote(ins[kind].at[mb], outs[kind].at[mb, me], ss, rs, 2)
        if kind == 2:
            return remote(dyg_ref.at[mb, at_y], dyg_ref.at[mb, at_y], ss, rs, 2)
        if kind in (3, 4):
            return remote(ins[kind - 3].at[mb], outs[kind - 3].at[mb, me], ss, rs, 4)
        if kind == 5:
            return remote(xg_ref.at[mb, at_x], xg_ref.at[mb, at_x], ss, rs, 4)
        which, origin = (kind - PART) % 2, (kind - PART) // 2
        if origin == 0:
            return remote(ins[which].at[mb], outs[which].at[mb, me], ss, rs, 1)
        slot = (at_x, at_y, at_d)[origin - 1]
        return remote(outs[which].at[mb, slot], outs[which].at[mb, slot], ss, rs, 1)

    for mb in range(2):
        for kind in (0, 3, 1, 4, 6, 7):
            copy(mb, kind).start()
    tok = x_ref.shape[1]
    eye = lax.broadcasted_iota(jnp.int32, (tok, tok), 0) == lax.broadcasted_iota(jnp.int32, (tok, tok), 1)
    for mb in range(2):
        routes, gates = route_ref[mb].astype(F32), gate_ref[mb]
        rows = [jnp.sum(jnp.where(eye, arr[:, j : j + 1], 0.0), axis=0, keepdims=True) for arr in (routes, gates) for j in range(TOPK)]
        mine[pl.ds(mb * 8, 8), :] = jnp.concatenate(rows, axis=0)
    rt_ref[me] = mine[...]
    for mask in range(1, NBLK):
        remote(mine, rt_ref.at[me], rt_send.at[mask], rt_recv.at[mask], mask).start()
    for mb in range(2):
        xg_ref[mb, me] = x_ref[mb]
        dyg_ref[mb, me] = dy_ref[mb]
    for mb in range(2):
        copy(mb, 0).wait_recv()
        copy(mb, 5).start()
        copy(mb, 8).start()
        copy(mb, 3).wait_recv()
        copy(mb, 10).start()
        copy(mb, 1).wait_recv()
        copy(mb, 9).start()
        copy(mb, 4).wait_recv()
        copy(mb, 2).start()
        copy(mb, 11).start()
    for mb in range(2):
        copy(mb, 5).wait_recv()
        copy(mb, 12).start()
        copy(mb, 2).wait_recv()
        copy(mb, 13).start()
    for mask in range(1, NBLK):
        remote(mine, rt_ref.at[me], rt_send.at[mask], rt_recv.at[mask], mask).wait()
    for mb in range(2):
        for kind in range(PART, 14):
            copy(mb, kind).wait_recv()
        for kind in range(14):
            copy(mb, kind).wait_send()


def gather_all(x, grad_y, route_idx, gates):
    _, tok, dim = x.shape
    vmem = pl.BlockSpec(memory_space=pltpu.VMEM)
    return pl.pallas_call(
        gather_kernel,
        out_shape=(
            jax.ShapeDtypeStruct((2, NBLK, tok, dim), BF),
            jax.ShapeDtypeStruct((2, NBLK, tok, dim), BF),
            jax.ShapeDtypeStruct((NBLK, 16, tok), F32),
        ),
        in_specs=[vmem] * 4,
        out_specs=(vmem,) * 3,
        scratch_shapes=[
            pltpu.VMEM((16, tok), F32),
            pltpu.SemaphoreType.DMA((2, 14)),
            pltpu.SemaphoreType.DMA((2, 14)),
            pltpu.SemaphoreType.DMA((NBLK,)),
            pltpu.SemaphoreType.DMA((NBLK,)),
        ],
        compiler_params=pltpu.CompilerParams(collective_id=0, has_side_effects=True, vmem_limit_bytes=16 << 20),
        name="gather_tokens",
    )(x, grad_y, route_idx, gates)


def tdot(lhs, rhs):
    return lax.dot_general(lhs, rhs, (((0,), (0,)), ((), ())), preferred_element_type=F32)


def ndot(lhs, rhs):
    return lax.dot_general(lhs, rhs, (((1,), (1,)), ((), ())), preferred_element_type=F32)


def dot(lhs, rhs):
    return jnp.dot(lhs, rhs, preferred_element_type=F32)


def expert_kernel(xg_ref, dyg_ref, rt_ref, wg_hbm, wu_hbm, wd_hbm, part_ref, dg_ref, gg_hbm, gu_hbm, gd_hbm,
                  wgu, wd, ggu, gd, rank, grow, disp0, disp12, xr, qr, dyr, gcol, z0, z12, p0, p12, dc0, dc12, more, in_sem, out_sem):
    tok, dim = xg_ref.shape[2], xg_ref.shape[3]
    ff = wd.shape[1]
    loads = []
    for l in range(NEXP):
        loads.append((
            pltpu.make_async_copy(wg_hbm.at[l], wgu.at[l, :, pl.ds(0, ff)], in_sem.at[l, 0]),
            pltpu.make_async_copy(wu_hbm.at[l], wgu.at[l, :, pl.ds(ff, ff)], in_sem.at[l, 1]),
            pltpu.make_async_copy(wd_hbm.at[l], wd.at[l], in_sem.at[l, 2]),
        ))
        for load in loads[-1]:
            load.start()
    first = (number() * NEXP).astype(F32)

    members = []
    for mb in range(2):
        routes, gates = rt_ref[:, mb * 8 : mb * 8 + 4, :], rt_ref[:, mb * 8 + 4 : mb * 8 + 8, :]
        for l in range(NEXP):
            hit = routes == first + l
            members.append(jnp.sum(jnp.where(hit, 1.0, 0.0), axis=1))
            grow[mb, l] = jnp.sum(jnp.where(hit, gates, 0.0), axis=1)
    member = jnp.concatenate(members, axis=0)
    before = lax.broadcasted_iota(jnp.int32, (tok, tok), 0) < lax.broadcasted_iota(jnp.int32, (tok, tok), 1)
    ranks = jnp.where(member > 0, dot(member.astype(BF), jnp.where(before, 1.0, 0.0).astype(BF)), -1.0)
    for mb in range(2):
        for l in range(NEXP):
            here = ranks[(mb * NEXP + l) * NBLK : (mb * NEXP + l + 1) * NBLK]
            rank[mb, l] = here
            more[mb * NEXP + l] = (jnp.max(here) >= SLAB - 0.5).astype(jnp.int32)
    any_more = [functools.reduce(jnp.maximum, [more[mb * NEXP + l] for l in range(NEXP)]) for mb in range(2)]
    slab_iota = lax.broadcasted_iota(jnp.int32, (SLAB, tok), 0).astype(F32)

    def dispatch(mb, b, slabs, disp):
        hot, gs = [], []
        for s in slabs:
            for l in range(NEXP):
                hot.append(jnp.where(rank[mb, l, pl.ds(b, 1), :] == slab_iota + s * SLAB, 1.0, 0.0))
                gs.append(jnp.broadcast_to(grow[mb, l, pl.ds(b, 1), :], (SLAB, tok)))
        hot = jnp.concatenate(hot, axis=0)
        gate = jnp.sum(hot * jnp.concatenate(gs, axis=0), axis=1, keepdims=True)
        hot = hot.astype(BF)
        disp[mb, b] = hot
        xs = dot(hot, xg_ref[mb, b]).astype(BF)
        dys = dot(hot, dyg_ref[mb, b])
        qs = (gate * dys).astype(BF)
        dys = dys.astype(BF)
        rows = pl.ds(pl.multiple_of(b * SLAB, SLAB), SLAB)
        for i, s in enumerate(slabs):
            pair, half = (0, mb) if s == 0 else (1 + mb, s - 1)
            for l in range(NEXP):
                cut = slice((i * NEXP + l) * SLAB, (i * NEXP + l + 1) * SLAB)
                xr[pair, l, half, rows, :] = xs[cut]
                dyr[pair, l, half, rows, :] = dys[cut]
                qr[pair, l, half, rows, :] = qs[cut]
                gcol[pair, l, half, rows, :] = gate[cut]

    for mb in range(2):
        @pl.loop(0, NBLK)
        def _(b):
            dispatch(mb, b, (0,), disp0)

        @pl.when(any_more[mb] > 0)
        def _():
            @pl.loop(0, NBLK)
            def _(b):
                dispatch(mb, b, (1, 2), disp12)

    rows = 2 * NBLK * SLAB

    def experts(pair, l, fresh):
        xs, qs = xr[pair, l].reshape(rows, dim), qr[pair, l].reshape(rows, dim)
        both = dot(xs, wgu[l]).astype(BF).astype(F32)
        u, v = both[:, :ff], both[:, ff:]
        s = jax.nn.sigmoid(u)
        hidden = (u * s * v).astype(BF)
        out = dot(hidden, wd[l]).astype(BF).astype(F32)
        back = ndot(qs, wd[l])
        d_up = (back * u * s).astype(BF)
        d_gate = (back * v * s * (1.0 + u * (1.0 - s))).astype(BF)
        d_both = jnp.concatenate([d_gate, d_up], axis=1)
        d_in = ndot(d_both, wgu[l]).astype(BF)
        if fresh:
            gd[l] = tdot(hidden, qs)
            ggu[l] = tdot(xs, d_both)
        else:
            gd[l] = gd[l] + tdot(hidden, qs)
            ggu[l] = ggu[l] + tdot(xs, d_both)
        dots = jnp.sum(dyr[pair, l].reshape(rows, dim).astype(F32) * out, axis=1, keepdims=True)
        z = gcol[pair, l].reshape(rows, 1) * out
        hi = z.astype(BF)
        rest = z - hi.astype(F32)
        mid = rest.astype(BF)
        low = (rest - mid.astype(F32)).astype(BF)
        return (hi, mid, low), d_in, dots

    def store0(l, zs, d_in, dots):
        for mb in range(2):
            for b in range(NBLK):
                cut = slice((mb * NBLK + b) * SLAB, (mb * NBLK + b + 1) * SLAB)
                at = pl.multiple_of(l * SLAB, SLAB)
                for i, part in enumerate(zs):
                    z0[mb, b, pl.ds(i * NEXP * SLAB + at, SLAB), :] = part[cut]
                p0[mb, b, pl.ds(at, SLAB), :] = d_in[cut]
                dc0[mb, b, pl.ds(at, SLAB), :] = dots[cut]

    def store12(mb, l, zs, d_in, dots):
        for s in range(2):
            for b in range(NBLK):
                cut = slice((s * NBLK + b) * SLAB, (s * NBLK + b + 1) * SLAB)
                at = pl.multiple_of((s * NEXP + l) * SLAB, SLAB)
                for i, part in enumerate(zs):
                    z12[mb, b, pl.ds(2 * i * NEXP * SLAB + at, SLAB), :] = part[cut]
                p12[mb, b, pl.ds(at, SLAB), :] = d_in[cut]
                dc12[mb, b, pl.ds(at, SLAB), :] = dots[cut]

    def stores(l):
        return (
            pltpu.make_async_copy(ggu.at[l, :, pl.ds(0, ff)], gg_hbm.at[l], out_sem.at[l, 0]),
            pltpu.make_async_copy(ggu.at[l, :, pl.ds(ff, ff)], gu_hbm.at[l], out_sem.at[l, 1]),
            pltpu.make_async_copy(gd.at[l], gd_hbm.at[l], out_sem.at[l, 2]),
        )

    for l in range(NEXP):
        for load in loads[l]:
            load.wait()

    @pl.loop(0, NEXP)
    def _(l):
        store0(l, *experts(0, l, True))

        @pl.loop(0, 2)
        def _(mb):
            flag = more[mb * NEXP + l]

            @pl.when(flag > 0)
            def _():
                store12(mb, l, *experts(1 + mb, l, False))

            @pl.when(flag == 0)
            def _():
                for s in range(2):
                    at = pl.multiple_of((s * NEXP + l) * SLAB, SLAB)
                    for i in range(3):
                        z12[mb, :, pl.ds(2 * i * NEXP * SLAB + at, SLAB), :] = jnp.zeros((NBLK, SLAB, dim), BF)
                    p12[mb, :, pl.ds(at, SLAB), :] = jnp.zeros((NBLK, SLAB, dim), BF)
                    dc12[mb, :, pl.ds(at, SLAB), :] = jnp.zeros((NBLK, SLAB, 1), F32)

        for store in stores(l):
            store.start()

    def by_slot(mb, b, hot, dots):
        spread = hot.astype(F32) * dots
        groups = spread.shape[0] // (NEXP * SLAB)
        routes = rt_ref[b, pl.ds(mb * 8, TOPK), :]
        total = jnp.zeros((TOPK, tok), F32)
        for l in range(NEXP):
            line = sum(jnp.sum(spread[(g * NEXP + l) * SLAB : (g * NEXP + l + 1) * SLAB], axis=0, keepdims=True) for g in range(groups))
            total = total + jnp.where(routes == first + l, line, 0.0)
        return total

    for mb in range(2):
        @pl.loop(0, NBLK)
        def _(b):
            hot = disp0[mb, b]
            part_ref[0, mb, b] = tdot(jnp.concatenate([hot] * 3, axis=0), z0[mb, b])
            part_ref[1, mb, b] = tdot(hot, p0[mb, b])
            dg_ref[b, pl.ds(mb * TOPK, TOPK), :] = by_slot(mb, b, hot, dc0[mb, b])

        @pl.when(any_more[mb] > 0)
        def _():
            @pl.loop(0, NBLK)
            def _(b):
                hot = disp12[mb, b]
                part_ref[0, mb, b] += tdot(jnp.concatenate([hot] * 3, axis=0), z12[mb, b])
                part_ref[1, mb, b] += tdot(hot, p12[mb, b])
                dg_ref[b, pl.ds(mb * TOPK, TOPK), :] += by_slot(mb, b, hot, dc12[mb, b])

    for l in range(NEXP):
        for store in stores(l):
            store.wait()


def run_experts(xg, dyg, rt, w_gate, w_up, w_down):
    _, _, tok, dim = xg.shape
    ff = w_gate.shape[2]
    vmem, hbm = pl.BlockSpec(memory_space=pltpu.VMEM), pl.BlockSpec(memory_space=pl.ANY)
    half = NBLK * SLAB
    one, two = NEXP * SLAB, 2 * NEXP * SLAB
    return pl.pallas_call(
        expert_kernel,
        out_shape=(
            jax.ShapeDtypeStruct((2, 2, NBLK, tok, dim), F32),
            jax.ShapeDtypeStruct((NBLK, 2 * TOPK, tok), F32),
            jax.ShapeDtypeStruct(w_gate.shape, F32),
            jax.ShapeDtypeStruct(w_up.shape, F32),
            jax.ShapeDtypeStruct(w_down.shape, F32),
        ),
        in_specs=[vmem] * 3 + [hbm] * 3,
        out_specs=(vmem, vmem, hbm, hbm, hbm),
        scratch_shapes=[
            pltpu.VMEM((NEXP, dim, 2 * ff), BF),
            pltpu.VMEM((NEXP, ff, dim), BF),
            pltpu.VMEM((NEXP, dim, 2 * ff), F32),
            pltpu.VMEM((NEXP, ff, dim), F32),
            pltpu.VMEM((2, NEXP, NBLK, tok), F32),
            pltpu.VMEM((2, NEXP, NBLK, tok), F32),
            pltpu.VMEM((2, NBLK, one, tok), BF),
            pltpu.VMEM((2, NBLK, two, tok), BF),
            pltpu.VMEM((3, NEXP, 2, half, dim), BF),
            pltpu.VMEM((3, NEXP, 2, half, dim), BF),
            pltpu.VMEM((3, NEXP, 2, half, dim), BF),
            pltpu.VMEM((3, NEXP, 2, half, 1), F32),
            pltpu.VMEM((2, NBLK, 3 * one, dim), BF),
            pltpu.VMEM((2, NBLK, 3 * two, dim), BF),
            pltpu.VMEM((2, NBLK, one, dim), BF),
            pltpu.VMEM((2, NBLK, two, dim), BF),
            pltpu.VMEM((2, NBLK, one, 1), F32),
            pltpu.VMEM((2, NBLK, two, 1), F32),
            pltpu.SMEM((2 * NEXP,), jnp.int32),
            pltpu.SemaphoreType.DMA((NEXP, 3)),
            pltpu.SemaphoreType.DMA((NEXP, 3)),
        ],
        compiler_params=pltpu.CompilerParams(vmem_limit_bytes=52 << 20),
        name="experts",
    )(xg, dyg, rt, w_gate, w_up, w_down)


def combine_kernel(part_ref, dg_ref, y_ref, dx_ref, gg_ref, near, chip_sum, first_in, second_in, out, dg_in,
                   near_send, near_recv, first_send, first_recv, second_send, second_recv, out_send, out_recv, dg_send, dg_recv):
    enter()
    _, row, col, core = coords()
    me = number()
    tok = dg_ref.shape[2]

    def blocks(mask):
        return number(mask) - core

    def to_partner(mb, mask):
        at = pl.ds(blocks(mask), 2)
        i = mask // 2
        return remote(part_ref.at[1 - core, mb, at], near.at[mb, i], near_send.at[mb, i], near_recv.at[mb, i], 1)

    def add_chip(mb, mask):
        to_partner(mb, mask).wait_recv()
        i = mask // 2
        chip_sum[mb, i] = part_ref[core, mb, pl.ds(blocks(mask), 2)] + near[mb, i]

    FIRST, SECOND = (2, 4), (4, 2)

    def first(mb, which):
        mask = (6, FIRST[mb])[which]
        return remote(chip_sum.at[mb, mask // 2], first_in.at[mb, which], first_send.at[mb, which], first_recv.at[mb, which], FIRST[mb])

    def second(mb, h):
        return remote(chip_sum.at[mb, SECOND[mb] // 2, h], second_in.at[mb, h], second_send.at[mb, h], second_recv.at[mb, h], SECOND[mb])

    def dg_copy(mask):
        return remote(dg_ref.at[number(mask)], dg_in.at[me], dg_send.at[mask], dg_recv.at[mask], mask)

    for which in range(4):
        for mb in range(2):
            to_partner(mb, (6, FIRST[mb], SECOND[mb], 0)[which]).start()
    for mask in range(1, NBLK):
        dg_copy(mask).start()
    for which in range(2):
        for mb in range(2):
            add_chip(mb, (6, FIRST[mb])[which])
            first(mb, which).start()
    for mb in range(2):
        add_chip(mb, SECOND[mb])
    for mb in range(2):
        first(mb, 0).wait_recv()
        for h in range(2):
            chip_sum[mb, SECOND[mb] // 2, h] += first_in[mb, 0, h]
            second(mb, h).start()
    dg_in[me] = dg_ref[me]
    for mb in range(2):
        add_chip(mb, 0)
    for mask in range(1, NBLK):
        dg_copy(mask).wait()
    grads = jnp.sum(dg_in[...], axis=0)
    eye = lax.broadcasted_iota(jnp.int32, (tok, tok), 0) == lax.broadcasted_iota(jnp.int32, (tok, tok), 1)
    for mb in range(2):
        cols = [jnp.sum(jnp.where(eye, grads[mb * TOPK + j : mb * TOPK + j + 1, :], 0.0), axis=1, keepdims=True) for j in range(TOPK)]
        gg_ref[mb] = jnp.concatenate(cols, axis=1)
    for mb in range(2):
        first(mb, 1).wait_recv()
        chip_sum[mb, 0] += first_in[mb, 1]

    def handover(mb):
        return remote(out.at[2, mb], out.at[core, mb], out_send.at[mb], out_recv.at[mb], 1)

    for h in range(2):
        for mb in range(2):
            second(mb, h).wait_recv()
            done = (chip_sum[mb, 0, h] + second_in[mb, h]).astype(BF)

            @pl.when(core == h)
            def _():
                out[core, mb] = done

            @pl.when(core != h)
            def _():
                out[2, mb] = done
    for mb in range(2):
        handover(mb).start()
    for mb in range(2):
        handover(mb).wait()
    y_ref[...] = out[0]
    dx_ref[...] = out[1]
    for mb in range(2):
        for i in range(4):
            to_partner(mb, 2 * i).wait_send()
        for i in range(2):
            first(mb, i).wait_send()
            second(mb, i).wait_send()


def combine(part, dg):
    _, _, _, tok, dim = part.shape
    vmem = pl.BlockSpec(memory_space=pltpu.VMEM)
    sem = pltpu.SemaphoreType.DMA
    return pl.pallas_call(
        combine_kernel,
        out_shape=(
            jax.ShapeDtypeStruct((2, tok, dim), BF),
            jax.ShapeDtypeStruct((2, tok, dim), BF),
            jax.ShapeDtypeStruct((2, tok, TOPK), F32),
        ),
        in_specs=[vmem] * 2,
        out_specs=(vmem,) * 3,
        scratch_shapes=[
            pltpu.VMEM((2, 4, 2, tok, dim), F32),
            pltpu.VMEM((2, 4, 2, tok, dim), F32),
            pltpu.VMEM((2, 2, 2, tok, dim), F32),
            pltpu.VMEM((2, 2, tok, dim), F32),
            pltpu.VMEM((3, 2, tok, dim), BF),
            pltpu.VMEM((NBLK, 2 * TOPK, tok), F32),
            sem((2, 4)), sem((2, 4)), sem((2, 2)), sem((2, 2)), sem((2, 2)), sem((2, 2)), sem((2,)), sem((2,)), sem((NBLK,)), sem((NBLK,)),
        ],
        compiler_params=pltpu.CompilerParams(collective_id=1, has_side_effects=True, vmem_limit_bytes=32 << 20),
        name="combine_tokens",
    )(part, dg)


def solution(mesh):
    tok_spec = P(None, ALL_AXES, None)
    w_spec = P(ALL_AXES, None, None)

    def moe_layer(x, route_idx, gates, w_gate, w_up, w_down, grad_y):
        xg, dyg, rt = gather_all(x, grad_y, route_idx, gates)
        part, dg, g_gate, g_up, g_down = run_experts(xg, dyg, rt, w_gate, w_up, w_down)
        y, dx, g_gates = combine(part, dg)
        return y, dx, g_gates, g_gate, g_up, g_down

    return jax.shard_map(moe_layer, mesh=mesh, in_specs=(tok_spec, tok_spec, tok_spec, w_spec, w_spec, w_spec, tok_spec), out_specs=(tok_spec, tok_spec, tok_spec, w_spec, w_spec, w_spec), check_vma=False)
```

time: 175 us -> 75.9 us (0.43)
  Pallas kernels: 0 us -> 66.2 us
  local copies, waits for them, and re-layouts: 56.1 us -> 8.81 us
  waiting for transfers between devices: 43 us -> 0 us
  matrix products: 39.9 us -> 0 us
  starting transfers between devices: 25.6 us -> 0 us
  other arithmetic: 8.13 us -> 0 us
    pallas_call x0 -> x3, Pallas kernels: none -> 66.2 us  [the longest x1 25.6 us: combine(): pl.pallas_call(combine_kernel, out_shape=(jax.ShapeDtypeStruct((2, tok, d...]
    all_to_all x8 -> x0, waiting for transfers between devices: 43 us -> none  [exchange(): return lax.all_to_all(send_buf, GROUP_AXES, 1, 1, tiled=True)]
    dot_general x24 -> x0, matrix products: 39.9 us -> none  [the longest x2 5.96 us: expert_backward(): jnp.einsum('lnd,lnf->ldf', x_rows, d_gate, preferred_element_type=jnp.flo...]
    all_to_all x8 -> x0, starting transfers between devices: 25.6 us -> none  [exchange(): return lax.all_to_all(send_buf, GROUP_AXES, 1, 1, tiled=True)]
    all_to_all x8 -> x0, local copies, waits for them, and re-layouts: 10.3 us -> none  [exchange(): return lax.all_to_all(send_buf, GROUP_AXES, 1, 1, tiled=True)]
    gather x8 -> x0, local copies, waits for them, and re-layouts: 8.83 us -> none  [the longest x4 4.41 us: moe_layer(): jnp.take(dx_back, slot_addr, axis=0).astype(jnp.float32)]
    scatter x2 -> x0, local copies, waits for them, and re-layouts: 5.99 us -> none  [route_tables(): jnp.zeros((local_experts * group_size * capacity,), jnp.float32)]
    reshape x4 -> x0, local copies, waits for them, and re-layouts: 4.72 us -> none  [the longest x2 2.41 us: moe_layer(): out_back = exchange(exp_out.reshape(buf_shape)).reshape(flat_shape)]
  transfers between devices with their start and end apart: 8 -> 0, of which waited for: 6 -> 0; matrix products, arithmetic and copies ran while one was open for 48% -> 0% of each run, Pallas kernels for 0% -> 0%
where the time goes in v1:
time: 75.9 us; the launch traced here: 75.7 us
  Pallas kernels  66.2 us (87%)
  local copies, waits for them, and re-layouts  8.81 us (12%)
    pallas_call x1, Pallas kernels, combine(): pl.pallas_call(combine_kernel, out_shape=(jax.ShapeDtypeStruct((2, tok, d...  25.6 us
    pallas_call x1, Pallas kernels, run_experts(): pl.pallas_call(expert_kernel, out_shape=(jax.ShapeDtypeStruct((2, 2, NBLK...  22.5 us
    pallas_call x1, Pallas kernels, gather_all(): pl.pallas_call(gather_kernel, out_shape=(jax.ShapeDtypeStruct((2, NBLK, t...  18.1 us
    unnamed x13, local copies, waits for them, and re-layouts  8.81 us

profile of v1, /device:TPU:0, one launch (start us, length us, event | category | flops | bytes accessed | tf_op | source)
XLA Modules:
  0.0 75.7 jit_solution(43538357020244778)
XLA Ops:
  0.6 0.8 %copy.13.route_ref = s32[2,96,4]{2,1,0:T(8,128)S(1)} copy(s32[2,96,4]{1,2,0:T(4,128)} %param.8) | data formatting | bytes 6144 | tf_op args[1]
  1.4 0.8 %copy.14.gate_ref = f32[2,96,4]{2,1,0:T(8,128)S(1)} copy(f32[2,96,4]{1,2,0:T(4,128)} %param.9) | data formatting | bytes 6144 | tf_op args[2]
  2.2 0.0 copy-start.2
  2.3 0.9 %copy-done.2 = bf16[2,96,384]{2,1,0:T(8,128)(2,1)S(1)} copy-done((bf16[2,96,384]{2,1,0:T(8,128)(2,1)S(1)}, bf16[2,96,384]{2,1,0:T(8,128)(2,1)}, u32[]{:S(2)}) %copy-start.2) | copy-done | bytes 147480
  3.2 0.0 copy-start.3
  3.2 0.9 %copy-done.3 = bf16[2,96,384]{2,1,0:T(8,128)(2,1)S(1)} copy-done((bf16[2,96,384]{2,1,0:T(8,128)(2,1)S(1)}, bf16[2,96,384]{2,1,0:T(8,128)(2,1)}, u32[]{:S(2)}) %copy-start.3) | copy-done | bytes 147480
  4.1 18.1 %gather_tokens.1 = (bf16[2,8,96,384]{3,2,1,0:T(8,128)(2,1)S(1)}, bf16[2,8,96,384]{3,2,1,0:T(8,128)(2,1)S(1)}, f32[8,16,96]{2,1,0:T(8,128)S(1)}) custom-call(bf16[2,96,384]{2,1,0:T(8,128)(2,1)S(1)} %copy-done.2, bf16[2,96,384]{2,1,0:T(8,128)(2,1)S(1)} %copy-done.3, s32[2,96,4]{2,1,0:T(8,128)S(1)} %copy.13.route_ref, f32[2,96,4]{2,1,0:T(8,128)S(1)} %copy.14.gate_ref), custom_call_target="tpu_custom_call" | custom-call | tf_op jit(solution)/shard_map/gather_tokens/pallas_call | solution.py:112
  22.1 0.0 copy-start.1
  22.2 1.1 %copy-done.1 = bf16[2,8,96,384]{3,2,1,0:T(8,128)(2,1)} copy-done((bf16[2,8,96,384]{3,2,1,0:T(8,128)(2,1)}, bf16[2,8,96,384]{3,2,1,0:T(8,128)(2,1)S(1)}, u32[]{:S(2)}) %copy-start.1) | copy-done | bytes 1179672
  23.2 22.5 %experts.1 = (f32[2,2,8,96,384]{4,3,2,1,0:T(8,128)}, f32[8,8,96]{2,1,0:T(8,128)S(1)}, f32[4,384,384]{2,1,0:T(8,128)}, f32[4,384,384]{2,1,0:T(8,128)}, f32[4,384,384]{2,1,0:T(8,128)}) custom-call(bf16[2,8,96,384]{3,2,1,0:T(8,128)(2,1)S(1)} %get-tuple-element.17.xg_ref, bf16[2,8,96,384]{3,2,1,0:T(8,128)(2,1)} %copy-done.1, ...), custom_call_target="tpu_custom_call" | custom-call | tf_op jit(solution)/shard_map/experts/pallas_call | solution.py:334
  45.7 0.0 copy-start
  45.7 2.3 %copy-done = f32[2,2,8,96,384]{4,3,2,1,0:T(8,128)S(1)} copy-done((f32[2,2,8,96,384]{4,3,2,1,0:T(8,128)S(1)}, f32[2,2,8,96,384]{4,3,2,1,0:T(8,128)}, u32[]{:S(2)}) %copy-start) | copy-done | bytes 4718616
  48.1 25.6 %combine_tokens.1 = (bf16[2,96,384]{2,1,0:T(8,128)(2,1)S(1)}, bf16[2,96,384]{2,1,0:T(8,128)(2,1)S(1)}, f32[2,96,4]{2,1,0:T(8,128)S(1)}) custom-call(f32[2,2,8,96,384]{4,3,2,1,0:T(8,128)S(1)} %copy-done, f32[8,8,96]{2,1,0:T(8,128)S(1)} %get-tuple-element.21.dg_ref), custom_call_target="tpu_custom_call" | custom-call | tf_op jit(solution)/shard_map/combine_tokens/pallas_call | solution.py:468
  73.7 0.7 copy.15
  74.3 0.7 copy.18
  75.0 0.7 copy.19
Async XLA Ops:
  2.2 0.9 %copy-start.2 = (bf16[2,96,384]{2,1,0:T(8,128)(2,1)S(1)}, bf16[2,96,384]{2,1,0:T(8,128)(2,1)}, u32[]{:S(2)}) copy-start(bf16[2,96,384]{2,1,0:T(8,128)(2,1)} %x_ref.1) | copy-start | bytes 442372
  3.2 0.9 %copy-start.3 = (bf16[2,96,384]{2,1,0:T(8,128)(2,1)S(1)}, bf16[2,96,384]{2,1,0:T(8,128)(2,1)}, u32[]{:S(2)}) copy-start(bf16[2,96,384]{2,1,0:T(8,128)(2,1)} %dy_ref.1) | copy-start | bytes 442372
  22.1 1.1 %copy-start.1 = (bf16[2,8,96,384]{3,2,1,0:T(8,128)(2,1)}, bf16[2,8,96,384]{3,2,1,0:T(8,128)(2,1)S(1)}, u32[]{:S(2)}) copy-start(bf16[2,8,96,384]{3,2,1,0:T(8,128)(2,1)S(1)} %get-tuple-element.18.dyg_ref) | copy-start | bytes 3538948
  45.7 2.3 %copy-start = (f32[2,2,8,96,384]{4,3,2,1,0:T(8,128)S(1)}, f32[2,2,8,96,384]{4,3,2,1,0:T(8,128)}, u32[]{:S(2)}) copy-start(f32[2,2,8,96,384]{4,3,2,1,0:T(8,128)} %get-tuple-element.20.part_ref) | copy-start | bytes 14155780

commit v2 on v1

--- a/solution.py
+++ b/solution.py
@@ -43,44 +43,37 @@
     return pltpu.make_async_remote_copy(src_ref=src, dst_ref=dst, send_sem=send_sem, recv_sem=recv_sem, device_id=peer(mask), device_id_type=MESH)
 
 
-def gather_kernel(x_ref, dy_ref, route_ref, gate_ref, xg_ref, dyg_ref, rt_ref, mine, send_sem, recv_sem, rt_send, rt_recv):
-    enter()
+def gather_kernel(x_hbm, dy_hbm, route_hbm, gate_hbm, xg_ref, dyg_ref, rt_ref, route_ref, gate_ref, mine, tab_sem, own_sem, send_sem, recv_sem, rt_send, rt_recv):
     me, at_x, at_y, at_d = number(0), number(2), number(4), number(6)
     outs = (xg_ref, dyg_ref)
-    ins = (x_ref, dy_ref)
     PART = 6
+    own = [[pltpu.make_async_copy(src.at[mb], dst.at[mb, me], own_sem.at[mb, i]) for i, (src, dst) in enumerate(((x_hbm, xg_ref), (dy_hbm, dyg_ref)))] for mb in range(2)]
+    tables = [pltpu.make_async_copy(src, dst, tab_sem.at[i]) for i, (src, dst) in enumerate(((route_hbm, route_ref), (gate_hbm, gate_ref)))]
+    for load in tables + own[0] + own[1]:
+        load.start()
+    for load in tables:
+        load.wait()
+    for mb in range(2):
+        mine[pl.ds(mb * 8, TOPK), :] = route_ref[mb].astype(F32)
+        mine[pl.ds(mb * 8 + TOPK, TOPK), :] = gate_ref[mb]
+    rt_ref[me] = mine[...]
+    enter()
 
     def copy(mb, kind):
-        ss, rs = send_sem.at[mb, kind], recv_sem.at[mb, kind]
-        if kind in (0, 1):
-            return remote(ins[kind].at[mb], outs[kind].at[mb, me], ss, rs, 2)
-        if kind == 2:
-            return remote(dyg_ref.at[mb, at_y], dyg_ref.at[mb, at_y], ss, rs, 2)
-        if kind in (3, 4):
-            return remote(ins[kind - 3].at[mb], outs[kind - 3].at[mb, me], ss, rs, 4)
-        if kind == 5:
-            return remote(xg_ref.at[mb, at_x], xg_ref.at[mb, at_x], ss, rs, 4)
-        which, origin = (kind - PART) % 2, (kind - PART) // 2
-        if origin == 0:
-            return remote(ins[which].at[mb], outs[which].at[mb, me], ss, rs, 1)
-        slot = (at_x, at_y, at_d)[origin - 1]
-        return remote(outs[which].at[mb, slot], outs[which].at[mb, slot], ss, rs, 1)
-
-    for mb in range(2):
-        for kind in (0, 3, 1, 4, 6, 7):
-            copy(mb, kind).start()
-    tok = x_ref.shape[1]
-    eye = lax.broadcasted_iota(jnp.int32, (tok, tok), 0) == lax.broadcasted_iota(jnp.int32, (tok, tok), 1)
-    for mb in range(2):
-        routes, gates = route_ref[mb].astype(F32), gate_ref[mb]
-        rows = [jnp.sum(jnp.where(eye, arr[:, j : j + 1], 0.0), axis=0, keepdims=True) for arr in (routes, gates) for j in range(TOPK)]
-        mine[pl.ds(mb * 8, 8), :] = jnp.concatenate(rows, axis=0)
-    rt_ref[me] = mine[...]
+        if kind < PART:
+            which, slot, mask = ((0, me, 2), (1, me, 2), (1, at_y, 2), (0, me, 4), (1, me, 4), (0, at_x, 4))[kind]
+        else:
+            which, slot, mask = (kind - PART) % 2, (me, at_x, at_y, at_d)[(kind - PART) // 2], 1
+        ref = outs[which].at[mb, slot]
+        return remote(ref, ref, send_sem.at[mb, kind], recv_sem.at[mb, kind], mask)
+
+    for mb in range(2):
+        for kinds, load in zip(((0, 3, 6), (1, 4, 7)), own[mb]):
+            load.wait()
+            for kind in kinds:
+                copy(mb, kind).start()
     for mask in range(1, NBLK):
         remote(mine, rt_ref.at[me], rt_send.at[mask], rt_recv.at[mask], mask).start()
-    for mb in range(2):
-        xg_ref[mb, me] = x_ref[mb]
-        dyg_ref[mb, me] = dy_ref[mb]
     for mb in range(2):
         copy(mb, 0).wait_recv()
         copy(mb, 5).start()
@@ -106,9 +99,9 @@
             copy(mb, kind).wait_send()
 
 
-def gather_all(x, grad_y, route_idx, gates):
+def gather_all(x, grad_y, route_rows, gate_rows):
     _, tok, dim = x.shape
-    vmem = pl.BlockSpec(memory_space=pltpu.VMEM)
+    vmem, hbm = pl.BlockSpec(memory_space=pltpu.VMEM), pl.BlockSpec(memory_space=pltpu.HBM)
     return pl.pallas_call(
         gather_kernel,
         out_shape=(
@@ -116,18 +109,22 @@
             jax.ShapeDtypeStruct((2, NBLK, tok, dim), BF),
             jax.ShapeDtypeStruct((NBLK, 16, tok), F32),
         ),
-        in_specs=[vmem] * 4,
+        in_specs=[hbm] * 4,
         out_specs=(vmem,) * 3,
         scratch_shapes=[
+            pltpu.VMEM((2, TOPK, tok), jnp.int32),
+            pltpu.VMEM((2, TOPK, tok), F32),
             pltpu.VMEM((16, tok), F32),
+            pltpu.SemaphoreType.DMA((2,)),
+            pltpu.SemaphoreType.DMA((2, 2)),
             pltpu.SemaphoreType.DMA((2, 14)),
             pltpu.SemaphoreType.DMA((2, 14)),
             pltpu.SemaphoreType.DMA((NBLK,)),
             pltpu.SemaphoreType.DMA((NBLK,)),
         ],
-        compiler_params=pltpu.CompilerParams(collective_id=0, has_side_effects=True, vmem_limit_bytes=16 << 20),
+        compiler_params=pltpu.CompilerParams(collective_id=0, has_side_effects=True, vmem_limit_bytes=8 << 20),
         name="gather_tokens",
-    )(x, grad_y, route_idx, gates)
+    )(x, grad_y, route_rows, gate_rows)
 
 
 def tdot(lhs, rhs):
@@ -365,7 +362,7 @@
             pltpu.SemaphoreType.DMA((NEXP, 3)),
             pltpu.SemaphoreType.DMA((NEXP, 3)),
         ],
-        compiler_params=pltpu.CompilerParams(vmem_limit_bytes=52 << 20),
+        compiler_params=pltpu.CompilerParams(vmem_limit_bytes=40 << 20),
         name="experts",
     )(xg, dyg, rt, w_gate, w_up, w_down)
 
@@ -375,7 +372,6 @@
     enter()
     _, row, col, core = coords()
     me = number()
-    tok = dg_ref.shape[2]
 
     def blocks(mask):
         return number(mask) - core
@@ -424,10 +420,8 @@
     for mask in range(1, NBLK):
         dg_copy(mask).wait()
     grads = jnp.sum(dg_in[...], axis=0)
-    eye = lax.broadcasted_iota(jnp.int32, (tok, tok), 0) == lax.broadcasted_iota(jnp.int32, (tok, tok), 1)
-    for mb in range(2):
-        cols = [jnp.sum(jnp.where(eye, grads[mb * TOPK + j : mb * TOPK + j + 1, :], 0.0), axis=1, keepdims=True) for j in range(TOPK)]
-        gg_ref[mb] = jnp.concatenate(cols, axis=1)
+    for mb in range(2):
+        gg_ref[mb] = grads[mb * TOPK : (mb + 1) * TOPK]
     for mb in range(2):
         first(mb, 1).wait_recv()
         chip_sum[mb, 0] += first_in[mb, 1]
@@ -470,7 +464,7 @@
         out_shape=(
             jax.ShapeDtypeStruct((2, tok, dim), BF),
             jax.ShapeDtypeStruct((2, tok, dim), BF),
-            jax.ShapeDtypeStruct((2, tok, TOPK), F32),
+            jax.ShapeDtypeStruct((2, TOPK, tok), F32),
         ),
         in_specs=[vmem] * 2,
         out_specs=(vmem,) * 3,
@@ -483,7 +477,7 @@
             pltpu.VMEM((NBLK, 2 * TOPK, tok), F32),
             sem((2, 4)), sem((2, 4)), sem((2, 2)), sem((2, 2)), sem((2, 2)), sem((2, 2)), sem((2,)), sem((2,)), sem((NBLK,)), sem((NBLK,)),
         ],
-        compiler_params=pltpu.CompilerParams(collective_id=1, has_side_effects=True, vmem_limit_bytes=32 << 20),
+        compiler_params=pltpu.CompilerParams(collective_id=1, has_side_effects=True, vmem_limit_bytes=16 << 20),
         name="combine_tokens",
     )(part, dg)
 
@@ -493,9 +487,12 @@
     w_spec = P(ALL_AXES, None, None)
 
     def moe_layer(x, route_idx, gates, w_gate, w_up, w_down, grad_y):
-        xg, dyg, rt = gather_all(x, grad_y, route_idx, gates)
+        stay = lambda arr: pltpu.with_memory_space_constraint(arr, pltpu.HBM)
+        x, grad_y, w_gate, w_up, w_down = (stay(arr) for arr in (x, grad_y, w_gate, w_up, w_down))
+        flat = lambda arr: jnp.transpose(arr, (0, 2, 1))
+        xg, dyg, rt = gather_all(x, grad_y, stay(flat(route_idx)), stay(flat(gates)))
         part, dg, g_gate, g_up, g_down = run_experts(xg, dyg, rt, w_gate, w_up, w_down)
         y, dx, g_gates = combine(part, dg)
-        return y, dx, g_gates, g_gate, g_up, g_down
+        return y, dx, flat(g_gates), g_gate, g_up, g_down
 
     return jax.shard_map(moe_layer, mesh=mesh, in_specs=(tok_spec, tok_spec, tok_spec, w_spec, w_spec, w_spec, tok_spec), out_specs=(tok_spec, tok_spec, tok_spec, w_spec, w_spec, w_spec), check_vma=False)

time: 75.9 us -> 66.4 us (0.87)
  local copies, waits for them, and re-layouts: 8.81 us -> 1.92 us
  Pallas kernels: 66.2 us -> 63.8 us
    pallas_call x1, Pallas kernels: 22.5 us -> 14 us  [run_experts(): pl.pallas_call(expert_kernel, out_shape=(jax.ShapeDtypeStruct((2, 2, NBLK...]
    unnamed x13 -> x3, local copies, waits for them, and re-layouts: 8.81 us -> 1.92 us
    pallas_call x1, Pallas kernels: 25.6 us -> 31 us  [combine(): pl.pallas_call(combine_kernel, out_shape=(jax.ShapeDtypeStruct((2, tok, d...]
    pallas_call x1, Pallas kernels: 18.1 us -> 18.8 us  [gather_all(): pl.pallas_call(gather_kernel, out_shape=(jax.ShapeDtypeStruct((2, NBLK, t...]
where the time goes in v2:
time: 66.4 us
  Pallas kernels  63.8 us (96%)
  local copies, waits for them, and re-layouts  1.92 us (3%)
    pallas_call x1, Pallas kernels, combine(): pl.pallas_call(combine_kernel, out_shape=(jax.ShapeDtypeStruct((2, tok, d...  31 us
    pallas_call x1, Pallas kernels, gather_all(): pl.pallas_call(gather_kernel, out_shape=(jax.ShapeDtypeStruct((2, NBLK, t...  18.8 us
    pallas_call x1, Pallas kernels, run_experts(): pl.pallas_call(expert_kernel, out_shape=(jax.ShapeDtypeStruct((2, 2, NBLK...  14 us
    unnamed x3, local copies, waits for them, and re-layouts  1.92 us

profile of v2, /device:TPU:0, one launch (start us, length us, event | category | flops | bytes accessed | tf_op | source)
XLA Modules:
  0.0 66.4 jit_solution(16739600165827381200)
XLA Ops:
  0.6 18.8 %gather_tokens.1 = (bf16[2,8,96,384]{3,2,1,0:T(8,128)(2,1)S(1)}, bf16[2,8,96,384]{3,2,1,0:T(8,128)(2,1)S(1)}, f32[8,16,96]{2,1,0:T(8,128)S(1)}) custom-call(bf16[2,96,384]{2,1,0:T(8,128)(2,1)} %x_hbm.1, bf16[2,96,384]{2,1,0:T(8,128)(2,1)} %dy_hbm.1, s32[2,4,96]{2,1,0:T(4,128)} %bitcast.4, f32[2,4,96]{2,1,0:T(4,128)} %bitcast.5), custom_call_target="tpu_custom_call" | custom-call | tf_op jit(solution)/shard_map/gather_tokens/pallas_call | solution.py:105
  19.5 14.0 %experts.1 = (f32[2,2,8,96,384]{4,3,2,1,0:T(8,128)S(1)}, f32[8,8,96]{2,1,0:T(8,128)S(1)}, f32[4,384,384]{2,1,0:T(8,128)}, f32[4,384,384]{2,1,0:T(8,128)}, f32[4,384,384]{2,1,0:T(8,128)}) custom-call(bf16[2,8,96,384]{3,2,1,0:T(8,128)(2,1)S(1)} %get-tuple-element.17.xg_ref, bf16[2,8,96,384]{3,2,1,0:T(8,128)(2,1)S(1)} %get-tuple-element.18.dyg_ref, ...), custom_call_target="tpu_custom_call" | custom-call | tf_op jit(solution)/shard_map/experts/pallas_call | solution.py:331
  33.5 31.0 %combine_tokens.1 = (bf16[2,96,384]{2,1,0:T(8,128)(2,1)S(1)}, bf16[2,96,384]{2,1,0:T(8,128)(2,1)S(1)}, f32[2,4,96]{2,1,0:T(4,128)S(1)}) custom-call(f32[2,2,8,96,384]{4,3,2,1,0:T(8,128)S(1)} %get-tuple-element.20.part_ref, f32[8,8,96]{2,1,0:T(8,128)S(1)} %get-tuple-element.21.dg_ref), custom_call_target="tpu_custom_call" | custom-call | tf_op jit(solution)/shard_map/combine_tokens/pallas_call | solution.py:462
  64.5 0.7 copy.16
  65.1 0.7 copy.17
  65.8 0.6 copy.18

commit v3 on v0

v3 whole, which is shorter than its diff:
```python
import functools

import jax
import jax.numpy as jnp
from jax import lax
from jax.experimental import pallas as pl
from jax.experimental.pallas import tpu as pltpu
from jax.sharding import PartitionSpec as P

ALL_AXES = ("rep", "row", "col", "core")
MESH = pl.DeviceIdType.MESH
BF = jnp.bfloat16
F32 = jnp.float32
NBLK = 8
QUAD = 4
NEXP = 4
TOPK = 4
NEAR, FAR = 0, 1
Y, DX = 0, 1


def coords():
    return (lax.axis_index("rep"), lax.axis_index("row"), lax.axis_index("col"), lax.axis_index("core"))


def peer(mask):
    rep, row, col, core = coords()
    flip = lambda pos, bit: 1 - pos if mask & bit else pos
    return (rep, flip(row, 4), flip(col, 2), flip(core, 1))


def number(mask=0):
    _, row, col, core = peer(mask)
    return row * 4 + col * 2 + core


def quad(mask=0):
    _, _, col, core = peer(mask)
    return col * 2 + core


def enter():
    barrier = pltpu.get_barrier_semaphore()
    for mask in range(1, NBLK):
        pl.semaphore_signal(barrier, inc=1, device_id=peer(mask), device_id_type=MESH)
    pl.semaphore_wait(barrier, NBLK - 1)


def remote(src, dst, send_sem, recv_sem, mask):
    return pltpu.make_async_remote_copy(src_ref=src, dst_ref=dst, send_sem=send_sem, recv_sem=recv_sem, device_id=peer(mask), device_id_type=MESH)


def tdot(lhs, rhs):
    return lax.dot_general(lhs, rhs, (((0,), (0,)), ((), ())), preferred_element_type=F32)


def ndot(lhs, rhs):
    return lax.dot_general(lhs, rhs, (((1,), (1,)), ((), ())), preferred_element_type=F32)


def dot(lhs, rhs):
    return jnp.dot(lhs, rhs, preferred_element_type=F32)


def layer_kernel(x_hbm, dy_hbm, route_hbm, gate_hbm, wg_hbm, wu_hbm, wd_hbm,
                 y_ref, dx_ref, gates_ref, gg_ref, gu_ref, gd_ref,
                 xg, dyg, rt, route_tab, gate_tab, mine, wgu, wd, rank, grow, disp, gblk, gcol, xr, qr, uv, hid, outs, zbuf, pbuf, dg,
                 part, near_in, chip_sum, first_in, second_in, dg_in,
                 tab_sem, own_sem, w_sem, g_send, g_recv, rt_send, rt_recv, d_send, d_recv, f_send, f_recv, s_send, s_recv, dg_send, dg_recv):
    tok, dim = xg.shape[2], xg.shape[3]
    ff = wd.shape[1]
    cap = tok // 2
    half = tok // 2
    _, row, col, core = coords()
    me, at_x, at_y, at_d = number(0), number(2), number(4), number(6)
    tokens = (xg, dyg)
    PART = 6

    tables = [pltpu.make_async_copy(src, dst, tab_sem.at[i]) for i, (src, dst) in enumerate(((route_hbm, route_tab), (gate_hbm, gate_tab)))]
    own = [[pltpu.make_async_copy(src.at[mb], dst.at[mb, me], own_sem.at[mb, i]) for i, (src, dst) in enumerate(((x_hbm, xg), (dy_hbm, dyg)))] for mb in range(2)]
    weights = []
    for l in range(NEXP):
        weights += [
            pltpu.make_async_copy(wg_hbm.at[l], wgu.at[l, :, pl.ds(0, ff)], w_sem.at[l, 0]),
            pltpu.make_async_copy(wu_hbm.at[l], wgu.at[l, :, pl.ds(ff, ff)], w_sem.at[l, 1]),
            pltpu.make_async_copy(wd_hbm.at[l], wd.at[l], w_sem.at[l, 2]),
        ]
    for load in own[0] + tables + own[1] + weights:
        load.start()
    for load in tables:
        load.wait()
    for mb in range(2):
        mine[pl.ds(mb * 8, TOPK), :] = route_tab[mb].astype(F32)
        mine[pl.ds(mb * 8 + TOPK, TOPK), :] = gate_tab[mb]
    rt[me] = mine[...]
    enter()

    def tok_copy(mb, kind):
        if kind < PART:
            which, slot, mask = ((0, me, 2), (1, me, 2), (1, at_y, 2), (0, me, 4), (1, me, 4), (0, at_x, 4))[kind]
        else:
            which, slot, mask = (kind - PART) % 2, (me, at_x, at_y, at_d)[(kind - PART) // 2], 1
        ref = tokens[which].at[mb, slot]
        return remote(ref, ref, g_send.at[mb, kind], g_recv.at[mb, kind], mask)

    def send_own(mb, which):
        own[mb][which].wait()
        for kind in (which, 3 + which, PART + which):
            tok_copy(mb, kind).start()

    def relay(mb, kind, *then):
        tok_copy(mb, kind).wait_recv()
        for nxt in then:
            tok_copy(mb, nxt).start()

    def rt_copy(mask):
        return remote(mine, rt.at[me], rt_send.at[mask], rt_recv.at[mask], mask)

    FIRST, SECOND = (2, 4), (4, 2)

    def to_partner(q, mb, mask):
        r, i = q * 2 + mb, mask // 2
        src = part.at[r, FAR if mask & 4 else NEAR, quad(mask | 1)]
        return remote(src, near_in.at[r, i], d_send.at[r, i], d_recv.at[r, i], 1)

    def partner_start(q, mb, far):
        for mask in ((6, 4) if far else (2, 0)):
            to_partner(q, mb, mask).start()

    def chip_add(q, mb, mask):
        r, i = q * 2 + mb, mask // 2
        to_partner(q, mb, mask).wait_recv()
        chip_sum[r, i] = part[r, FAR if mask & 4 else NEAR, quad(mask)] + near_in[r, i]

    def first(q, mb, h, which):
        r, mask = q * 2 + mb, (6, FIRST[h])[which]
        src = chip_sum.at[r, mask // 2, pl.ds(h * half, half)]
        return remote(src, first_in.at[r, h, which], f_send.at[r, h, which], f_recv.at[r, h, which], FIRST[h])

    def second(q, mb, h):
        r = q * 2 + mb
        src = chip_sum.at[r, SECOND[h] // 2, pl.ds(h * half, half)]
        return remote(src, second_in.at[r, h], s_send.at[r, h], s_recv.at[r, h], SECOND[h])

    def far_send(q, mb):
        chip_add(q, mb, 6)
        first(q, mb, 0, 0).start()
        first(q, mb, 1, 0).start()
        chip_add(q, mb, 4)
        first(q, mb, 1, 1).start()

    def near_send(q, mb):
        chip_add(q, mb, 2)
        first(q, mb, 0, 1).start()
        chip_add(q, mb, 0)

    def second_send(q, mb):
        for h in range(2):
            first(q, mb, h, 0).wait_recv()
            chip_sum[q * 2 + mb, SECOND[h] // 2, pl.ds(h * half, half), :] += first_in[q * 2 + mb, h, 0]
            second(q, mb, h).start()

    def finish(q, mb):
        r = q * 2 + mb
        for h in range(2):
            first(q, mb, h, 1).wait_recv()
            second(q, mb, h).wait_recv()
            rows = pl.ds(h * half, half)
            (y_ref, dx_ref)[q][mb, rows, :] = (chip_sum[r, 0, rows, :] + first_in[r, h, 1] + second_in[r, h]).astype(BF)

    first_id = (me * NEXP).astype(F32)
    slot_iota = lax.broadcasted_iota(jnp.int32, (cap, tok), 0).astype(F32)

    def block_of(far, b):
        return (1 - row if far else row) * QUAD + b

    def make_ranks():
        members = []
        for mb in range(2):
            routes, gates = rt[:, mb * 8 : mb * 8 + 4, :], rt[:, mb * 8 + 4 : mb * 8 + 8, :]
            for l in range(NEXP):
                hit = routes == first_id + l
                members.append(jnp.sum(jnp.where(hit, 1.0, 0.0), axis=1))
                grow[mb, l] = jnp.sum(jnp.where(hit, gates, 0.0), axis=1)
        member = jnp.concatenate(members, axis=0)
        before = lax.broadcasted_iota(jnp.int32, (tok, tok), 0) < lax.broadcasted_iota(jnp.int32, (tok, tok), 1)
        ranks = jnp.where(member > 0, dot(member.astype(BF), jnp.where(before, 1.0, 0.0).astype(BF)), -1.0)
        for mb in range(2):
            for l in range(NEXP):
                rank[mb, l] = ranks[(mb * NEXP + l) * NBLK : (mb * NEXP + l + 1) * NBLK]

    def per_block(body):
        @pl.loop(0, QUAD)
        def _(b):
            body(b)

    def dispatch_x(mb, far):
        u = mb * 2 + far

        def body(b):
            blk = block_of(far, b)
            hot = jnp.concatenate([jnp.where(rank[mb, l, pl.ds(blk, 1), :] == slot_iota, 1.0, 0.0) for l in range(NEXP)], axis=0)
            gs = jnp.concatenate([jnp.broadcast_to(grow[mb, l, pl.ds(blk, 1), :], (cap, tok)) for l in range(NEXP)], axis=0)
            gate = jnp.sum(hot * gs, axis=1, keepdims=True)
            hot = hot.astype(BF)
            disp[u, b] = hot
            gblk[u, b] = gate
            xs = dot(hot, xg[mb, blk]).astype(BF)
            rows = pl.ds(pl.multiple_of(b * cap, cap), cap)
            for l in range(NEXP):
                xr[l, u, rows, :] = xs[l * cap : (l + 1) * cap]
                gcol[l, u, rows, :] = gate[l * cap : (l + 1) * cap]

        per_block(body)

    def forward(mb, far):
        u = mb * 2 + far

        @pl.loop(0, NEXP)
        def _(l):
            both = dot(xr[l, u], wgu[l]).astype(BF)
            uv[l, u] = both
            both = both.astype(F32)
            gate_pre, up_pre = both[:, :ff], both[:, ff:]
            hidden = (gate_pre * jax.nn.sigmoid(gate_pre) * up_pre).astype(BF)
            hid[l, u] = hidden
            out = dot(hidden, wd[l]).astype(BF)
            outs[l, u] = out
            z = gcol[l, u] * out.astype(F32)
            hi = z.astype(BF)
            rest = z - hi.astype(F32)
            mid = rest.astype(BF)
            low = (rest - mid.astype(F32)).astype(BF)
            at = pl.multiple_of(l * cap, cap)
            for b in range(QUAD):
                for i, piece in enumerate((hi, mid, low)):
                    zbuf[b, pl.ds(i * NEXP * cap + at, cap), :] = piece[b * cap : (b + 1) * cap]

        def body(b):
            part[Y * 2 + mb, far, b] = tdot(jnp.concatenate([disp[u, b]] * 3, axis=0), zbuf[b])

        per_block(body)

    def dispatch_dy(mb, far):
        u = mb * 2 + far

        def body(b):
            blk = block_of(far, b)
            hot = disp[u, b]
            dys = dot(hot, dyg[mb, blk])
            qs = (gblk[u, b] * dys).astype(BF)
            rows = pl.ds(pl.multiple_of(b * cap, cap), cap)
            hot_f = hot.astype(F32)
            routes = rt[blk, pl.ds(mb * 8, TOPK), :]
            total = jnp.zeros((TOPK, tok), F32)
            for l in range(NEXP):
                cut = slice(l * cap, (l + 1) * cap)
                qr[l, u, rows, :] = qs[cut]
                dots = jnp.sum(dys[cut] * outs[l, u, rows, :].astype(F32), axis=1, keepdims=True)
                line = jnp.sum(hot_f[cut] * dots, axis=0, keepdims=True)
                total = total + jnp.where(routes == first_id + l, line, 0.0)
            dg[blk, pl.ds(mb * TOPK, TOPK), :] = total

        per_block(body)

    def backward(mb, far):
        u = mb * 2 + far

        @pl.loop(0, NEXP)
        def _(l):
            both = uv[l, u].astype(F32)
            gate_pre, up_pre = both[:, :ff], both[:, ff:]
            sig = jax.nn.sigmoid(gate_pre)
            back = ndot(qr[l, u], wd[l])
            d_up = (back * gate_pre * sig).astype(BF)
            d_gate = (back * up_pre * sig * (1.0 + gate_pre * (1.0 - sig))).astype(BF)
            d_both = jnp.concatenate([d_gate, d_up], axis=1)
            uv[l, u] = d_both
            d_in = ndot(d_both, wgu[l]).astype(BF)
            at = pl.multiple_of(l * cap, cap)
            for b in range(QUAD):
                pbuf[b, pl.ds(at, cap), :] = d_in[b * cap : (b + 1) * cap]

        def body(b):
            part[DX * 2 + mb, far, b] = tdot(disp[u, b], pbuf[b])

        per_block(body)

    def weight_grads(l):
        rows = 2 * 2 * QUAD * cap
        gd_ref[l] = tdot(hid[l].reshape(rows, ff), qr[l].reshape(rows, dim))
        xs, d_both = xr[l].reshape(rows, dim), uv[l].reshape(rows, 2 * ff)
        gg_ref[l] = tdot(xs, d_both[:, :ff])
        gu_ref[l] = tdot(xs, d_both[:, ff:])

    send_own(0, 0)
    for mask in range(1, NBLK):
        rt_copy(mask).start()
    send_own(0, 1)
    for mask in range(1, NBLK):
        rt_copy(mask).wait_recv()
    make_ranks()
    for load in weights:
        load.wait()
    relay(0, 0, 5, 8)
    relay(0, 3, 10)
    send_own(1, 0)
    relay(0, 6)
    relay(0, 8)
    dispatch_x(0, NEAR)
    relay(0, 1, 9)
    relay(0, 4, 2, 11)
    forward(0, NEAR)
    partner_start(Y, 0, NEAR)

    relay(0, 5, 12)
    relay(0, 10)
    send_own(1, 1)
    relay(1, 0, 5, 8)
    relay(1, 3, 10)
    near_send(Y, 0)
    relay(0, 12)
    dispatch_x(0, FAR)
    forward(0, FAR)
    partner_start(Y, 0, FAR)

    relay(0, 2, 13)
    relay(1, 5, 12)
    relay(1, 1, 9)
    relay(1, 4, 2, 11)
    for kind in (6, 8, 10, 12):
        relay(1, kind)
    dispatch_x(1, FAR)
    far_send(Y, 0)
    forward(1, FAR)
    partner_start(Y, 1, FAR)

    relay(1, 2, 13)
    dispatch_x(1, NEAR)
    far_send(Y, 1)
    forward(1, NEAR)
    partner_start(Y, 1, NEAR)

    second_send(Y, 0)
    for kind in (7, 9, 11, 13):
        relay(0, kind)
    dispatch_dy(0, FAR)
    near_send(Y, 1)
    backward(0, FAR)
    partner_start(DX, 0, FAR)

    second_send(Y, 1)
    dispatch_dy(0, NEAR)
    far_send(DX, 0)
    backward(0, NEAR)
    partner_start(DX, 0, NEAR)

    finish(Y, 0)
    for kind in (7, 9, 11, 13):
        relay(1, kind)
    dispatch_dy(1, FAR)
    near_send(DX, 0)
    backward(1, FAR)
    partner_start(DX, 1, FAR)

    finish(Y, 1)
    dispatch_dy(1, NEAR)
    far_send(DX, 1)
    second_send(DX, 0)
    backward(1, NEAR)
    partner_start(DX, 1, NEAR)

    def dg_copy(mask):
        return remote(dg.at[number(mask)], dg_in.at[me], dg_send.at[mask], dg_recv.at[mask], mask)

    for mask in range(1, NBLK):
        dg_copy(mask).start()
    dg_in[me] = dg[me]
    weight_grads(0)
    near_send(DX, 1)
    second_send(DX, 1)
    weight_grads(1)
    finish(DX, 0)
    weight_grads(2)
    weight_grads(3)
    for mask in range(1, NBLK):
        dg_copy(mask).wait()
    grads = jnp.sum(dg_in[...], axis=0)
    for mb in range(2):
        gates_ref[mb] = grads[mb * TOPK : (mb + 1) * TOPK]
    finish(DX, 1)
    for mask in range(1, NBLK):
        rt_copy(mask).wait_send()
    for mb in range(2):
        for kind in range(14):
            tok_copy(mb, kind).wait_send()
        for q in (Y, DX):
            for mask in (0, 2, 4, 6):
                to_partner(q, mb, mask).wait_send()
            for h in range(2):
                second(q, mb, h).wait_send()
                for which in range(2):
                    first(q, mb, h, which).wait_send()


def layer(x, grad_y, route_rows, gate_rows, w_gate, w_up, w_down):
    _, tok, dim = x.shape
    ff = w_gate.shape[2]
    cap = tok // 2
    hbm, vmem = pl.BlockSpec(memory_space=pltpu.HBM), pl.BlockSpec(memory_space=pltpu.VMEM)
    dma = pltpu.SemaphoreType.DMA
    unit = QUAD * cap
    shape = jax.ShapeDtypeStruct
    return pl.pallas_call(
        layer_kernel,
        out_shape=(
            shape((2, tok, dim), BF), shape((2, tok, dim), BF), shape((2, TOPK, tok), F32),
            shape(w_gate.shape, F32), shape(w_up.shape, F32), shape(w_down.shape, F32),
        ),
        in_specs=[hbm] * 7,
        out_specs=(vmem,) * 6,
        scratch_shapes=[
            pltpu.VMEM((2, NBLK, tok, dim), BF),
            pltpu.VMEM((2, NBLK, tok, dim), BF),
            pltpu.VMEM((NBLK, 16, tok), F32),
            pltpu.VMEM((2, TOPK, tok), jnp.int32),
            pltpu.VMEM((2, TOPK, tok), F32),
            pltpu.VMEM((16, tok), F32),
            pltpu.VMEM((NEXP, dim, 2 * ff), BF),
            pltpu.VMEM((NEXP, ff, dim), BF),
            pltpu.VMEM((2, NEXP, NBLK, tok), F32),
            pltpu.VMEM((2, NEXP, NBLK, tok), F32),
            pltpu.VMEM((4, QUAD, NEXP * cap, tok), BF),
            pltpu.VMEM((4, QUAD, NEXP * cap, 1), F32),
            pltpu.VMEM((NEXP, 4, unit, 1), F32),
            pltpu.VMEM((NEXP, 4, unit, dim), BF),
            pltpu.VMEM((NEXP, 4, unit, dim), BF),
            pltpu.VMEM((NEXP, 4, unit, 2 * ff), BF),
            pltpu.VMEM((NEXP, 4, unit, ff), BF),
            pltpu.VMEM((NEXP, 4, unit, dim), BF),
            pltpu.VMEM((QUAD, 3 * NEXP * cap, dim), BF),
            pltpu.VMEM((QUAD, NEXP * cap, dim), BF),
            pltpu.VMEM((NBLK, 2 * TOPK, tok), F32),
            pltpu.VMEM((4, 2, QUAD, tok, dim), F32),
            pltpu.VMEM((4, 4, tok, dim), F32),
            pltpu.VMEM((4, 4, tok, dim), F32),
            pltpu.VMEM((4, 2, 2, tok // 2, dim), F32),
            pltpu.VMEM((4, 2, tok // 2, dim), F32),
            pltpu.VMEM((NBLK, 2 * TOPK, tok), F32),
            dma((2,)), dma((2, 2)), dma((NEXP, 3)), dma((2, 14)), dma((2, 14)), dma((NBLK,)), dma((NBLK,)),
            dma((4, 4)), dma((4, 4)), dma((4, 2, 2)), dma((4, 2, 2)), dma((4, 2)), dma((4, 2)), dma((NBLK,)), dma((NBLK,)),
        ],
        compiler_params=pltpu.CompilerParams(collective_id=0, has_side_effects=True, vmem_limit_bytes=46 << 20),
        name="moe_layer",
    )(x, grad_y, route_rows, gate_rows, w_gate, w_up, w_down)


def flush_kernel(*refs):
    count = (len(refs) - 1) // 2
    sem = refs[-1]
    copies = [pltpu.make_async_copy(refs[i], refs[count + i], sem.at[i]) for i in range(count)]
    for copy in copies:
        copy.start()
    for copy in copies:
        copy.wait()


def flush(arrays):
    hbm, vmem = pl.BlockSpec(memory_space=pltpu.HBM), pl.BlockSpec(memory_space=pltpu.VMEM)
    return pl.pallas_call(
        flush_kernel,
        out_shape=tuple(jax.ShapeDtypeStruct(arr.shape, arr.dtype) for arr in arrays),
        in_specs=[vmem] * len(arrays),
        out_specs=(hbm,) * len(arrays),
        scratch_shapes=[pltpu.SemaphoreType.DMA((len(arrays),))],
        compiler_params=pltpu.CompilerParams(vmem_limit_bytes=12 << 20),
        name="write_out",
    )(*arrays)


def solution(mesh):
    tok_spec = P(None, ALL_AXES, None)
    w_spec = P(ALL_AXES, None, None)

    def moe_layer(x, route_idx, gates, w_gate, w_up, w_down, grad_y):
        stay = lambda arr: pltpu.with_memory_space_constraint(arr, pltpu.HBM)
        flat = lambda arr: jnp.transpose(arr, (0, 2, 1))
        args = [stay(arr) for arr in (x, grad_y, flat(route_idx), flat(gates), w_gate, w_up, w_down)]
        y, dx, g_gates, g_gate, g_up, g_down = flush(layer(*args))
        return y, dx, flat(g_gates), g_gate, g_up, g_down

    return jax.shard_map(moe_layer, mesh=mesh, in_specs=(tok_spec, tok_spec, tok_spec, w_spec, w_spec, w_spec, tok_spec), out_specs=(tok_spec, tok_spec, tok_spec, w_spec, w_spec, w_spec), check_vma=False)
```

time: 175 us -> 62.8 us (0.36)
  Pallas kernels: 0 us -> 62 us
  local copies, waits for them, and re-layouts: 56.1 us -> 0 us
  waiting for transfers between devices: 43 us -> 0 us
  matrix products: 39.9 us -> 0 us
  starting transfers between devices: 25.6 us -> 0 us
  other arithmetic: 8.13 us -> 0 us
    pallas_call x0 -> x2, Pallas kernels: none -> 62 us  [the longest x1 58.9 us: layer(): pl.pallas_call(layer_kernel, out_shape=(shape((2, tok, dim), BF), shape((...]
    all_to_all x8 -> x0, waiting for transfers between devices: 43 us -> none  [exchange(): return lax.all_to_all(send_buf, GROUP_AXES, 1, 1, tiled=True)]
    dot_general x24 -> x0, matrix products: 39.9 us -> none  [the longest x2 5.96 us: expert_backward(): jnp.einsum('lnd,lnf->ldf', x_rows, d_gate, preferred_element_type=jnp.flo...]
    all_to_all x8 -> x0, starting transfers between devices: 25.6 us -> none  [exchange(): return lax.all_to_all(send_buf, GROUP_AXES, 1, 1, tiled=True)]
    all_to_all x8 -> x0, local copies, waits for them, and re-layouts: 10.3 us -> none  [exchange(): return lax.all_to_all(send_buf, GROUP_AXES, 1, 1, tiled=True)]
    gather x8 -> x0, local copies, waits for them, and re-layouts: 8.83 us -> none  [the longest x4 4.41 us: moe_layer(): jnp.take(dx_back, slot_addr, axis=0).astype(jnp.float32)]
    unnamed x102 -> x0, local copies, waits for them, and re-layouts: 8.66 us -> none
    scatter x2 -> x0, local copies, waits for them, and re-layouts: 5.99 us -> none  [route_tables(): jnp.zeros((local_experts * group_size * capacity,), jnp.float32)]
  transfers between devices with their start and end apart: 8 -> 0, of which waited for: 6 -> 0; matrix products, arithmetic and copies ran while one was open for 48% -> 0% of each run, Pallas kernels for 0% -> 0%
where the time goes in v3:
time: 62.8 us; the launch traced here: 62.7 us
  Pallas kernels  62 us (99%)
  between operations  0.64 us (1%)
    pallas_call x1, Pallas kernels, layer(): pl.pallas_call(layer_kernel, out_shape=(shape((2, tok, dim), BF), shape((...  58.9 us
    pallas_call x1, Pallas kernels, flush(): pl.pallas_call(flush_kernel, out_shape=tuple((jax.ShapeDtypeStruct(arr.sh...  3.12 us

profile of v3, /device:TPU:0, one launch (start us, length us, event | category | flops | bytes accessed | tf_op | source)
XLA Modules:
  0.0 62.7 jit_solution(1991734229043907474)
XLA Ops:
  0.6 58.9 %moe_layer.1 = (bf16[2,96,384]{2,1,0:T(8,128)(2,1)S(1)}, bf16[2,96,384]{2,1,0:T(8,128)(2,1)S(1)}, f32[2,4,96]{2,1,0:T(4,128)S(1)}, f32[4,384,384]{2,1,0:T(8,128)...) custom-call(bf16[2,96,384]{2,1,0:T(8,128)(2,1)} %x_hbm.1, bf16[2,96,384]{2,1,0:T(8,128)(2,1)} %dy_hbm.1, ...), custom_call_target="tpu_custom_call" | custom-call | tf_op jit(solution)/shard_map/moe_layer/pallas_call | solution.py:414
  59.5 3.1 %write_out.1 = (bf16[2,96,384]{2,1,0:T(8,128)(2,1)}, bf16[2,96,384]{2,1,0:T(8,128)(2,1)}, f32[2,4,96]{2,1,0:T(4,128)}, f32[4,384,384]{2,1,0:T(8,128)}, f32[4,384,384]{2,1,0:T(8,128)}, /*index=5*/f32[4,384,384]{2,1,0:T(8,128)}) custom-call(bf16[2,96,384]{2,1,0:T(8,128)(2,1)S(1)} %get-tuple-element.18.refs_0_, ...), custom_call_target="tpu_custom_call" | custom-call | tf_op jit(solution)/shard_map/write_out/pallas_call | solution.py:470

commit v4 on v3

--- a/solution.py
+++ b/solution.py
@@ -15,6 +15,7 @@
 QUAD = 4
 NEXP = 4
 TOPK = 4
+LANES = 128
 NEAR, FAR = 0, 1
 Y, DX = 0, 1
 
@@ -39,11 +40,14 @@
     return col * 2 + core
 
 
-def enter():
+def announce():
     barrier = pltpu.get_barrier_semaphore()
     for mask in range(1, NBLK):
         pl.semaphore_signal(barrier, inc=1, device_id=peer(mask), device_id_type=MESH)
-    pl.semaphore_wait(barrier, NBLK - 1)
+
+
+def all_entered():
+    pl.semaphore_wait(pltpu.get_barrier_semaphore(), NBLK - 1)
 
 
 def remote(src, dst, send_sem, recv_sem, mask):
@@ -76,6 +80,7 @@
     tokens = (xg, dyg)
     PART = 6
 
+    announce()
     tables = [pltpu.make_async_copy(src, dst, tab_sem.at[i]) for i, (src, dst) in enumerate(((route_hbm, route_tab), (gate_hbm, gate_tab)))]
     own = [[pltpu.make_async_copy(src.at[mb], dst.at[mb, me], own_sem.at[mb, i]) for i, (src, dst) in enumerate(((x_hbm, xg), (dy_hbm, dyg)))] for mb in range(2)]
     weights = []
@@ -85,15 +90,16 @@
             pltpu.make_async_copy(wu_hbm.at[l], wgu.at[l, :, pl.ds(ff, ff)], w_sem.at[l, 1]),
             pltpu.make_async_copy(wd_hbm.at[l], wd.at[l], w_sem.at[l, 2]),
         ]
-    for load in own[0] + tables + own[1] + weights:
+    for load in tables + own[0] + own[1] + weights:
         load.start()
     for load in tables:
         load.wait()
     for mb in range(2):
-        mine[pl.ds(mb * 8, TOPK), :] = route_tab[mb].astype(F32)
-        mine[pl.ds(mb * 8 + TOPK, TOPK), :] = gate_tab[mb]
-    rt[me] = mine[...]
-    enter()
+        mine[mb] = jnp.zeros(mine.shape[1:], F32)
+        mine[mb, pl.ds(0, TOPK), pl.ds(0, tok)] = route_tab[mb].astype(F32)
+        mine[mb, pl.ds(TOPK, TOPK), pl.ds(0, tok)] = gate_tab[mb]
+        rt[mb, me] = mine[mb]
+    all_entered()
 
     def tok_copy(mb, kind):
         if kind < PART:
@@ -103,9 +109,8 @@
         ref = tokens[which].at[mb, slot]
         return remote(ref, ref, g_send.at[mb, kind], g_recv.at[mb, kind], mask)
 
-    def send_own(mb, which):
-        own[mb][which].wait()
-        for kind in (which, 3 + which, PART + which):
+    def send_own(mb, *kinds):
+        for kind in kinds:
             tok_copy(mb, kind).start()
 
     def relay(mb, kind, *then):
@@ -113,8 +118,16 @@
         for nxt in then:
             tok_copy(mb, nxt).start()
 
-    def rt_copy(mask):
-        return remote(mine, rt.at[me], rt_send.at[mask], rt_recv.at[mask], mask)
+    def rt_copy(mb, mask):
+        return remote(mine.at[mb], rt.at[mb, me], rt_send.at[mb, mask], rt_recv.at[mb, mask], mask)
+
+    def send_tables(mb):
+        for mask in (2, 4, 6, 3, 5, 7, 1):
+            rt_copy(mb, mask).start()
+
+    def await_tables(mb):
+        for mask in range(1, NBLK):
+            rt_copy(mb, mask).wait_recv()
 
     FIRST, SECOND = (2, 4), (4, 2)
 
@@ -174,24 +187,22 @@
     def block_of(far, b):
         return (1 - row if far else row) * QUAD + b
 
-    def make_ranks():
+    before = lax.broadcasted_iota(jnp.int32, (tok, tok), 0) < lax.broadcasted_iota(jnp.int32, (tok, tok), 1)
+
+    def make_ranks(mb):
+        routes, gates = rt[mb, :, 0:TOPK, 0:tok], rt[mb, :, TOPK : 2 * TOPK, 0:tok]
         members = []
-        for mb in range(2):
-            routes, gates = rt[:, mb * 8 : mb * 8 + 4, :], rt[:, mb * 8 + 4 : mb * 8 + 8, :]
-            for l in range(NEXP):
-                hit = routes == first_id + l
-                members.append(jnp.sum(jnp.where(hit, 1.0, 0.0), axis=1))
-                grow[mb, l] = jnp.sum(jnp.where(hit, gates, 0.0), axis=1)
+        for l in range(NEXP):
+            hit = routes == first_id + l
+            members.append(jnp.sum(jnp.where(hit, 1.0, 0.0), axis=1))
+            grow[mb, l] = jnp.sum(jnp.where(hit, gates, 0.0), axis=1)
         member = jnp.concatenate(members, axis=0)
-        before = lax.broadcasted_iota(jnp.int32, (tok, tok), 0) < lax.broadcasted_iota(jnp.int32, (tok, tok), 1)
         ranks = jnp.where(member > 0, dot(member.astype(BF), jnp.where(before, 1.0, 0.0).astype(BF)), -1.0)
-        for mb in range(2):
-            for l in range(NEXP):
-                rank[mb, l] = ranks[(mb * NEXP + l) * NBLK : (mb * NEXP + l + 1) * NBLK]
+        for l in range(NEXP):
+            rank[mb, l] = ranks[l * NBLK : (l + 1) * NBLK]
 
     def per_block(body):
-        @pl.loop(0, QUAD)
-        def _(b):
+        for b in range(QUAD):
             body(b)
 
     def dispatch_x(mb, far):
@@ -213,10 +224,10 @@
 
         per_block(body)
 
-    def forward(mb, far):
+    def forward(mb, far, between=lambda: None):
         u = mb * 2 + far
 
-        @pl.loop(0, NEXP)
+        @pl.loop(0, NEXP, unroll=NEXP)
         def _(l):
             both = dot(xr[l, u], wgu[l]).astype(BF)
             uv[l, u] = both
@@ -236,6 +247,8 @@
                 for i, piece in enumerate((hi, mid, low)):
                     zbuf[b, pl.ds(i * NEXP * cap + at, cap), :] = piece[b * cap : (b + 1) * cap]
 
+        between()
+
         def body(b):
             part[Y * 2 + mb, far, b] = tdot(jnp.concatenate([disp[u, b]] * 3, axis=0), zbuf[b])
 
@@ -251,7 +264,7 @@
             qs = (gblk[u, b] * dys).astype(BF)
             rows = pl.ds(pl.multiple_of(b * cap, cap), cap)
             hot_f = hot.astype(F32)
-            routes = rt[blk, pl.ds(mb * 8, TOPK), :]
+            routes = rt[mb, blk, 0:TOPK, 0:tok]
             total = jnp.zeros((TOPK, tok), F32)
             for l in range(NEXP):
                 cut = slice(l * cap, (l + 1) * cap)
@@ -259,14 +272,14 @@
                 dots = jnp.sum(dys[cut] * outs[l, u, rows, :].astype(F32), axis=1, keepdims=True)
                 line = jnp.sum(hot_f[cut] * dots, axis=0, keepdims=True)
                 total = total + jnp.where(routes == first_id + l, line, 0.0)
-            dg[blk, pl.ds(mb * TOPK, TOPK), :] = total
+            dg[blk, pl.ds(mb * TOPK, TOPK), pl.ds(0, tok)] = total
 
         per_block(body)
 
-    def backward(mb, far):
+    def backward(mb, far, between=lambda: None):
         u = mb * 2 + far
 
-        @pl.loop(0, NEXP)
+        @pl.loop(0, NEXP, unroll=NEXP)
         def _(l):
             both = uv[l, u].astype(F32)
             gate_pre, up_pre = both[:, :ff], both[:, ff:]
@@ -281,6 +294,8 @@
             for b in range(QUAD):
                 pbuf[b, pl.ds(at, cap), :] = d_in[b * cap : (b + 1) * cap]
 
+        between()
+
         def body(b):
             part[DX * 2 + mb, far, b] = tdot(disp[u, b], pbuf[b])
 
@@ -293,92 +308,107 @@
         gg_ref[l] = tdot(xs, d_both[:, :ff])
         gu_ref[l] = tdot(xs, d_both[:, ff:])
 
-    send_own(0, 0)
-    for mask in range(1, NBLK):
-        rt_copy(mask).start()
-    send_own(0, 1)
-    for mask in range(1, NBLK):
-        rt_copy(mask).wait_recv()
-    make_ranks()
+    def dg_copy(mask):
+        return remote(dg.at[number(mask)], dg_in.at[me], dg_send.at[mask], dg_recv.at[mask], mask)
+
+    send_tables(0)
+    own[0][0].wait()
+    send_own(0, 0, 3, 6)
+    own[1][0].wait()
+    send_own(1, 0, 3, 6)
+    send_tables(1)
+    own[0][1].wait()
+    send_own(0, 1, 7)
+    own[1][1].wait()
+    send_own(1, 1, 7)
+    await_tables(0)
+    make_ranks(0)
+    await_tables(1)
+    make_ranks(1)
     for load in weights:
         load.wait()
     relay(0, 0, 5, 8)
     relay(0, 3, 10)
-    send_own(1, 0)
+    send_own(0, 4)
     relay(0, 6)
     relay(0, 8)
     dispatch_x(0, NEAR)
-    relay(0, 1, 9)
-    relay(0, 4, 2, 11)
-    forward(0, NEAR)
+    relay(1, 0, 5, 8)
+    relay(1, 3, 10)
+    send_own(1, 4)
+    forward(0, NEAR, lambda: relay(0, 1, 9))
     partner_start(Y, 0, NEAR)
 
+    relay(1, 6)
+    relay(1, 8)
+    dispatch_x(1, NEAR)
     relay(0, 5, 12)
     relay(0, 10)
-    send_own(1, 1)
-    relay(1, 0, 5, 8)
-    relay(1, 3, 10)
-    near_send(Y, 0)
+
+    def during():
+        near_send(Y, 0)
+        relay(1, 1, 9)
+
+    forward(1, NEAR, during)
+    partner_start(Y, 1, NEAR)
+
+    relay(1, 5, 12)
+    relay(1, 10)
     relay(0, 12)
     dispatch_x(0, FAR)
-    forward(0, FAR)
+    relay(0, 4, 2, 11)
+
+    def during():
+        near_send(Y, 1)
+        relay(1, 4, 2, 11)
+
+    forward(0, FAR, during)
     partner_start(Y, 0, FAR)
 
+    relay(1, 12)
+    dispatch_x(1, FAR)
+    forward(1, FAR, lambda: far_send(Y, 0))
+    partner_start(Y, 1, FAR)
+
+    relay(0, 7)
+    relay(0, 9)
+    dispatch_dy(0, NEAR)
     relay(0, 2, 13)
-    relay(1, 5, 12)
-    relay(1, 1, 9)
-    relay(1, 4, 2, 11)
-    for kind in (6, 8, 10, 12):
-        relay(1, kind)
-    dispatch_x(1, FAR)
-    far_send(Y, 0)
-    forward(1, FAR)
-    partner_start(Y, 1, FAR)
-
-    relay(1, 2, 13)
-    dispatch_x(1, NEAR)
-    far_send(Y, 1)
-    forward(1, NEAR)
-    partner_start(Y, 1, NEAR)
+
+    def during():
+        far_send(Y, 1)
+        relay(1, 2, 13)
+
+    backward(0, NEAR, during)
+    partner_start(DX, 0, NEAR)
 
     second_send(Y, 0)
-    for kind in (7, 9, 11, 13):
-        relay(0, kind)
+    relay(0, 11)
+    relay(0, 13)
     dispatch_dy(0, FAR)
-    near_send(Y, 1)
-    backward(0, FAR)
+    backward(0, FAR, lambda: near_send(DX, 0))
     partner_start(DX, 0, FAR)
 
     second_send(Y, 1)
-    dispatch_dy(0, NEAR)
-    far_send(DX, 0)
-    backward(0, NEAR)
-    partner_start(DX, 0, NEAR)
-
-    finish(Y, 0)
     for kind in (7, 9, 11, 13):
         relay(1, kind)
     dispatch_dy(1, FAR)
-    near_send(DX, 0)
-    backward(1, FAR)
+    backward(1, FAR, lambda: far_send(DX, 0))
     partner_start(DX, 1, FAR)
 
-    finish(Y, 1)
+    finish(Y, 0)
     dispatch_dy(1, NEAR)
-    far_send(DX, 1)
-    second_send(DX, 0)
-    backward(1, NEAR)
-    partner_start(DX, 1, NEAR)
-
-    def dg_copy(mask):
-        return remote(dg.at[number(mask)], dg_in.at[me], dg_send.at[mask], dg_recv.at[mask], mask)
-
     for mask in range(1, NBLK):
         dg_copy(mask).start()
     dg_in[me] = dg[me]
+    backward(1, NEAR, lambda: far_send(DX, 1))
+    partner_start(DX, 1, NEAR)
+
+    second_send(DX, 0)
     weight_grads(0)
     near_send(DX, 1)
     second_send(DX, 1)
+    finish(Y, 1)
     weight_grads(1)
     finish(DX, 0)
     weight_grads(2)
@@ -387,11 +417,11 @@
         dg_copy(mask).wait()
     grads = jnp.sum(dg_in[...], axis=0)
     for mb in range(2):
-        gates_ref[mb] = grads[mb * TOPK : (mb + 1) * TOPK]
+        gates_ref[mb] = grads[mb * TOPK : (mb + 1) * TOPK, :tok]
     finish(DX, 1)
-    for mask in range(1, NBLK):
-        rt_copy(mask).wait_send()
     for mb in range(2):
+        for mask in range(1, NBLK):
+            rt_copy(mb, mask).wait_send()
         for kind in range(14):
             tok_copy(mb, kind).wait_send()
         for q in (Y, DX):
@@ -422,10 +452,10 @@
         scratch_shapes=[
             pltpu.VMEM((2, NBLK, tok, dim), BF),
             pltpu.VMEM((2, NBLK, tok, dim), BF),
-            pltpu.VMEM((NBLK, 16, tok), F32),
+            pltpu.VMEM((2, NBLK, 2 * TOPK, LANES), F32),
             pltpu.VMEM((2, TOPK, tok), jnp.int32),
             pltpu.VMEM((2, TOPK, tok), F32),
-            pltpu.VMEM((16, tok), F32),
+            pltpu.VMEM((2, 2 * TOPK, LANES), F32),
             pltpu.VMEM((NEXP, dim, 2 * ff), BF),
             pltpu.VMEM((NEXP, ff, dim), BF),
             pltpu.VMEM((2, NEXP, NBLK, tok), F32),
@@ -440,14 +470,14 @@
             pltpu.VMEM((NEXP, 4, unit, dim), BF),
             pltpu.VMEM((QUAD, 3 * NEXP * cap, dim), BF),
             pltpu.VMEM((QUAD, NEXP * cap, dim), BF),
-            pltpu.VMEM((NBLK, 2 * TOPK, tok), F32),
+            pltpu.VMEM((NBLK, 2 * TOPK, LANES), F32),
             pltpu.VMEM((4, 2, QUAD, tok, dim), F32),
             pltpu.VMEM((4, 4, tok, dim), F32),
             pltpu.VMEM((4, 4, tok, dim), F32),
             pltpu.VMEM((4, 2, 2, tok // 2, dim), F32),
             pltpu.VMEM((4, 2, tok // 2, dim), F32),
-            pltpu.VMEM((NBLK, 2 * TOPK, tok), F32),
-            dma((2,)), dma((2, 2)), dma((NEXP, 3)), dma((2, 14)), dma((2, 14)), dma((NBLK,)), dma((NBLK,)),
+            pltpu.VMEM((NBLK, 2 * TOPK, LANES), F32),
+            dma((2,)), dma((2, 2)), dma((NEXP, 3)), dma((2, 14)), dma((2, 14)), dma((2, NBLK)), dma((2, NBLK)),
             dma((4, 4)), dma((4, 4)), dma((4, 2, 2)), dma((4, 2, 2)), dma((4, 2)), dma((4, 2)), dma((NBLK,)), dma((NBLK,)),
         ],
         compiler_params=pltpu.CompilerParams(collective_id=0, has_side_effects=True, vmem_limit_bytes=46 << 20),

time: 62.8 us -> 51.4 us (0.82)
  Pallas kernels: 62 us -> 50.5 us
    pallas_call x1, Pallas kernels: 58.9 us -> 47.3 us  [layer(): pl.pallas_call(layer_kernel, out_shape=(shape((2, tok, dim), BF), shape((...]
where the time goes in v4:
time: 51.4 us; the launch traced here: 51.3 us
  Pallas kernels  50.5 us (98%)
  between operations  0.8 us (2%)
    pallas_call x1, Pallas kernels, layer(): pl.pallas_call(layer_kernel, out_shape=(shape((2, tok, dim), BF), shape((...  47.3 us
    pallas_call x1, Pallas kernels, flush(): pl.pallas_call(flush_kernel, out_shape=tuple((jax.ShapeDtypeStruct(arr.sh...  3.12 us

profile of v4, /device:TPU:0, one launch (start us, length us, event | category | flops | bytes accessed | tf_op | source)
XLA Modules:
  0.0 51.3 jit_solution(13847556548359314635)
XLA Ops:
  0.6 47.3 %moe_layer.1 = (bf16[2,96,384]{2,1,0:T(8,128)(2,1)S(1)}, bf16[2,96,384]{2,1,0:T(8,128)(2,1)S(1)}, f32[2,4,96]{2,1,0:T(4,128)S(1)}, f32[4,384,384]{2,1,0:T(8,128)...) custom-call(bf16[2,96,384]{2,1,0:T(8,128)(2,1)} %x_hbm.1, bf16[2,96,384]{2,1,0:T(8,128)(2,1)} %dy_hbm.1, ...), custom_call_target="tpu_custom_call" | custom-call | tf_op jit(solution)/shard_map/moe_layer/pallas_call | solution.py:444
  48.0 3.1 %write_out.1 = (bf16[2,96,384]{2,1,0:T(8,128)(2,1)}, bf16[2,96,384]{2,1,0:T(8,128)(2,1)}, f32[2,4,96]{2,1,0:T(4,128)}, f32[4,384,384]{2,1,0:T(8,128)}, f32[4,384,384]{2,1,0:T(8,128)}, /*index=5*/f32[4,384,384]{2,1,0:T(8,128)}) custom-call(bf16[2,96,384]{2,1,0:T(8,128)(2,1)S(1)} %get-tuple-element.18.refs_0_, ...), custom_call_target="tpu_custom_call" | custom-call | tf_op jit(solution)/shard_map/write_out/pallas_call | solution.py:500

commit v5 on v4

v5 whole, which is shorter than its diff:
```python
import functools

import jax
import jax.numpy as jnp
from jax import lax
from jax.experimental import pallas as pl
from jax.experimental.pallas import tpu as pltpu
from jax.sharding import PartitionSpec as P

ALL_AXES = ("rep", "row", "col", "core")
MESH = pl.DeviceIdType.MESH
BF = jnp.bfloat16
F32 = jnp.float32
NBLK = 8
QUAD = 4
NEXP = 4
TOPK = 4
LANES = 128
OWN, XY0, XY1, DIAG = 0, 1, 2, 3
Y, DX = 0, 1


def coords():
    return (lax.axis_index("rep"), lax.axis_index("row"), lax.axis_index("col"), lax.axis_index("core"))


def peer(mask):
    rep, row, col, core = coords()
    flip = lambda pos, bit: 1 - pos if mask & bit else pos
    return (rep, flip(row, 4), flip(col, 2), flip(core, 1))


def number(mask=0):
    _, row, col, core = peer(mask)
    return row * 4 + col * 2 + core


def announce():
    barrier = pltpu.get_barrier_semaphore()
    for mask in range(1, NBLK):
        pl.semaphore_signal(barrier, inc=1, device_id=peer(mask), device_id_type=MESH)


def all_entered():
    pl.semaphore_wait(pltpu.get_barrier_semaphore(), NBLK - 1)


def remote(src, dst, send_sem, recv_sem, mask):
    return pltpu.make_async_remote_copy(src_ref=src, dst_ref=dst, send_sem=send_sem, recv_sem=recv_sem, device_id=peer(mask), device_id_type=MESH)


def tdot(lhs, rhs):
    return lax.dot_general(lhs, rhs, (((0,), (0,)), ((), ())), preferred_element_type=F32)


def ndot(lhs, rhs):
    return lax.dot_general(lhs, rhs, (((1,), (1,)), ((), ())), preferred_element_type=F32)


def dot(lhs, rhs):
    return jnp.dot(lhs, rhs, preferred_element_type=F32)


CHIPS = {
    OWN: ((0, 0), (1, 0)),
    XY0: ((0, 2), (0, 4)),
    XY1: ((1, 4), (1, 2)),
    DIAG: ((0, 6), (1, 6)),
}
BLOCKS = {unit: tuple((mb, mask, c) for mb, mask in chips for c in range(2)) for unit, chips in CHIPS.items()}


def layer_kernel(x_hbm, dy_hbm, route_hbm, gate_hbm, wg_hbm, wu_hbm, wd_hbm,
                 y_ref, dx_ref, gates_ref, gg_ref, gu_ref, gd_ref,
                 xg, dyg, rt, route_tab, gate_tab, mine, wgu, wd, rank, grow, disp, gblk, gcol, xr, qr, uv, hid, outs, zbuf, pbuf, dg,
                 part, near_in, chip_sum, first_in, second_in, dg_in,
                 tab_sem, own_sem, w_sem, g_send, g_recv, rt_send, rt_recv, d_send, d_recv, f_send, f_recv, s_send, s_recv, dg_send, dg_recv):
    tok, dim = xg.shape[2], xg.shape[3]
    ff = wd.shape[1]
    cap = tok // 2
    _, row, col, core = coords()
    me, at_x, at_y, at_d = number(0), number(2), number(4), number(6)
    tokens = (xg, dyg)
    PART = 6

    announce()
    tables = [pltpu.make_async_copy(src, dst, tab_sem.at[i]) for i, (src, dst) in enumerate(((route_hbm, route_tab), (gate_hbm, gate_tab)))]
    own = [[pltpu.make_async_copy(src.at[mb], dst.at[mb, me], own_sem.at[mb, i]) for i, (src, dst) in enumerate(((x_hbm, xg), (dy_hbm, dyg)))] for mb in range(2)]
    weights = []
    for l in range(NEXP):
        weights += [
            pltpu.make_async_copy(wg_hbm.at[l], wgu.at[l, :, pl.ds(0, ff)], w_sem.at[l, 0]),
            pltpu.make_async_copy(wu_hbm.at[l], wgu.at[l, :, pl.ds(ff, ff)], w_sem.at[l, 1]),
            pltpu.make_async_copy(wd_hbm.at[l], wd.at[l], w_sem.at[l, 2]),
        ]
    for load in tables + own[0] + own[1] + weights:
        load.start()
    for load in tables:
        load.wait()
    mine[...] = jnp.zeros(mine.shape, F32)
    for mb in range(2):
        mine[pl.ds(mb * 2 * TOPK, TOPK), pl.ds(0, tok)] = route_tab[mb].astype(F32)
        mine[pl.ds(mb * 2 * TOPK + TOPK, TOPK), pl.ds(0, tok)] = gate_tab[mb]
    rt[me] = mine[...]
    all_entered()

    def tok_copy(mb, kind):
        if kind < PART:
            slot, mask = (me, 2) if kind in (0, 1) else (me, 4) if kind in (3, 4) else ((at_x, 4), (at_y, 2))[mb]
            which = int(kind in (1, 2, 4))
        else:
            which, slot, mask = (kind - PART) % 2, (me, at_x, at_y, at_d)[(kind - PART) // 2], 1
        ref = tokens[which].at[mb, slot]
        return remote(ref, ref, g_send.at[mb, kind], g_recv.at[mb, kind], mask)

    def send_own(mb, *kinds):
        for kind in kinds:
            tok_copy(mb, kind).start()

    def relay(mb, kind, *then):
        tok_copy(mb, kind).wait_recv()
        for nxt in then:
            tok_copy(mb, nxt).start()

    def rt_copy(mask):
        return remote(mine, rt.at[me], rt_send.at[mask], rt_recv.at[mask], mask)

    FIRST, SECOND = (2, 4), (4, 2)

    def to_partner(q, mb, mask):
        r, i = q * 2 + mb, mask // 2
        return remote(part.at[r, i, 1 - core], near_in.at[r, i], d_send.at[r, i], d_recv.at[r, i], 1)

    def partner_start(q, unit):
        for mb, mask in CHIPS[unit]:
            to_partner(q, mb, mask).start()

    def chip_add(q, mb, mask):
        r, i = q * 2 + mb, mask // 2
        to_partner(q, mb, mask).wait_recv()
        chip_sum[r, i] = part[r, i, core] + near_in[r, i]

    def first(q, mb, which):
        r = q * 2 + mb
        src = chip_sum.at[r, (3, FIRST[mb] // 2)[which]]
        return remote(src, first_in.at[r, which], f_send.at[r, which], f_recv.at[r, which], FIRST[mb])

    def second(q, mb):
        r = q * 2 + mb
        return remote(chip_sum.at[r, SECOND[mb] // 2], second_in.at[r], s_send.at[r], s_recv.at[r], SECOND[mb])

    def leave(q, unit):
        for mb, mask in CHIPS[unit]:
            if mask in (6, FIRST[mb]):
                chip_add(q, mb, mask)
                first(q, mb, 0 if mask == 6 else 1).start()
        for mb, mask in CHIPS[unit]:
            if mask not in (6, FIRST[mb]):
                chip_add(q, mb, mask)

    def second_send(q, mb):
        first(q, mb, 0).wait_recv()
        chip_sum[q * 2 + mb, SECOND[mb] // 2] += first_in[q * 2 + mb, 0]
        second(q, mb).start()

    def finish(q, mb):
        r = q * 2 + mb
        first(q, mb, 1).wait_recv()
        second(q, mb).wait_recv()
        (y_ref, dx_ref)[q][mb] = (chip_sum[r, 0] + first_in[r, 1] + second_in[r]).astype(BF)

    first_id = (me * NEXP).astype(F32)
    slot_iota = lax.broadcasted_iota(jnp.int32, (cap, tok), 0).astype(F32)

    def block_of(mask, c):
        return number(mask) - core + c

    before = lax.broadcasted_iota(jnp.int32, (tok, tok), 0) < lax.broadcasted_iota(jnp.int32, (tok, tok), 1)

    def make_ranks(mask):
        tables = rt[pl.ds(number(mask) - core, 2)]
        members, weights_of = [], []
        for mb in range(2):
            at = mb * 2 * TOPK
            routes, gates = tables[:, at : at + TOPK, :tok], tables[:, at + TOPK : at + 2 * TOPK, :tok]
            for l in range(NEXP):
                hit = routes == first_id + l
                members.append(jnp.sum(jnp.where(hit, 1.0, 0.0), axis=1))
                weights_of.append(jnp.sum(jnp.where(hit, gates, 0.0), axis=1))
        member = jnp.concatenate(members, axis=0)
        rank[mask // 2] = jnp.where(member > 0, dot(member.astype(BF), jnp.where(before, 1.0, 0.0).astype(BF)), -1.0)
        grow[mask // 2] = jnp.concatenate(weights_of, axis=0)

    def dispatch_x(unit):
        for b, (mb, mask, c) in enumerate(BLOCKS[unit]):
            lines = [pl.ds((mb * NEXP + l) * 2 + c, 1) for l in range(NEXP)]
            hot = jnp.concatenate([jnp.where(rank[mask // 2, line, :] == slot_iota, 1.0, 0.0) for line in lines], axis=0)
            gs = jnp.concatenate([jnp.broadcast_to(grow[mask // 2, line, :], (cap, tok)) for line in lines], axis=0)
            gate = jnp.sum(hot * gs, axis=1, keepdims=True)
            hot = hot.astype(BF)
            disp[unit, b] = hot
            gblk[unit, b] = gate
            xs = dot(hot, xg[mb, block_of(mask, c)]).astype(BF)
            rows = pl.ds(b * cap, cap)
            for l in range(NEXP):
                xr[l, unit, rows, :] = xs[l * cap : (l + 1) * cap]
                gcol[l, unit, rows, :] = gate[l * cap : (l + 1) * cap]

    def forward(u, between=lambda: None):
        @pl.loop(0, NEXP, unroll=NEXP)
        def _(l):
            both = dot(xr[l, u], wgu[l]).astype(BF)
            uv[l, u] = both
            both = both.astype(F32)
            gate_pre, up_pre = both[:, :ff], both[:, ff:]
            hidden = (gate_pre * jax.nn.sigmoid(gate_pre) * up_pre).astype(BF)
            hid[l, u] = hidden
            out = dot(hidden, wd[l]).astype(BF)
            outs[l, u] = out
            z = gcol[l, u] * out.astype(F32)
            hi = z.astype(BF)
            rest = z - hi.astype(F32)
            mid = rest.astype(BF)
            low = (rest - mid.astype(F32)).astype(BF)
            at = pl.multiple_of(l * cap, cap)
            for b in range(QUAD):
                for i, piece in enumerate((hi, mid, low)):
                    zbuf[b, pl.ds(i * NEXP * cap + at, cap), :] = piece[b * cap : (b + 1) * cap]

        between()

        for b, (mb, mask, c) in enumerate(BLOCKS[u]):
            part[Y * 2 + mb, mask // 2, c] = tdot(jnp.concatenate([disp[u, b]] * 3, axis=0), zbuf[b])

    def dispatch_dy(unit):
        for b, (mb, mask, c) in enumerate(BLOCKS[unit]):
            blk = block_of(mask, c)
            hot = disp[unit, b]
            dys = dot(hot, dyg[mb, blk])
            qs = (gblk[unit, b] * dys).astype(BF)
            rows = pl.ds(b * cap, cap)
            hot_f = hot.astype(F32)
            routes = rt[blk, mb * 2 * TOPK : mb * 2 * TOPK + TOPK, 0:tok]
            total = jnp.zeros((TOPK, tok), F32)
            for l in range(NEXP):
                cut = slice(l * cap, (l + 1) * cap)
                qr[l, unit, rows, :] = qs[cut]
                dots = jnp.sum(dys[cut] * outs[l, unit, rows, :].astype(F32), axis=1, keepdims=True)
                line = jnp.sum(hot_f[cut] * dots, axis=0, keepdims=True)
                total = total + jnp.where(routes == first_id + l, line, 0.0)
            dg[blk, pl.ds(mb * TOPK, TOPK), pl.ds(0, tok)] = total

    def backward(u, between=lambda: None):
        @pl.loop(0, NEXP, unroll=NEXP)
        def _(l):
            both = uv[l, u].astype(F32)
            gate_pre, up_pre = both[:, :ff], both[:, ff:]
            sig = jax.nn.sigmoid(gate_pre)
            back = ndot(qr[l, u], wd[l])
            d_up = (back * gate_pre * sig).astype(BF)
            d_gate = (back * up_pre * sig * (1.0 + gate_pre * (1.0 - sig))).astype(BF)
            d_both = jnp.concatenate([d_gate, d_up], axis=1)
            uv[l, u] = d_both
            d_in = ndot(d_both, wgu[l]).astype(BF)
            at = pl.multiple_of(l * cap, cap)
            for b in range(QUAD):
                pbuf[b, pl.ds(at, cap), :] = d_in[b * cap : (b + 1) * cap]

        between()

        for b, (mb, mask, c) in enumerate(BLOCKS[u]):
            part[DX * 2 + mb, mask // 2, c] = tdot(disp[u, b], pbuf[b])

    def weight_grads(l):
        rows = 2 * 2 * QUAD * cap
        gd_ref[l] = tdot(hid[l].reshape(rows, ff), qr[l].reshape(rows, dim))
        xs, d_both = xr[l].reshape(rows, dim), uv[l].reshape(rows, 2 * ff)
        gg_ref[l] = tdot(xs, d_both[:, :ff])
        gu_ref[l] = tdot(xs, d_both[:, ff:])

    def dg_copy(mask):
        return remote(dg.at[number(mask)], dg_in.at[me], dg_send.at[mask], dg_recv.at[mask], mask)

    for mask in (1, 2, 4, 3, 5, 6, 7):
        rt_copy(mask).start()
    for mb in range(2):
        own[mb][0].wait()
        send_own(mb, 6, 0, 3)
    own[0][1].wait()
    send_own(0, 7, 1)
    own[1][1].wait()
    send_own(1, 7)
    rt_copy(1).wait_recv()
    make_ranks(0)
    for load in weights:
        load.wait()
    relay(0, 6)
    relay(1, 6)
    dispatch_x(OWN)
    forward(OWN)
    partner_start(Y, OWN)

    relay(0, 0, 5, 8)
    relay(0, 3, 10)
    send_own(1, 4)
    for mask in (2, 3, 4, 5):
        rt_copy(mask).wait_recv()
    make_ranks(2)
    make_ranks(4)
    relay(0, 7)
    relay(1, 7)
    dispatch_dy(OWN)
    relay(1, 3, 5, 10)
    relay(1, 0, 8)
    send_own(1, 1)
    send_own(0, 4)
    relay(0, 8)
    relay(0, 10)
    dispatch_x(XY0)
    forward(XY0, lambda: relay(0, 1, 2, 9))
    partner_start(Y, XY0)

    for mask in (6, 7):
        rt_copy(mask).wait_recv()
    make_ranks(6)
    relay(0, 5, 12)
    relay(1, 8)
    relay(1, 10)
    dispatch_x(XY1)

    def during():
        relay(1, 4, 2, 11)
        relay(1, 5, 12)
        leave(Y, XY0)

    forward(XY1, during)
    partner_start(Y, XY1)

    relay(0, 12)
    relay(1, 12)
    dispatch_x(DIAG)
    relay(0, 4, 11)
    relay(1, 1, 9)

    def during():
        relay(0, 2, 13)
        leave(Y, XY1)

    forward(DIAG, during)
    partner_start(Y, DIAG)

    relay(1, 2, 13)
    leave(Y, OWN)
    relay(0, 9)
    relay(0, 11)
    dispatch_dy(XY0)
    leave(Y, DIAG)
    relay(1, 9)
    relay(1, 11)
    dispatch_dy(XY1)
    relay(0, 13)
    relay(1, 13)
    dispatch_dy(DIAG)
    for mask in range(1, NBLK):
        dg_copy(mask).start()
    dg_in[me] = dg[me]
    backward(DIAG)
    partner_start(DX, DIAG)

    backward(XY0, lambda: leave(DX, DIAG))
    partner_start(DX, XY0)

    def during():
        leave(DX, XY0)
        second_send(Y, 0)
        second_send(Y, 1)

    backward(XY1, during)
    partner_start(DX, XY1)

    def during():
        leave(DX, XY1)
        second_send(DX, 0)
        second_send(DX, 1)

    backward(OWN, during)
    partner_start(DX, OWN)

    weight_grads(0)
    leave(DX, OWN)
    weight_grads(1)
    weight_grads(2)
    weight_grads(3)
    finish(Y, 0)
    finish(Y, 1)
    for mask in range(1, NBLK):
        dg_copy(mask).wait()
    grads = jnp.sum(dg_in[...], axis=0)
    for mb in range(2):
        gates_ref[mb] = grads[mb * TOPK : (mb + 1) * TOPK, :tok]
    finish(DX, 0)
    finish(DX, 1)
    for mask in range(1, NBLK):
        rt_copy(mask).wait_send()
    for mb in range(2):
        for kind in range(14):
            tok_copy(mb, kind).wait_send()
        for q in (Y, DX):
            for mask in (0, 2, 4, 6):
                to_partner(q, mb, mask).wait_send()
            for which in range(2):
                first(q, mb, which).wait_send()
            second(q, mb).wait_send()


def layer(x, grad_y, route_rows, gate_rows, w_gate, w_up, w_down):
    _, tok, dim = x.shape
    ff = w_gate.shape[2]
    cap = tok // 2
    hbm, vmem = pl.BlockSpec(memory_space=pltpu.HBM), pl.BlockSpec(memory_space=pltpu.VMEM)
    dma = pltpu.SemaphoreType.DMA
    unit = QUAD * cap
    shape = jax.ShapeDtypeStruct
    return pl.pallas_call(
        layer_kernel,
        out_shape=(
            shape((2, tok, dim), BF), shape((2, tok, dim), BF), shape((2, TOPK, tok), F32),
            shape(w_gate.shape, F32), shape(w_up.shape, F32), shape(w_down.shape, F32),
        ),
        in_specs=[hbm] * 7,
        out_specs=(vmem,) * 6,
        scratch_shapes=[
            pltpu.VMEM((2, NBLK, tok, dim), BF),
            pltpu.VMEM((2, NBLK, tok, dim), BF),
            pltpu.VMEM((NBLK, 4 * TOPK, LANES), F32),
            pltpu.VMEM((2, TOPK, tok), jnp.int32),
            pltpu.VMEM((2, TOPK, tok), F32),
            pltpu.VMEM((4 * TOPK, LANES), F32),
            pltpu.VMEM((NEXP, dim, 2 * ff), BF),
            pltpu.VMEM((NEXP, ff, dim), BF),
            pltpu.VMEM((4, 4 * NEXP, tok), F32),
            pltpu.VMEM((4, 4 * NEXP, tok), F32),
            pltpu.VMEM((4, QUAD, NEXP * cap, tok), BF),
            pltpu.VMEM((4, QUAD, NEXP * cap, 1), F32),
            pltpu.VMEM((NEXP, 4, unit, 1), F32),
            pltpu.VMEM((NEXP, 4, unit, dim), BF),
            pltpu.VMEM((NEXP, 4, unit, dim), BF),
            pltpu.VMEM((NEXP, 4, unit, 2 * ff), BF),
            pltpu.VMEM((NEXP, 4, unit, ff), BF),
            pltpu.VMEM((NEXP, 4, unit, dim), BF),
            pltpu.VMEM((QUAD, 3 * NEXP * cap, dim), BF),
            pltpu.VMEM((QUAD, NEXP * cap, dim), BF),
            pltpu.VMEM((NBLK, 2 * TOPK, LANES), F32),
            pltpu.VMEM((4, 4, 2, tok, dim), F32),
            pltpu.VMEM((4, 4, tok, dim), F32),
            pltpu.VMEM((4, 4, tok, dim), F32),
            pltpu.VMEM((4, 2, tok, dim), F32),
            pltpu.VMEM((4, tok, dim), F32),
            pltpu.VMEM((NBLK, 2 * TOPK, LANES), F32),
            dma((2,)), dma((2, 2)), dma((NEXP, 3)), dma((2, 14)), dma((2, 14)), dma((NBLK,)), dma((NBLK,)),
            dma((4, 4)), dma((4, 4)), dma((4, 2)), dma((4, 2)), dma((4,)), dma((4,)), dma((NBLK,)), dma((NBLK,)),
        ],
        compiler_params=pltpu.CompilerParams(collective_id=0, has_side_effects=True, vmem_limit_bytes=46 << 20),
        name="moe_layer",
    )(x, grad_y, route_rows, gate_rows, w_gate, w_up, w_down)


def flush_kernel(*refs):
    count = (len(refs) - 1) // 2
    sem = refs[-1]
    copies = [pltpu.make_async_copy(refs[i], refs[count + i], sem.at[i]) for i in range(count)]
    for copy in copies:
        copy.start()
    for copy in copies:
        copy.wait()


def flush(arrays):
    hbm, vmem = pl.BlockSpec(memory_space=pltpu.HBM), pl.BlockSpec(memory_space=pltpu.VMEM)
    return pl.pallas_call(
        flush_kernel,
        out_shape=tuple(jax.ShapeDtypeStruct(arr.shape, arr.dtype) for arr in arrays),
        in_specs=[vmem] * len(arrays),
        out_specs=(hbm,) * len(arrays),
        scratch_shapes=[pltpu.SemaphoreType.DMA((len(arrays),))],
        compiler_params=pltpu.CompilerParams(vmem_limit_bytes=12 << 20),
        name="write_out",
    )(*arrays)


def solution(mesh):
    tok_spec = P(None, ALL_AXES, None)
    w_spec = P(ALL_AXES, None, None)

    def moe_layer(x, route_idx, gates, w_gate, w_up, w_down, grad_y):
        stay = lambda arr: pltpu.with_memory_space_constraint(arr, pltpu.HBM)
        flat = lambda arr: jnp.transpose(arr, (0, 2, 1))
        args = [stay(arr) for arr in (x, grad_y, flat(route_idx), flat(gates), w_gate, w_up, w_down)]
        y, dx, g_gates, g_gate, g_up, g_down = flush(layer(*args))
        return y, dx, flat(g_gates), g_gate, g_up, g_down

    return jax.shard_map(moe_layer, mesh=mesh, in_specs=(tok_spec, tok_spec, tok_spec, w_spec, w_spec, w_spec, tok_spec), out_specs=(tok_spec, tok_spec, tok_spec, w_spec, w_spec, w_spec), check_vma=False)
```

time: 51.4 us -> 46.6 us (0.907)
  Pallas kernels: 50.5 us -> 45.7 us
    pallas_call x1, Pallas kernels: 47.3 us -> 42.5 us  [layer(): pl.pallas_call(layer_kernel, out_shape=(shape((2, tok, dim), BF), shape((...]
where the time goes in v5:
time: 46.6 us; the launch traced here: 46.5 us
  Pallas kernels  45.7 us (98%)
  between operations  0.8 us (2%)
    pallas_call x1, Pallas kernels, layer(): pl.pallas_call(layer_kernel, out_shape=(shape((2, tok, dim), BF), shape((...  42.5 us
    pallas_call x1, Pallas kernels, flush(): pl.pallas_call(flush_kernel, out_shape=tuple((jax.ShapeDtypeStruct(arr.sh...  3.12 us

profile of v5, /device:TPU:0, one launch (start us, length us, event | category | flops | bytes accessed | tf_op | source)
XLA Modules:
  0.0 46.5 jit_solution(11279122450344784422)
XLA Ops:
  0.6 42.5 %moe_layer.1 = (bf16[2,96,384]{2,1,0:T(8,128)(2,1)S(1)}, bf16[2,96,384]{2,1,0:T(8,128)(2,1)S(1)}, f32[2,4,96]{2,1,0:T(4,128)S(1)}, f32[4,384,384]{2,1,0:T(8,128)...) custom-call(bf16[2,96,384]{2,1,0:T(8,128)(2,1)} %x_hbm.1, bf16[2,96,384]{2,1,0:T(8,128)(2,1)} %dy_hbm.1, ...), custom_call_target="tpu_custom_call" | custom-call | tf_op jit(solution)/shard_map/moe_layer/pallas_call | solution.py:424
  43.2 3.1 %write_out.1 = (bf16[2,96,384]{2,1,0:T(8,128)(2,1)}, bf16[2,96,384]{2,1,0:T(8,128)(2,1)}, f32[2,4,96]{2,1,0:T(4,128)}, f32[4,384,384]{2,1,0:T(8,128)}, f32[4,384,384]{2,1,0:T(8,128)}, /*index=5*/f32[4,384,384]{2,1,0:T(8,128)}) custom-call(bf16[2,96,384]{2,1,0:T(8,128)(2,1)S(1)} %get-tuple-element.18.refs_0_, ...), custom_call_target="tpu_custom_call" | custom-call | tf_op jit(solution)/shard_map/write_out/pallas_call | solution.py:480

commit v6 on v5

--- a/solution.py
+++ b/solution.py
@@ -126,6 +126,7 @@
         return remote(mine, rt.at[me], rt_send.at[mask], rt_recv.at[mask], mask)
 
     FIRST, SECOND = (2, 4), (4, 2)
+    half = tok // 2
 
     def to_partner(q, mb, mask):
         r, i = q * 2 + mb, mask // 2
@@ -140,34 +141,38 @@
         to_partner(q, mb, mask).wait_recv()
         chip_sum[r, i] = part[r, i, core] + near_in[r, i]
 
-    def first(q, mb, which):
+    def rows_of(h):
+        return pl.ds(h * half, half)
+
+    def first(q, mb, h, which):
         r = q * 2 + mb
-        src = chip_sum.at[r, (3, FIRST[mb] // 2)[which]]
-        return remote(src, first_in.at[r, which], f_send.at[r, which], f_recv.at[r, which], FIRST[mb])
-
-    def second(q, mb):
+        src = chip_sum.at[r, (3, FIRST[h] // 2)[which], rows_of(h)]
+        return remote(src, first_in.at[r, h, which], f_send.at[r, h, which], f_recv.at[r, h, which], FIRST[h])
+
+    def second(q, mb, h):
         r = q * 2 + mb
-        return remote(chip_sum.at[r, SECOND[mb] // 2], second_in.at[r], s_send.at[r], s_recv.at[r], SECOND[mb])
+        return remote(chip_sum.at[r, SECOND[h] // 2, rows_of(h)], second_in.at[r, h], s_send.at[r, h], s_recv.at[r, h], SECOND[h])
 
     def leave(q, unit):
         for mb, mask in CHIPS[unit]:
-            if mask in (6, FIRST[mb]):
-                chip_add(q, mb, mask)
-                first(q, mb, 0 if mask == 6 else 1).start()
-        for mb, mask in CHIPS[unit]:
-            if mask not in (6, FIRST[mb]):
-                chip_add(q, mb, mask)
+            chip_add(q, mb, mask)
+            for h in range(2):
+                if mask in (6, FIRST[h]):
+                    first(q, mb, h, 0 if mask == 6 else 1).start()
 
     def second_send(q, mb):
-        first(q, mb, 0).wait_recv()
-        chip_sum[q * 2 + mb, SECOND[mb] // 2] += first_in[q * 2 + mb, 0]
-        second(q, mb).start()
+        for h in range(2):
+            first(q, mb, h, 0).wait_recv()
+            chip_sum[q * 2 + mb, SECOND[h] // 2, rows_of(h), :] += first_in[q * 2 + mb, h, 0]
+            second(q, mb, h).start()
 
     def finish(q, mb):
         r = q * 2 + mb
-        first(q, mb, 1).wait_recv()
-        second(q, mb).wait_recv()
-        (y_ref, dx_ref)[q][mb] = (chip_sum[r, 0] + first_in[r, 1] + second_in[r]).astype(BF)
+        for h in range(2):
+            first(q, mb, h, 1).wait_recv()
+            second(q, mb, h).wait_recv()
+            done = chip_sum[r, 0, rows_of(h), :] + first_in[r, h, 1] + second_in[r, h]
+            (y_ref, dx_ref)[q][mb, rows_of(h), :] = done.astype(BF)
 
     first_id = (me * NEXP).astype(F32)
     slot_iota = lax.broadcasted_iota(jnp.int32, (cap, tok), 0).astype(F32)
@@ -207,25 +212,30 @@
                 gcol[l, unit, rows, :] = gate[l * cap : (l + 1) * cap]
 
     def forward(u, between=lambda: None):
-        @pl.loop(0, NEXP, unroll=NEXP)
-        def _(l):
-            both = dot(xr[l, u], wgu[l]).astype(BF)
+        def spread(l, out):
+            z = gcol[l, u] * out.astype(F32)
+            hi = z.astype(BF)
+            rest = z - hi.astype(F32)
+            mid = rest.astype(BF)
+            low = (rest - mid.astype(F32)).astype(BF)
+            for b in range(QUAD):
+                for i, piece in enumerate((hi, mid, low)):
+                    zbuf[b, pl.ds((i * NEXP + l) * cap, cap), :] = piece[b * cap : (b + 1) * cap]
+
+        both, out = dot(xr[0, u], wgu[0]).astype(BF), None
+        for l in range(NEXP):
+            ahead = dot(xr[l + 1, u], wgu[l + 1]).astype(BF) if l + 1 < NEXP else None
             uv[l, u] = both
             both = both.astype(F32)
             gate_pre, up_pre = both[:, :ff], both[:, ff:]
             hidden = (gate_pre * jax.nn.sigmoid(gate_pre) * up_pre).astype(BF)
             hid[l, u] = hidden
+            if out is not None:
+                spread(l - 1, out)
             out = dot(hidden, wd[l]).astype(BF)
             outs[l, u] = out
-            z = gcol[l, u] * out.astype(F32)
-            hi = z.astype(BF)
-            rest = z - hi.astype(F32)
-            mid = rest.astype(BF)
-            low = (rest - mid.astype(F32)).astype(BF)
-            at = pl.multiple_of(l * cap, cap)
-            for b in range(QUAD):
-                for i, piece in enumerate((hi, mid, low)):
-                    zbuf[b, pl.ds(i * NEXP * cap + at, cap), :] = piece[b * cap : (b + 1) * cap]
+            both = ahead
+        spread(NEXP - 1, out)
 
         between()
 
@@ -251,20 +261,20 @@
             dg[blk, pl.ds(mb * TOPK, TOPK), pl.ds(0, tok)] = total
 
     def backward(u, between=lambda: None):
-        @pl.loop(0, NEXP, unroll=NEXP)
-        def _(l):
+        back = ndot(qr[0, u], wd[0])
+        for l in range(NEXP):
+            ahead = ndot(qr[l + 1, u], wd[l + 1]) if l + 1 < NEXP else None
             both = uv[l, u].astype(F32)
             gate_pre, up_pre = both[:, :ff], both[:, ff:]
             sig = jax.nn.sigmoid(gate_pre)
-            back = ndot(qr[l, u], wd[l])
             d_up = (back * gate_pre * sig).astype(BF)
             d_gate = (back * up_pre * sig * (1.0 + gate_pre * (1.0 - sig))).astype(BF)
             d_both = jnp.concatenate([d_gate, d_up], axis=1)
             uv[l, u] = d_both
             d_in = ndot(d_both, wgu[l]).astype(BF)
-            at = pl.multiple_of(l * cap, cap)
             for b in range(QUAD):
-                pbuf[b, pl.ds(at, cap), :] = d_in[b * cap : (b + 1) * cap]
+                pbuf[b, pl.ds(l * cap, cap), :] = d_in[b * cap : (b + 1) * cap]
+            back = ahead
 
         between()
 
@@ -275,8 +285,9 @@
         rows = 2 * 2 * QUAD * cap
         gd_ref[l] = tdot(hid[l].reshape(rows, ff), qr[l].reshape(rows, dim))
         xs, d_both = xr[l].reshape(rows, dim), uv[l].reshape(rows, 2 * ff)
-        gg_ref[l] = tdot(xs, d_both[:, :ff])
-        gu_ref[l] = tdot(xs, d_both[:, ff:])
+        grads = tdot(xs, d_both)
+        gg_ref[l] = grads[:, :ff]
+        gu_ref[l] = grads[:, ff:]
 
     def dg_copy(mask):
         return remote(dg.at[number(mask)], dg_in.at[me], dg_send.at[mask], dg_recv.at[mask], mask)
@@ -289,7 +300,7 @@
     own[0][1].wait()
     send_own(0, 7, 1)
     own[1][1].wait()
-    send_own(1, 7)
+    send_own(1, 7, 4)
     rt_copy(1).wait_recv()
     make_ranks(0)
     for load in weights:
@@ -302,7 +313,6 @@
 
     relay(0, 0, 5, 8)
     relay(0, 3, 10)
-    send_own(1, 4)
     for mask in (2, 3, 4, 5):
         rt_copy(mask).wait_recv()
     make_ranks(2)
@@ -323,13 +333,13 @@
     for mask in (6, 7):
         rt_copy(mask).wait_recv()
     make_ranks(6)
-    relay(0, 5, 12)
+    relay(1, 4, 2, 11)
     relay(1, 8)
     relay(1, 10)
     dispatch_x(XY1)
+    relay(0, 5, 12)
 
     def during():
-        relay(1, 4, 2, 11)
         relay(1, 5, 12)
         leave(Y, XY0)
 
@@ -380,11 +390,11 @@
 
     def during():
         leave(DX, XY1)
-        second_send(DX, 0)
-        second_send(DX, 1)
 
     backward(OWN, during)
     partner_start(DX, OWN)
+    second_send(DX, 0)
+    second_send(DX, 1)
 
     weight_grads(0)
     leave(DX, OWN)
@@ -408,9 +418,10 @@
         for q in (Y, DX):
             for mask in (0, 2, 4, 6):
                 to_partner(q, mb, mask).wait_send()
-            for which in range(2):
-                first(q, mb, which).wait_send()
-            second(q, mb).wait_send()
+            for h in range(2):
+                second(q, mb, h).wait_send()
+                for which in range(2):
+                    first(q, mb, h, which).wait_send()
 
 
 def layer(x, grad_y, route_rows, gate_rows, w_gate, w_up, w_down):
@@ -454,11 +465,11 @@
             pltpu.VMEM((4, 4, 2, tok, dim), F32),
             pltpu.VMEM((4, 4, tok, dim), F32),
             pltpu.VMEM((4, 4, tok, dim), F32),
-            pltpu.VMEM((4, 2, tok, dim), F32),
-            pltpu.VMEM((4, tok, dim), F32),
+            pltpu.VMEM((4, 2, 2, tok // 2, dim), F32),
+            pltpu.VMEM((4, 2, tok // 2, dim), F32),
             pltpu.VMEM((NBLK, 2 * TOPK, LANES), F32),
             dma((2,)), dma((2, 2)), dma((NEXP, 3)), dma((2, 14)), dma((2, 14)), dma((NBLK,)), dma((NBLK,)),
-            dma((4, 4)), dma((4, 4)), dma((4, 2)), dma((4, 2)), dma((4,)), dma((4,)), dma((NBLK,)), dma((NBLK,)),
+            dma((4, 4)), dma((4, 4)), dma((4, 2, 2)), dma((4, 2, 2)), dma((4, 2)), dma((4, 2)), dma((NBLK,)), dma((NBLK,)),
         ],
         compiler_params=pltpu.CompilerParams(collective_id=0, has_side_effects=True, vmem_limit_bytes=46 << 20),
         name="moe_layer",

time: 46.6 us -> 44.5 us (0.955)
  Pallas kernels: 45.7 us -> 43.6 us
    pallas_call x1, Pallas kernels: 42.5 us -> 40.5 us  [layer(): pl.pallas_call(layer_kernel, out_shape=(shape((2, tok, dim), BF), shape((...]
where the time goes in v6:
time: 44.5 us; the launch traced here: 44.4 us
  Pallas kernels  43.6 us (98%)
  between operations  0.8 us (2%)
    pallas_call x1, Pallas kernels, layer(): pl.pallas_call(layer_kernel, out_shape=(shape((2, tok, dim), BF), shape((...  40.5 us
    pallas_call x1, Pallas kernels, flush(): pl.pallas_call(flush_kernel, out_shape=tuple((jax.ShapeDtypeStruct(arr.sh...  3.12 us

profile of v6, /device:TPU:0, one launch (start us, length us, event | category | flops | bytes accessed | tf_op | source)
XLA Modules:
  0.0 44.4 jit_solution(993982111947474020)
XLA Ops:
  0.6 40.5 %moe_layer.1 = (bf16[2,96,384]{2,1,0:T(8,128)(2,1)S(1)}, bf16[2,96,384]{2,1,0:T(8,128)(2,1)S(1)}, f32[2,4,96]{2,1,0:T(4,128)S(1)}, f32[4,384,384]{2,1,0:T(8,128)...) custom-call(bf16[2,96,384]{2,1,0:T(8,128)(2,1)} %x_hbm.1, bf16[2,96,384]{2,1,0:T(8,128)(2,1)} %dy_hbm.1, ...), custom_call_target="tpu_custom_call" | custom-call | tf_op jit(solution)/shard_map/moe_layer/pallas_call | solution.py:435
  41.1 3.1 %write_out.1 = (bf16[2,96,384]{2,1,0:T(8,128)(2,1)}, bf16[2,96,384]{2,1,0:T(8,128)(2,1)}, f32[2,4,96]{2,1,0:T(4,128)}, f32[4,384,384]{2,1,0:T(8,128)}, f32[4,384,384]{2,1,0:T(8,128)}, /*index=5*/f32[4,384,384]{2,1,0:T(8,128)}) custom-call(bf16[2,96,384]{2,1,0:T(8,128)(2,1)S(1)} %get-tuple-element.18.refs_0_, ...), custom_call_target="tpu_custom_call" | custom-call | tf_op jit(solution)/shard_map/write_out/pallas_call | solution.py:491

commit v7 on v6

--- a/solution.py
+++ b/solution.py
@@ -70,9 +70,16 @@
 BLOCKS = {unit: tuple((mb, mask, c) for mb, mask in chips for c in range(2)) for unit, chips in CHIPS.items()}
 
 
+PAIRS = (
+    ((0, 6), (1, 6)), ((0, 7), (1, 7)), ((0, 8), (0, 10)), ((1, 8), (1, 10)),
+    ((0, 9), (0, 11)), ((1, 9), (1, 11)), ((0, 12), (1, 12)), ((0, 13), (1, 13)),
+)
+PAIR = {item: 12 + i for i, pair in enumerate(PAIRS) for item in pair}
+
+
 def layer_kernel(x_hbm, dy_hbm, route_hbm, gate_hbm, wg_hbm, wu_hbm, wd_hbm,
                  y_ref, dx_ref, gates_ref, gg_ref, gu_ref, gd_ref,
-                 xg, dyg, rt, route_tab, gate_tab, mine, wgu, wd, rank, grow, disp, gblk, gcol, xr, qr, uv, hid, outs, zbuf, pbuf, dg,
+                 xg, dyg, rt, route_tab, gate_tab, wgu, wd, rank, grow, disp, gblk, gcol, xr, qr, uv, hid, outs, zbuf, pbuf, dg,
                  part, near_in, chip_sum, first_in, second_in, dg_in,
                  tab_sem, own_sem, w_sem, g_send, g_recv, rt_send, rt_recv, d_send, d_recv, f_send, f_recv, s_send, s_recv, dg_send, dg_recv):
     tok, dim = xg.shape[2], xg.shape[3]
@@ -86,22 +93,19 @@
     announce()
     tables = [pltpu.make_async_copy(src, dst, tab_sem.at[i]) for i, (src, dst) in enumerate(((route_hbm, route_tab), (gate_hbm, gate_tab)))]
     own = [[pltpu.make_async_copy(src.at[mb], dst.at[mb, me], own_sem.at[mb, i]) for i, (src, dst) in enumerate(((x_hbm, xg), (dy_hbm, dyg)))] for mb in range(2)]
-    weights = []
-    for l in range(NEXP):
-        weights += [
-            pltpu.make_async_copy(wg_hbm.at[l], wgu.at[l, :, pl.ds(0, ff)], w_sem.at[l, 0]),
-            pltpu.make_async_copy(wu_hbm.at[l], wgu.at[l, :, pl.ds(ff, ff)], w_sem.at[l, 1]),
-            pltpu.make_async_copy(wd_hbm.at[l], wd.at[l], w_sem.at[l, 2]),
-        ]
+    weights = [
+        pltpu.make_async_copy(wg_hbm, wgu.at[:, :, pl.ds(0, ff)], w_sem.at[0]),
+        pltpu.make_async_copy(wu_hbm, wgu.at[:, :, pl.ds(ff, ff)], w_sem.at[1]),
+        pltpu.make_async_copy(wd_hbm, wd, w_sem.at[2]),
+    ]
     for load in tables + own[0] + own[1] + weights:
         load.start()
     for load in tables:
         load.wait()
-    mine[...] = jnp.zeros(mine.shape, F32)
+    rt[me] = jnp.zeros(rt.shape[1:], F32)
     for mb in range(2):
-        mine[pl.ds(mb * 2 * TOPK, TOPK), pl.ds(0, tok)] = route_tab[mb].astype(F32)
-        mine[pl.ds(mb * 2 * TOPK + TOPK, TOPK), pl.ds(0, tok)] = gate_tab[mb]
-    rt[me] = mine[...]
+        rt[me, pl.ds(mb * 2 * TOPK, TOPK), pl.ds(0, tok)] = route_tab[mb].astype(F32)
+        rt[me, pl.ds(mb * 2 * TOPK + TOPK, TOPK), pl.ds(0, tok)] = gate_tab[mb]
     all_entered()
 
     def tok_copy(mb, kind):
@@ -111,7 +115,13 @@
         else:
             which, slot, mask = (kind - PART) % 2, (me, at_x, at_y, at_d)[(kind - PART) // 2], 1
         ref = tokens[which].at[mb, slot]
-        return remote(ref, ref, g_send.at[mb, kind], g_recv.at[mb, kind], mask)
+        arrival = mb * PART + kind if kind < PART else PAIR[mb, kind]
+        return remote(ref, ref, g_send.at[which], g_recv.at[arrival], mask)
+
+    def await_pair(mb, kind):
+        which = (kind - PART) % 2
+        two = tokens[which].at[0, pl.ds(0, 2)]
+        remote(two, two, g_send.at[which], g_recv.at[PAIR[mb, kind]], 1).wait_recv()
 
     def send_own(mb, *kinds):
         for kind in kinds:
@@ -122,24 +132,25 @@
         for nxt in then:
             tok_copy(mb, nxt).start()
 
-    def rt_copy(mask):
-        return remote(mine, rt.at[me], rt_send.at[mask], rt_recv.at[mask], mask)
+    def rt_copy(kind):
+        slot, mask = ((me, 1), (me, 2), (me, 4), (at_x, 4), (at_x, 1), (at_y, 1), (at_d, 1))[kind]
+        return remote(rt.at[slot], rt.at[slot], rt_send.at[0], rt_recv.at[kind], mask)
+
+    def rt_relay(kind, *then):
+        rt_copy(kind).wait_recv()
+        for nxt in then:
+            rt_copy(nxt).start()
 
     FIRST, SECOND = (2, 4), (4, 2)
     half = tok // 2
 
-    def to_partner(q, mb, mask):
+    def to_partner(q, unit, mb, mask):
         r, i = q * 2 + mb, mask // 2
-        return remote(part.at[r, i, 1 - core], near_in.at[r, i], d_send.at[r, i], d_recv.at[r, i], 1)
+        return remote(part.at[r, i, 1 - core], near_in.at[r, i], d_send.at[0], d_recv.at[q, unit], 1)
 
     def partner_start(q, unit):
         for mb, mask in CHIPS[unit]:
-            to_partner(q, mb, mask).start()
-
-    def chip_add(q, mb, mask):
-        r, i = q * 2 + mb, mask // 2
-        to_partner(q, mb, mask).wait_recv()
-        chip_sum[r, i] = part[r, i, core] + near_in[r, i]
+            to_partner(q, unit, mb, mask).start()
 
     def rows_of(h):
         return pl.ds(h * half, half)
@@ -147,31 +158,38 @@
     def first(q, mb, h, which):
         r = q * 2 + mb
         src = chip_sum.at[r, (3, FIRST[h] // 2)[which], rows_of(h)]
-        return remote(src, first_in.at[r, h, which], f_send.at[r, h, which], f_recv.at[r, h, which], FIRST[h])
+        return remote(src, first_in.at[r, which, h], f_send.at[0], f_recv.at[r, which], FIRST[h])
 
     def second(q, mb, h):
         r = q * 2 + mb
-        return remote(chip_sum.at[r, SECOND[h] // 2, rows_of(h)], second_in.at[r, h], s_send.at[r, h], s_recv.at[r, h], SECOND[h])
+        return remote(chip_sum.at[r, SECOND[h] // 2, rows_of(h)], second_in.at[r, h], s_send.at[0], s_recv.at[r], SECOND[h])
+
+    def await_both(ref, sem):
+        remote(ref, ref, s_send.at[0], sem, 2).wait_recv()
 
     def leave(q, unit):
+        two = near_in.at[0, pl.ds(0, 2)]
+        remote(two, two, d_send.at[0], d_recv.at[q, unit], 1).wait_recv()
         for mb, mask in CHIPS[unit]:
-            chip_add(q, mb, mask)
+            r, i = q * 2 + mb, mask // 2
+            chip_sum[r, i] = part[r, i, core] + near_in[r, i]
             for h in range(2):
                 if mask in (6, FIRST[h]):
                     first(q, mb, h, 0 if mask == 6 else 1).start()
 
     def second_send(q, mb):
+        r = q * 2 + mb
+        await_both(first_in.at[r, 0], f_recv.at[r, 0])
         for h in range(2):
-            first(q, mb, h, 0).wait_recv()
-            chip_sum[q * 2 + mb, SECOND[h] // 2, rows_of(h), :] += first_in[q * 2 + mb, h, 0]
+            chip_sum[r, SECOND[h] // 2, rows_of(h), :] += first_in[r, 0, h]
             second(q, mb, h).start()
 
     def finish(q, mb):
         r = q * 2 + mb
+        await_both(first_in.at[r, 1], f_recv.at[r, 1])
+        await_both(second_in.at[r], s_recv.at[r])
         for h in range(2):
-            first(q, mb, h, 1).wait_recv()
-            second(q, mb, h).wait_recv()
-            done = chip_sum[r, 0, rows_of(h), :] + first_in[r, h, 1] + second_in[r, h]
+            done = chip_sum[r, 0, rows_of(h), :] + first_in[r, 1, h] + second_in[r, h]
             (y_ref, dx_ref)[q][mb, rows_of(h), :] = done.astype(BF)
 
     first_id = (me * NEXP).astype(F32)
@@ -211,7 +229,7 @@
                 xr[l, unit, rows, :] = xs[l * cap : (l + 1) * cap]
                 gcol[l, unit, rows, :] = gate[l * cap : (l + 1) * cap]
 
-    def forward(u, between=lambda: None):
+    def forward(u, between=lambda: None, early=lambda: None):
         def spread(l, out):
             z = gcol[l, u] * out.astype(F32)
             hi = z.astype(BF)
@@ -235,6 +253,8 @@
             out = dot(hidden, wd[l]).astype(BF)
             outs[l, u] = out
             both = ahead
+            if l == 2:
+                early()
         spread(NEXP - 1, out)
 
         between()
@@ -260,7 +280,7 @@
                 total = total + jnp.where(routes == first_id + l, line, 0.0)
             dg[blk, pl.ds(mb * TOPK, TOPK), pl.ds(0, tok)] = total
 
-    def backward(u, between=lambda: None):
+    def backward(u, between=lambda: None, early=lambda: None):
         back = ndot(qr[0, u], wd[0])
         for l in range(NEXP):
             ahead = ndot(qr[l + 1, u], wd[l + 1]) if l + 1 < NEXP else None
@@ -275,6 +295,8 @@
             for b in range(QUAD):
                 pbuf[b, pl.ds(l * cap, cap), :] = d_in[b * cap : (b + 1) * cap]
             back = ahead
+            if l == 1:
+                early()
 
         between()
 
@@ -290,86 +312,82 @@
         gu_ref[l] = grads[:, ff:]
 
     def dg_copy(mask):
-        return remote(dg.at[number(mask)], dg_in.at[me], dg_send.at[mask], dg_recv.at[mask], mask)
-
-    for mask in (1, 2, 4, 3, 5, 6, 7):
-        rt_copy(mask).start()
+        return remote(dg.at[number(mask)], dg_in.at[me], dg_send.at[0], dg_recv.at[0], mask)
+
+    for kind in range(3):
+        rt_copy(kind).start()
     for mb in range(2):
         own[mb][0].wait()
         send_own(mb, 6, 0, 3)
     own[0][1].wait()
     send_own(0, 7, 1)
     own[1][1].wait()
-    send_own(1, 7, 4)
-    rt_copy(1).wait_recv()
+    send_own(1, 7)
+    rt_relay(0)
     make_ranks(0)
     for load in weights:
         load.wait()
-    relay(0, 6)
-    relay(1, 6)
+    await_pair(0, 6)
     dispatch_x(OWN)
-    forward(OWN)
+
+    def during():
+        rt_relay(1, 3, 4)
+        rt_relay(2, 5)
+
+    forward(OWN, lambda: None, during)
     partner_start(Y, OWN)
 
     relay(0, 0, 5, 8)
+    send_own(1, 4)
     relay(0, 3, 10)
-    for mask in (2, 3, 4, 5):
-        rt_copy(mask).wait_recv()
+    rt_relay(4)
+    rt_relay(5)
     make_ranks(2)
     make_ranks(4)
-    relay(0, 7)
-    relay(1, 7)
+    await_pair(0, 7)
     dispatch_dy(OWN)
     relay(1, 3, 5, 10)
     relay(1, 0, 8)
     send_own(1, 1)
     send_own(0, 4)
-    relay(0, 8)
-    relay(0, 10)
+    await_pair(0, 8)
     dispatch_x(XY0)
-    forward(XY0, lambda: relay(0, 1, 2, 9))
+    forward(XY0, lambda: relay(0, 1, 2, 9), lambda: rt_relay(3, 6))
     partner_start(Y, XY0)
 
-    for mask in (6, 7):
-        rt_copy(mask).wait_recv()
+    rt_relay(6)
     make_ranks(6)
-    relay(1, 4, 2, 11)
-    relay(1, 8)
-    relay(1, 10)
+    relay(0, 5, 12)
+    await_pair(1, 8)
     dispatch_x(XY1)
-    relay(0, 5, 12)
 
     def during():
         relay(1, 5, 12)
-        leave(Y, XY0)
-
-    forward(XY1, during)
+        relay(1, 4, 2, 11)
+
+    forward(XY1, lambda: leave(Y, XY0), during)
     partner_start(Y, XY1)
 
-    relay(0, 12)
-    relay(1, 12)
+    await_pair(0, 12)
     dispatch_x(DIAG)
     relay(0, 4, 11)
     relay(1, 1, 9)
 
     def during():
+        leave(Y, XY1)
         relay(0, 2, 13)
-        leave(Y, XY1)
-
-    forward(DIAG, during)
+
+    forward(DIAG, lambda: None, during)
     partner_start(Y, DIAG)
 
     relay(1, 2, 13)
     leave(Y, OWN)
-    relay(0, 9)
-    relay(0, 11)
+    await_pair(0, 9)
     dispatch_dy(XY0)
+    await_pair(1, 9)
+    dispatch_dy(XY1)
     leave(Y, DIAG)
-    relay(1, 9)
-    relay(1, 11)
-    dispatch_dy(XY1)
-    relay(0, 13)
-    relay(1, 13)
+    await_pair(0, 13)
     dispatch_dy(DIAG)
     for mask in range(1, NBLK):
         dg_copy(mask).start()
@@ -381,47 +399,41 @@
     partner_start(DX, XY0)
 
     def during():
-        leave(DX, XY0)
         second_send(Y, 0)
         second_send(Y, 1)
 
-    backward(XY1, during)
+    backward(XY1, lambda: leave(DX, XY0), during)
     partner_start(DX, XY1)
 
-    def during():
-        leave(DX, XY1)
-
-    backward(OWN, during)
+    backward(OWN, lambda: leave(DX, XY1))
     partner_start(DX, OWN)
+    weight_grads(0)
     second_send(DX, 0)
     second_send(DX, 1)
-
-    weight_grads(0)
     leave(DX, OWN)
     weight_grads(1)
     weight_grads(2)
     weight_grads(3)
     finish(Y, 0)
     finish(Y, 1)
-    for mask in range(1, NBLK):
-        dg_copy(mask).wait()
+    seven = dg_in.at[pl.ds(0, NBLK - 1)]
+    others = remote(seven, seven, dg_send.at[0], dg_recv.at[0], 1)
+    others.wait_recv()
+    others.wait_send()
     grads = jnp.sum(dg_in[...], axis=0)
     for mb in range(2):
         gates_ref[mb] = grads[mb * TOPK : (mb + 1) * TOPK, :tok]
+    def sent(ref, sem):
+        remote(ref, ref, sem, s_recv.at[0], 1).wait_send()
+
+    sent(rt.at[pl.ds(0, 7)], rt_send.at[0])
+    for which in range(2):
+        sent(tokens[which].at[:, pl.ds(0, 7)], g_send.at[which])
+    sent(near_in, d_send.at[0])
+    sent(first_in, f_send.at[0])
     finish(DX, 0)
     finish(DX, 1)
-    for mask in range(1, NBLK):
-        rt_copy(mask).wait_send()
-    for mb in range(2):
-        for kind in range(14):
-            tok_copy(mb, kind).wait_send()
-        for q in (Y, DX):
-            for mask in (0, 2, 4, 6):
-                to_partner(q, mb, mask).wait_send()
-            for h in range(2):
-                second(q, mb, h).wait_send()
-                for which in range(2):
-                    first(q, mb, h, which).wait_send()
+    sent(second_in, s_send.at[0])
 
 
 def layer(x, grad_y, route_rows, gate_rows, w_gate, w_up, w_down):
@@ -446,7 +458,6 @@
             pltpu.VMEM((NBLK, 4 * TOPK, LANES), F32),
             pltpu.VMEM((2, TOPK, tok), jnp.int32),
             pltpu.VMEM((2, TOPK, tok), F32),
-            pltpu.VMEM((4 * TOPK, LANES), F32),
             pltpu.VMEM((NEXP, dim, 2 * ff), BF),
             pltpu.VMEM((NEXP, ff, dim), BF),
             pltpu.VMEM((4, 4 * NEXP, tok), F32),
@@ -468,8 +479,8 @@
             pltpu.VMEM((4, 2, 2, tok // 2, dim), F32),
             pltpu.VMEM((4, 2, tok // 2, dim), F32),
             pltpu.VMEM((NBLK, 2 * TOPK, LANES), F32),
-            dma((2,)), dma((2, 2)), dma((NEXP, 3)), dma((2, 14)), dma((2, 14)), dma((NBLK,)), dma((NBLK,)),
-            dma((4, 4)), dma((4, 4)), dma((4, 2, 2)), dma((4, 2, 2)), dma((4, 2)), dma((4, 2)), dma((NBLK,)), dma((NBLK,)),
+            dma((2,)), dma((2, 2)), dma((3,)), dma((2,)), dma((20,)), dma((1,)), dma((7,)),
+            dma((1,)), dma((2, 4)), dma((1,)), dma((4, 2)), dma((1,)), dma((4,)), dma((1,)), dma((1,)),
         ],
         compiler_params=pltpu.CompilerParams(collective_id=0, has_side_effects=True, vmem_limit_bytes=46 << 20),
         name="moe_layer",
@@ -480,7 +491,7 @@
     count = (len(refs) - 1) // 2
     sem = refs[-1]
     copies = [pltpu.make_async_copy(refs[i], refs[count + i], sem.at[i]) for i in range(count)]
-    for copy in copies:
+    for copy in reversed(copies):
         copy.start()
     for copy in copies:
         copy.wait()

time: 44.5 us -> 42.2 us (0.948)
  Pallas kernels: 43.6 us -> 41.3 us
    pallas_call x1, Pallas kernels: 40.5 us -> 38.2 us  [layer(): pl.pallas_call(layer_kernel, out_shape=(shape((2, tok, dim), BF), shape((...]
where the time goes in v7:
time: 42.2 us; the launch traced here: 42.1 us
  Pallas kernels  41.3 us (98%)
  between operations  0.8 us (2%)
    pallas_call x1, Pallas kernels, layer(): pl.pallas_call(layer_kernel, out_shape=(shape((2, tok, dim), BF), shape((...  38.2 us
    pallas_call x1, Pallas kernels, flush(): pl.pallas_call(flush_kernel, out_shape=tuple((jax.ShapeDtypeStruct(arr.sh...  3.03 us

profile of v7, /device:TPU:0, one launch (start us, length us, event | category | flops | bytes accessed | tf_op | source)
XLA Modules:
  0.0 42.1 jit_solution(1871783958091995847)
XLA Ops:
  0.6 38.2 %moe_layer.1 = (bf16[2,96,384]{2,1,0:T(8,128)(2,1)S(1)}, bf16[2,96,384]{2,1,0:T(8,128)(2,1)S(1)}, f32[2,4,96]{2,1,0:T(4,128)S(1)}, f32[4,384,384]{2,1,0:T(8,128)...) custom-call(bf16[2,96,384]{2,1,0:T(8,128)(2,1)} %x_hbm.1, bf16[2,96,384]{2,1,0:T(8,128)(2,1)} %dy_hbm.1, ...), custom_call_target="tpu_custom_call" | custom-call | tf_op jit(solution)/shard_map/moe_layer/pallas_call | solution.py:447
  38.9 3.0 %write_out.1 = (bf16[2,96,384]{2,1,0:T(8,128)(2,1)}, bf16[2,96,384]{2,1,0:T(8,128)(2,1)}, f32[2,4,96]{2,1,0:T(4,128)}, f32[4,384,384]{2,1,0:T(8,128)}, f32[4,384,384]{2,1,0:T(8,128)}, /*index=5*/f32[4,384,384]{2,1,0:T(8,128)}) custom-call(bf16[2,96,384]{2,1,0:T(8,128)(2,1)S(1)} %get-tuple-element.18.refs_0_, ...), custom_call_target="tpu_custom_call" | custom-call | tf_op jit(solution)/shard_map/write_out/pallas_call | solution.py:502

commit v8 on v7

--- a/solution.py
+++ b/solution.py
@@ -381,21 +381,21 @@
     partner_start(Y, DIAG)
 
     relay(1, 2, 13)
-    leave(Y, OWN)
     await_pair(0, 9)
     dispatch_dy(XY0)
-    await_pair(1, 9)
-    dispatch_dy(XY1)
     leave(Y, DIAG)
     await_pair(0, 13)
     dispatch_dy(DIAG)
+    backward(DIAG)
+    partner_start(DX, DIAG)
+
+    await_pair(1, 9)
+    dispatch_dy(XY1)
     for mask in range(1, NBLK):
         dg_copy(mask).start()
     dg_in[me] = dg[me]
-    backward(DIAG)
-    partner_start(DX, DIAG)
-
-    backward(XY0, lambda: leave(DX, DIAG))
+    leave(DX, DIAG)
+    backward(XY0, lambda: leave(Y, OWN))
     partner_start(DX, XY0)
 
     def during():

time: 42.2 us -> 41.5 us (0.983)
  Pallas kernels: 41.3 us -> 40.6 us
    pallas_call x1, Pallas kernels: 38.2 us -> 37.6 us  [layer(): pl.pallas_call(layer_kernel, out_shape=(shape((2, tok, dim), BF), shape((...]
where the time goes in v8:
time: 41.5 us; the launch traced here: 41.4 us
  Pallas kernels  40.6 us (98%)
  between operations  0.8 us (2%)
    pallas_call x1, Pallas kernels, layer(): pl.pallas_call(layer_kernel, out_shape=(shape((2, tok, dim), BF), shape((...  37.6 us
    pallas_call x1, Pallas kernels, flush(): pl.pallas_call(flush_kernel, out_shape=tuple((jax.ShapeDtypeStruct(arr.sh...  3.03 us

profile of v8, /device:TPU:0, one launch (start us, length us, event | category | flops | bytes accessed | tf_op | source)
XLA Modules:
  0.0 41.4 jit_solution(12398534168353254613)
XLA Ops:
  0.6 37.6 %moe_layer.1 = (bf16[2,96,384]{2,1,0:T(8,128)(2,1)S(1)}, bf16[2,96,384]{2,1,0:T(8,128)(2,1)S(1)}, f32[2,4,96]{2,1,0:T(4,128)S(1)}, f32[4,384,384]{2,1,0:T(8,128)...) custom-call(bf16[2,96,384]{2,1,0:T(8,128)(2,1)} %x_hbm.1, bf16[2,96,384]{2,1,0:T(8,128)(2,1)} %dy_hbm.1, ...), custom_call_target="tpu_custom_call" | custom-call | tf_op jit(solution)/shard_map/moe_layer/pallas_call | solution.py:447
  38.2 3.0 %write_out.1 = (bf16[2,96,384]{2,1,0:T(8,128)(2,1)}, bf16[2,96,384]{2,1,0:T(8,128)(2,1)}, f32[2,4,96]{2,1,0:T(4,128)}, f32[4,384,384]{2,1,0:T(8,128)}, f32[4,384,384]{2,1,0:T(8,128)}, /*index=5*/f32[4,384,384]{2,1,0:T(8,128)}) custom-call(bf16[2,96,384]{2,1,0:T(8,128)(2,1)S(1)} %get-tuple-element.18.refs_0_, ...), custom_call_target="tpu_custom_call" | custom-call | tf_op jit(solution)/shard_map/write_out/pallas_call | solution.py:502

commit v9 on v8

--- a/solution.py
+++ b/solution.py
@@ -229,7 +229,7 @@
                 xr[l, unit, rows, :] = xs[l * cap : (l + 1) * cap]
                 gcol[l, unit, rows, :] = gate[l * cap : (l + 1) * cap]
 
-    def forward(u, between=lambda: None, early=lambda: None):
+    def forward(u, between=lambda: None, early=lambda: None, at=2):
         def spread(l, out):
             z = gcol[l, u] * out.astype(F32)
             hi = z.astype(BF)
@@ -253,7 +253,7 @@
             out = dot(hidden, wd[l]).astype(BF)
             outs[l, u] = out
             both = ahead
-            if l == 2:
+            if l == at:
                 early()
         spread(NEXP - 1, out)
 
@@ -350,9 +350,10 @@
     relay(1, 0, 8)
     send_own(1, 1)
     send_own(0, 4)
+    rt_relay(3, 6)
     await_pair(0, 8)
     dispatch_x(XY0)
-    forward(XY0, lambda: relay(0, 1, 2, 9), lambda: rt_relay(3, 6))
+    forward(XY0, lambda: relay(0, 1, 2, 9))
     partner_start(Y, XY0)
 
     rt_relay(6)
@@ -364,8 +365,9 @@
     def during():
         relay(1, 5, 12)
         relay(1, 4, 2, 11)
-
-    forward(XY1, lambda: leave(Y, XY0), during)
+        leave(Y, XY0)
+
+    forward(XY1, lambda: None, during, 1)
     partner_start(Y, XY1)
 
     await_pair(0, 12)

time: 41.5 us -> 41.7 us (level)
  no operation moved by 1% of the time
where the time goes in v9:
time: 41.7 us; the launch traced here: 41.6 us
  Pallas kernels  40.8 us (98%)
  between operations  0.8 us (2%)
    pallas_call x1, Pallas kernels, layer(): pl.pallas_call(layer_kernel, out_shape=(shape((2, tok, dim), BF), shape((...  37.8 us
    pallas_call x1, Pallas kernels, flush(): pl.pallas_call(flush_kernel, out_shape=tuple((jax.ShapeDtypeStruct(arr.sh...  3.03 us

profile of v9, /device:TPU:0, one launch (start us, length us, event | category | flops | bytes accessed | tf_op | source)
XLA Modules:
  0.0 41.6 jit_solution(10546636256198643654)
XLA Ops:
  0.6 37.8 %moe_layer.1 = (bf16[2,96,384]{2,1,0:T(8,128)(2,1)S(1)}, bf16[2,96,384]{2,1,0:T(8,128)(2,1)S(1)}, f32[2,4,96]{2,1,0:T(4,128)S(1)}, f32[4,384,384]{2,1,0:T(8,128)...) custom-call(bf16[2,96,384]{2,1,0:T(8,128)(2,1)} %x_hbm.1, bf16[2,96,384]{2,1,0:T(8,128)(2,1)} %dy_hbm.1, ...), custom_call_target="tpu_custom_call" | custom-call | tf_op jit(solution)/shard_map/moe_layer/pallas_call | solution.py:449
  38.4 3.0 %write_out.1 = (bf16[2,96,384]{2,1,0:T(8,128)(2,1)}, bf16[2,96,384]{2,1,0:T(8,128)(2,1)}, f32[2,4,96]{2,1,0:T(4,128)}, f32[4,384,384]{2,1,0:T(8,128)}, f32[4,384,384]{2,1,0:T(8,128)}, /*index=5*/f32[4,384,384]{2,1,0:T(8,128)}) custom-call(bf16[2,96,384]{2,1,0:T(8,128)(2,1)S(1)} %get-tuple-element.18.refs_0_, ...), custom_call_target="tpu_custom_call" | custom-call | tf_op jit(solution)/shard_map/write_out/pallas_call | solution.py:504

commit v10 on v8

--- a/solution.py
+++ b/solution.py
@@ -80,7 +80,7 @@
 def layer_kernel(x_hbm, dy_hbm, route_hbm, gate_hbm, wg_hbm, wu_hbm, wd_hbm,
                  y_ref, dx_ref, gates_ref, gg_ref, gu_ref, gd_ref,
                  xg, dyg, rt, route_tab, gate_tab, wgu, wd, rank, grow, disp, gblk, gcol, xr, qr, uv, hid, outs, zbuf, pbuf, dg,
-                 part, near_in, chip_sum, first_in, second_in, dg_in,
+                 part, near_in, chip_sum, first_in, second_in, dg_in, dg_near, dg_sum,
                  tab_sem, own_sem, w_sem, g_send, g_recv, rt_send, rt_recv, d_send, d_recv, f_send, f_recv, s_send, s_recv, dg_send, dg_recv):
     tok, dim = xg.shape[2], xg.shape[3]
     ff = wd.shape[1]
@@ -312,7 +312,10 @@
         gu_ref[l] = grads[:, ff:]
 
     def dg_copy(mask):
-        return remote(dg.at[number(mask)], dg_in.at[me], dg_send.at[0], dg_recv.at[0], mask)
+        return remote(dg_sum.at[mask // 2], dg_in.at[mask // 2], dg_send.at[1], dg_recv.at[1], mask)
+
+    def dg_near_copy(mask):
+        return remote(dg.at[number(mask | 1)], dg_near.at[mask // 2], dg_send.at[0], dg_recv.at[0], 1)
 
     for kind in range(3):
         rt_copy(kind).start()
@@ -391,10 +394,14 @@
 
     await_pair(1, 9)
     dispatch_dy(XY1)
-    for mask in range(1, NBLK):
+    for mask in (0, 2, 4, 6):
+        dg_near_copy(mask).start()
+    leave(DX, DIAG)
+    remote(dg_near, dg_near, dg_send.at[0], dg_recv.at[0], 1).wait_recv()
+    for mask in (0, 2, 4, 6):
+        dg_sum[mask // 2] = dg[number(mask)] + dg_near[mask // 2]
+    for mask in (6, 2, 4):
         dg_copy(mask).start()
-    dg_in[me] = dg[me]
-    leave(DX, DIAG)
     backward(XY0, lambda: leave(Y, OWN))
     partner_start(DX, XY0)
 
@@ -416,11 +423,10 @@
     weight_grads(3)
     finish(Y, 0)
     finish(Y, 1)
-    seven = dg_in.at[pl.ds(0, NBLK - 1)]
-    others = remote(seven, seven, dg_send.at[0], dg_recv.at[0], 1)
-    others.wait_recv()
-    others.wait_send()
-    grads = jnp.sum(dg_in[...], axis=0)
+    remote(dg_near, dg_near, dg_send.at[0], dg_recv.at[0], 1).wait_send()
+    three = dg_in.at[pl.ds(1, 3)]
+    remote(three, three, dg_send.at[1], dg_recv.at[1], 2).wait()
+    grads = dg_sum[0] + dg_in[1] + dg_in[2] + dg_in[3]
     for mb in range(2):
         gates_ref[mb] = grads[mb * TOPK : (mb + 1) * TOPK, :tok]
     def sent(ref, sem):
@@ -478,9 +484,11 @@
             pltpu.VMEM((4, 4, tok, dim), F32),
             pltpu.VMEM((4, 2, 2, tok // 2, dim), F32),
             pltpu.VMEM((4, 2, tok // 2, dim), F32),
-            pltpu.VMEM((NBLK, 2 * TOPK, LANES), F32),
+            pltpu.VMEM((4, 2 * TOPK, LANES), F32),
+            pltpu.VMEM((4, 2 * TOPK, LANES), F32),
+            pltpu.VMEM((4, 2 * TOPK, LANES), F32),
             dma((2,)), dma((2, 2)), dma((3,)), dma((2,)), dma((20,)), dma((1,)), dma((7,)),
-            dma((1,)), dma((2, 4)), dma((1,)), dma((4, 2)), dma((1,)), dma((4,)), dma((1,)), dma((1,)),
+            dma((1,)), dma((2, 4)), dma((1,)), dma((4, 2)), dma((1,)), dma((4,)), dma((2,)), dma((2,)),
         ],
         compiler_params=pltpu.CompilerParams(collective_id=0, has_side_effects=True, vmem_limit_bytes=46 << 20),
         name="moe_layer",

time: 41.5 us -> 41.4 us (level)
  no operation moved by 1% of the time
where the time goes in v10:
time: 41.4 us; the launch traced here: 41.3 us
  Pallas kernels  40.5 us (98%)
  between operations  0.8 us (2%)
    pallas_call x1, Pallas kernels, layer(): pl.pallas_call(layer_kernel, out_shape=(shape((2, tok, dim), BF), shape((...  37.5 us
    pallas_call x1, Pallas kernels, flush(): pl.pallas_call(flush_kernel, out_shape=tuple((jax.ShapeDtypeStruct(arr.sh...  3.03 us

profile of v10, /device:TPU:0, one launch (start us, length us, event | category | flops | bytes accessed | tf_op | source)
XLA Modules:
  0.0 41.3 jit_solution(7661803213913536686)
XLA Ops:
  0.6 37.5 %moe_layer.1 = (bf16[2,96,384]{2,1,0:T(8,128)(2,1)S(1)}, bf16[2,96,384]{2,1,0:T(8,128)(2,1)S(1)}, f32[2,4,96]{2,1,0:T(4,128)S(1)}, f32[4,384,384]{2,1,0:T(8,128)...) custom-call(bf16[2,96,384]{2,1,0:T(8,128)(2,1)} %x_hbm.1, bf16[2,96,384]{2,1,0:T(8,128)(2,1)} %dy_hbm.1, ...), custom_call_target="tpu_custom_call" | custom-call | tf_op jit(solution)/shard_map/moe_layer/pallas_call | solution.py:453
  38.1 3.0 %write_out.1 = (bf16[2,96,384]{2,1,0:T(8,128)(2,1)}, bf16[2,96,384]{2,1,0:T(8,128)(2,1)}, f32[2,4,96]{2,1,0:T(4,128)}, f32[4,384,384]{2,1,0:T(8,128)}, f32[4,384,384]{2,1,0:T(8,128)}, /*index=5*/f32[4,384,384]{2,1,0:T(8,128)}) custom-call(bf16[2,96,384]{2,1,0:T(8,128)(2,1)S(1)} %get-tuple-element.18.refs_0_, ...), custom_call_target="tpu_custom_call" | custom-call | tf_op jit(solution)/shard_map/write_out/pallas_call | solution.py:510

commit v11 on v10

--- a/solution.py
+++ b/solution.py
@@ -81,7 +81,7 @@
                  y_ref, dx_ref, gates_ref, gg_ref, gu_ref, gd_ref,
                  xg, dyg, rt, route_tab, gate_tab, wgu, wd, rank, grow, disp, gblk, gcol, xr, qr, uv, hid, outs, zbuf, pbuf, dg,
                  part, near_in, chip_sum, first_in, second_in, dg_in, dg_near, dg_sum,
-                 tab_sem, own_sem, w_sem, g_send, g_recv, rt_send, rt_recv, d_send, d_recv, f_send, f_recv, s_send, s_recv, dg_send, dg_recv):
+                 tab_sem, own_sem, w_sem, g_send, g_recv, rt_send, rt_recv, d_send, d_recv, f_send, f_recv, s_send, dg_send, dg_recv):
     tok, dim = xg.shape[2], xg.shape[3]
     ff = wd.shape[1]
     cap = tok // 2
@@ -162,7 +162,7 @@
 
     def second(q, mb, h):
         r = q * 2 + mb
-        return remote(chip_sum.at[r, SECOND[h] // 2, rows_of(h)], second_in.at[r, h], s_send.at[0], s_recv.at[r], SECOND[h])
+        return remote(chip_sum.at[r, SECOND[h] // 2, rows_of(h)], second_in.at[r, h], s_send.at[0], f_recv.at[r, 1], SECOND[h])
 
     def await_both(ref, sem):
         remote(ref, ref, s_send.at[0], sem, 2).wait_recv()
@@ -186,8 +186,7 @@
 
     def finish(q, mb):
         r = q * 2 + mb
-        await_both(first_in.at[r, 1], f_recv.at[r, 1])
-        await_both(second_in.at[r], s_recv.at[r])
+        await_both(first_in.at[r], f_recv.at[r, 1])
         for h in range(2):
             done = chip_sum[r, 0, rows_of(h), :] + first_in[r, 1, h] + second_in[r, h]
             (y_ref, dx_ref)[q][mb, rows_of(h), :] = done.astype(BF)
@@ -430,7 +429,7 @@
     for mb in range(2):
         gates_ref[mb] = grads[mb * TOPK : (mb + 1) * TOPK, :tok]
     def sent(ref, sem):
-        remote(ref, ref, sem, s_recv.at[0], 1).wait_send()
+        remote(ref, ref, sem, f_recv.at[0, 0], 1).wait_send()
 
     sent(rt.at[pl.ds(0, 7)], rt_send.at[0])
     for which in range(2):
@@ -488,7 +487,7 @@
             pltpu.VMEM((4, 2 * TOPK, LANES), F32),
             pltpu.VMEM((4, 2 * TOPK, LANES), F32),
             dma((2,)), dma((2, 2)), dma((3,)), dma((2,)), dma((20,)), dma((1,)), dma((7,)),
-            dma((1,)), dma((2, 4)), dma((1,)), dma((4, 2)), dma((1,)), dma((4,)), dma((2,)), dma((2,)),
+            dma((1,)), dma((2, 4)), dma((1,)), dma((4, 2)), dma((1,)), dma((2,)), dma((2,)),
         ],
         compiler_params=pltpu.CompilerParams(collective_id=0, has_side_effects=True, vmem_limit_bytes=46 << 20),
         name="moe_layer",

time: 41.4 us -> 41.4 us (level)
  no operation moved by 1% of the time
where the time goes in v11:
time: 41.4 us; the launch traced here: 41.3 us
  Pallas kernels  40.5 us (98%)
  between operations  0.8 us (2%)
    pallas_call x1, Pallas kernels, layer(): pl.pallas_call(layer_kernel, out_shape=(shape((2, tok, dim), BF), shape((...  37.4 us
    pallas_call x1, Pallas kernels, flush(): pl.pallas_call(flush_kernel, out_shape=tuple((jax.ShapeDtypeStruct(arr.sh...  3.03 us

profile of v11, /device:TPU:0, one launch (start us, length us, event | category | flops | bytes accessed | tf_op | source)
XLA Modules:
  0.0 41.3 jit_solution(5002243676586771323)
XLA Ops:
  0.6 37.4 %moe_layer.1 = (bf16[2,96,384]{2,1,0:T(8,128)(2,1)S(1)}, bf16[2,96,384]{2,1,0:T(8,128)(2,1)S(1)}, f32[2,4,96]{2,1,0:T(4,128)S(1)}, f32[4,384,384]{2,1,0:T(8,128)...) custom-call(bf16[2,96,384]{2,1,0:T(8,128)(2,1)} %x_hbm.1, bf16[2,96,384]{2,1,0:T(8,128)(2,1)} %dy_hbm.1, ...), custom_call_target="tpu_custom_call" | custom-call | tf_op jit(solution)/shard_map/moe_layer/pallas_call | solution.py:452
  38.1 3.0 %write_out.1 = (bf16[2,96,384]{2,1,0:T(8,128)(2,1)}, bf16[2,96,384]{2,1,0:T(8,128)(2,1)}, f32[2,4,96]{2,1,0:T(4,128)}, f32[4,384,384]{2,1,0:T(8,128)}, f32[4,384,384]{2,1,0:T(8,128)}, /*index=5*/f32[4,384,384]{2,1,0:T(8,128)}) custom-call(bf16[2,96,384]{2,1,0:T(8,128)(2,1)S(1)} %get-tuple-element.18.refs_0_, ...), custom_call_target="tpu_custom_call" | custom-call | tf_op jit(solution)/shard_map/write_out/pallas_call | solution.py:509

commit v12 on v11

--- a/solution.py
+++ b/solution.py
@@ -134,7 +134,7 @@
 
     def rt_copy(kind):
         slot, mask = ((me, 1), (me, 2), (me, 4), (at_x, 4), (at_x, 1), (at_y, 1), (at_d, 1))[kind]
-        return remote(rt.at[slot], rt.at[slot], rt_send.at[0], rt_recv.at[kind], mask)
+        return remote(rt.at[slot], rt.at[slot], rt_send.at[0], rt_recv.at[4 if kind == 5 else kind], mask)
 
     def rt_relay(kind, *then):
         rt_copy(kind).wait_recv()
@@ -342,8 +342,8 @@
     relay(0, 0, 5, 8)
     send_own(1, 4)
     relay(0, 3, 10)
-    rt_relay(4)
-    rt_relay(5)
+    two = rt.at[pl.ds(0, 2)]
+    remote(two, two, rt_send.at[0], rt_recv.at[4], 1).wait_recv()
     make_ranks(2)
     make_ranks(4)
     await_pair(0, 7)

time: 41.4 us -> 41.4 us (level)
  no operation moved by 1% of the time
where the time goes in v12:
time: 41.4 us; the launch traced here: 41.3 us
  Pallas kernels  40.5 us (98%)
  between operations  0.8 us (2%)
    pallas_call x1, Pallas kernels, layer(): pl.pallas_call(layer_kernel, out_shape=(shape((2, tok, dim), BF), shape((...  37.4 us
    pallas_call x1, Pallas kernels, flush(): pl.pallas_call(flush_kernel, out_shape=tuple((jax.ShapeDtypeStruct(arr.sh...  3.03 us

profile of v12, /device:TPU:0, one launch (start us, length us, event | category | flops | bytes accessed | tf_op | source)
XLA Modules:
  0.0 41.3 jit_solution(6383725101215776452)
XLA Ops:
  0.6 37.4 %moe_layer.1 = (bf16[2,96,384]{2,1,0:T(8,128)(2,1)S(1)}, bf16[2,96,384]{2,1,0:T(8,128)(2,1)S(1)}, f32[2,4,96]{2,1,0:T(4,128)S(1)}, f32[4,384,384]{2,1,0:T(8,128)...) custom-call(bf16[2,96,384]{2,1,0:T(8,128)(2,1)} %x_hbm.1, bf16[2,96,384]{2,1,0:T(8,128)(2,1)} %dy_hbm.1, ...), custom_call_target="tpu_custom_call" | custom-call | tf_op jit(solution)/shard_map/moe_layer/pallas_call | solution.py:452
  38.1 3.0 %write_out.1 = (bf16[2,96,384]{2,1,0:T(8,128)(2,1)}, bf16[2,96,384]{2,1,0:T(8,128)(2,1)}, f32[2,4,96]{2,1,0:T(4,128)}, f32[4,384,384]{2,1,0:T(8,128)}, f32[4,384,384]{2,1,0:T(8,128)}, /*index=5*/f32[4,384,384]{2,1,0:T(8,128)}) custom-call(bf16[2,96,384]{2,1,0:T(8,128)(2,1)S(1)} %get-tuple-element.18.refs_0_, ...), custom_call_target="tpu_custom_call" | custom-call | tf_op jit(solution)/shard_map/write_out/pallas_call | solution.py:509
